TPU v7x, 32 devices: a whole 2x2x4 slice. The times are simulated.
32 devices in a mesh: share: 4 (over z), row: 8 (over y, x, core).
Axes of the slice: x: 2, y: 2, z: 4, core: 2. Of those that a mesh axis runs over, the one named last changes fastest.
Arguments:
- remaining_coded_pieces: float32 [16, 128, 8192], P('share', 'row'), may hold values from -6 to 6
- alive_piece_indices: int32 [16], replicated, may hold values from 0 to 19, as said below
- slab_starting_positions: int32 [2], replicated, may hold values from 0 to 48
Outputs:
- decoded: float32 [16, 128, 4096], P('share', None, 'row')
Inputs may be any that keep to these rules, and one draw needn't show every extreme that they name: `alive_piece_indices`: 16 different share numbers in rising order.
All inputs are finite; a program needn't handle non-finite values.
Results may differ from a plain program's by a relative error of at most 0.00007.
Values sent between devices are 32-bit elements; how exact they have to be, the bound alone decides.
No kernel may reach another device: no remote copies, remote signals or barrier semaphores. Data moves between devices by JAX's collectives and lax.ppermute only.
A program may use at most 64 MiB of HBM per device.

v0:
```python
import jax
import jax.numpy as jnp
from jax import lax
from jax.sharding import PartitionSpec as P

K = 16
CODED_PIECES_ALL = 20
W = 2048


def recovery_operator(alive_piece_indices):
    numbers = jnp.arange(CODED_PIECES_ALL, dtype=jnp.float32)
    nodes = jnp.cos(jnp.pi * (2.0 * numbers + 1.0) / (2.0 * CODED_PIECES_ALL))
    chosen_coded_pieces = (
        alive_piece_indices[:, None] == jnp.arange(CODED_PIECES_ALL, dtype=jnp.int32)[None, :]
    ).astype(jnp.float32)
    points = jnp.sum(chosen_coded_pieces * nodes[None, :], axis=1)
    polynomial_degrees = jnp.arange(K, dtype=jnp.float32)
    angles = jnp.pi * (2.0 * polynomial_degrees + 1.0) / (2.0 * K)
    samples = jnp.cos(angles)
    same = jnp.arange(K, dtype=jnp.int32)[:, None] == jnp.arange(K, dtype=jnp.int32)[None, :]
    spacing = jnp.where(same, 1.0, points[:, None] - points[None, :])
    factors = (samples[None, None, :] - points[None, :, None]) / spacing[:, :, None]
    factors = jnp.where(same[:, :, None], 1.0, factors)
    lagrange = jnp.prod(factors, axis=1)
    table = jnp.cos(polynomial_degrees[:, None] * angles[None, :])
    recovery_coefficients = 2.0 / K * jnp.sum(table[:, None, :] * lagrange[None, :, :], axis=2)
    return recovery_coefficients * jnp.where(polynomial_degrees == 0.0, 0.5, 1.0)[:, None]


def body(remaining_coded_pieces, alive_piece_indices, slab_starting_positions):
    recovery_coefficients = recovery_operator(alive_piece_indices)
    first = lax.dynamic_slice_in_dim(remaining_coded_pieces, slab_starting_positions[0] * 128, W, 2)
    second = lax.dynamic_slice_in_dim(
        remaining_coded_pieces, slab_starting_positions[1] * 128, W, 2
    )
    slabs = jnp.concatenate([first, second], axis=2)
    spread = lax.all_to_all(slabs, "row", split_axis=2, concat_axis=1, tiled=True)
    mixed = jnp.einsum(
        "ki,irc->krc",
        recovery_coefficients,
        lax.all_to_all(spread, "share", split_axis=1, concat_axis=0, tiled=True),
        precision=lax.Precision.HIGHEST,
    )
    decoded = lax.all_to_all(mixed, "share", split_axis=0, concat_axis=1, tiled=True)
    return decoded


def solution(mesh):
    placed = (P("share", "row", None), P(), P())
    return jax.shard_map(
        body, mesh=mesh, in_specs=placed, out_specs=P("share", None, "row"), check_vma=False
    )
```

profile of v0, /device:TPU:0, one launch (start us, length us, event | category | flops | bytes accessed | tf_op | source)
XLA Modules:
  0.0 122.4 jit_solution(14569518644108636004)
XLA Ops:
  0.0 1.4 %fusion.7 = (s32[1]{0:T(128)}, s32[1]{0:T(128)}) fusion(s32[2]{0:T(128)} %param.5), kind=kLoop, calls=%fused_computation.21 | loop fusion | bytes 16 | tf_op jit(solution)/shard_map/slice | solution.py:33
  2.7 1.3 %constant_dynamic-slice_fusion.1 = (f32[4,16,2048]{2,1,0:T(8,128)S(1)}, f32[4,16,2048]{2,1,0:T(8,128)S(1)}) fusion(f32[4,16,8192]{2,1,0:T(8,128)} %param.3, s32[]{:T(128)S(6)} %select_n.29, s32[]{:T(128)S(6)} %select_n.30), kind=kLoop, calls=%fused_computation.17 | loop fusion | bytes 2097160 | tf_op jit(solution)/shard_map/dynamic_slice | solution.py:33
  4.0 0.1 pad_maximum_fusion
  4.1 5.9 %copy.27 = f32[4,16,4096]{1,0,2:T(4,128)} copy(f32[4,16,4096]{2,1,0:T(8,128)S(1)} %pad_maximum_fusion) | data formatting | bytes 2097152 | tf_op jit(solution)/shard_map/concatenate | solution.py:37
  10.0 9.3 %reshape.130 = f32[8,1,32768]{2,1,0:T(1,128)S(1)} reshape(f32[4096,4,16]{2,1,0:T(4,128)} %bitcast.22) | data formatting | bytes 2097152
  19.3 20.3 %all_to_all.54 = f32[8,1,32768]{2,1,0:T(1,128)S(1)} all-to-all(f32[8,1,32768]{2,1,0:T(1,128)S(1)} %reshape.130), channel_id=1, replica_groups=mesh['share'=4,'row'=8] {'row'}, dimensions={0} | all-to-all | bytes 2097152 | tf_op jit(solution)/shard_map/all_to_all | solution.py:38
  39.6 0.5 broadcast.161
  40.1 3.1 %reduce = f32[8,32768]{1,0:T(8,128)S(1)} reduce(f32[8,1,32768]{2,1,0:T(1,128)S(1)} %all_to_all.54, f32[]{:T(128)} %broadcast.161), dimensions={1}, to_apply=%all_to_all.39.reduce_sub_computation | reduce | bytes 2097156 | tf_op jit(solution)/shard_map/all_to_all | solution.py:38
  43.3 9.0 %reshape.131 = f32[4096,4,16]{2,1,0:T(4,128)} reshape(f32[8,32768]{1,0:T(8,128)S(1)} %reduce) | data formatting | bytes 2097152
  52.2 0.0 copy-start
  52.2 6.7 %copy.36 = f32[4,16,8,512]{3,1,2,0:T(8,128)S(1)} copy(f32[4,16,8,512]{1,0,3,2:T(4,128)} %bitcast.23) | data formatting | bytes 2097152 | tf_op jit(solution)/shard_map/all_to_all | solution.py:38
  58.9 1.7 %copy.30 = f32[4,128,512]{2,0,1:T(4,128)} copy(f32[4,128,512]{2,1,0:T(8,128)S(1)} %bitcast.24) | data formatting | bytes 2097152 | tf_op jit(solution)/shard_map/all_to_all | solution.py:38
  60.6 4.9 %all-to-all-start.1 = ((f32[4,128,512]{2,0,1:T(4,128)}), f32[4,128,512]{2,0,1:T(4,128)S(1)}, u32[]{:S(2)}, u32[]{:S(2)}) async-start(f32[4,128,512]{2,0,1:T(4,128)} %copy.30), calls=%async_computation.1 | async-start | bytes 2097152 | tf_op jit(solution)/shard_map/all_to_all | solution.py:42
  65.6 0.0 copy-done
  65.6 0.2 select_reduce_fusion
  65.8 0.1 broadcast_subtract_fusion
  65.9 0.1 fusion
  66.0 0.1 multiply_cosine_fusion
  66.1 0.1 multiply_reduce_fusion
  66.2 24.4 %all-to-all-done.1 = f32[4,128,512]{2,0,1:T(4,128)S(1)} async-done(((f32[4,128,512]{2,0,1:T(4,128)}), f32[4,128,512]{2,0,1:T(4,128)S(1)}, u32[]{:S(2)}, u32[]{:S(2)}) %all-to-all-start.1) | async-done | bytes 1048608 | tf_op jit(solution)/shard_map/all_to_all | solution.py:42
  90.6 0.3 copy.31
  91.0 0.7 copy.32
  91.6 0.4 all_to_all.46
  92.0 1.0 fusion.1
  93.1 0.6 copy.33
  93.7 27.7 %all_to_all.55 = f32[16,32,512]{2,1,0:T(8,128)S(1)} all-to-all(f32[16,32,512]{2,1,0:T(8,128)S(1)} %copy.33), channel_id=1, replica_groups=mesh['share'=4,'row'=8] {'share'}, dimensions={0} | all-to-all | bytes 2097152 | tf_op jit(solution)/shard_map/all_to_all | solution.py:45
  121.4 1.1 copy.34
  (5 shorter events, 0.1 us)
Async XLA Ops:
  52.2 13.3 %copy-start = (s32[16]{0:T(128)S(1)}, s32[16]{0:T(128)}, u32[]{:S(2)}) copy-start(s32[16]{0:T(128)} %param.4) | copy-start | bytes 196
  60.6 30.0 %all-to-all-start.1 = ((f32[4,128,512]{2,0,1:T(4,128)}), f32[4,128,512]{2,0,1:T(4,128)S(1)}, u32[]{:S(2)}, u32[]{:S(2)}) async-start(f32[4,128,512]{2,0,1:T(4,128)} %copy.30), calls=%async_computation.1 | async-start | bytes 2097152 | tf_op jit(solution)/shard_map/all_to_all | solution.py:42
where the time goes:
time: 123 us; the launch traced here: 122 us
  blocking collectives  48 us (39%)
  local copies, waits for them, and re-layouts  38.7 us (31%)
  waiting for transfers between devices  24.4 us (20%)
  starting transfers between devices  4.87 us (4%)
  other arithmetic  3.89 us (3%)
  between operations  1.47 us (1%)
    all_to_all x1, blocking collectives, body(): lax.all_to_all(mixed, 'share', split_axis=0, concat_axis=1, tiled=True)  27.7 us
    all_to_all x1, waiting for transfers between devices, body(): lax.all_to_all(spread, 'share', split_axis=1, concat_axis=0, tiled=True)  24.4 us
    all_to_all x1, blocking collectives, body(): lax.all_to_all(slabs, 'row', split_axis=2, concat_axis=1, tiled=True)  20.3 us
    unnamed x4, local copies, waits for them, and re-layouts  18.3 us
    all_to_all x3, local copies, waits for them, and re-layouts, body(): lax.all_to_all(slabs, 'row', split_axis=2, concat_axis=1, tiled=True)  8.84 us
    concatenate x1, local copies, waits for them, and re-layouts, body(): slabs = jnp.concatenate([first, second], axis=2)  5.88 us
    all_to_all x1, starting transfers between devices, body(): lax.all_to_all(spread, 'share', split_axis=1, concat_axis=0, tiled=True)  4.87 us
    all_to_all x1, other arithmetic, body(): lax.all_to_all(slabs, 'row', split_axis=2, concat_axis=1, tiled=True)  3.13 us
  transfers between devices with their start and end apart: 1, of which 1 were waited for; matrix products, arithmetic and copies ran while one was open for 1% of the time, Pallas kernels for 0%

commit v1 on v0

--- a/solution.py
+++ b/solution.py
@@ -28,25 +28,30 @@
     return recovery_coefficients * jnp.where(polynomial_degrees == 0.0, 0.5, 1.0)[:, None]
 
 
-def body(remaining_coded_pieces, alive_piece_indices, slab_starting_positions):
-    recovery_coefficients = recovery_operator(alive_piece_indices)
-    first = lax.dynamic_slice_in_dim(remaining_coded_pieces, slab_starting_positions[0] * 128, W, 2)
-    second = lax.dynamic_slice_in_dim(
-        remaining_coded_pieces, slab_starting_positions[1] * 128, W, 2
-    )
-    slabs = jnp.concatenate([first, second], axis=2)
-    spread = lax.all_to_all(slabs, "row", split_axis=2, concat_axis=1, tiled=True)
-    mixed = jnp.einsum(
-        "ki,irc->krc",
-        recovery_coefficients,
-        lax.all_to_all(spread, "share", split_axis=1, concat_axis=0, tiled=True),
-        precision=lax.Precision.HIGHEST,
-    )
-    decoded = lax.all_to_all(mixed, "share", split_axis=0, concat_axis=1, tiled=True)
-    return decoded
+def solution(mesh):
+    shares, rows = mesh.shape["share"], mesh.shape["row"]
 
+    def body(pieces, alive, starts):
+        weights = recovery_operator(alive)
+        held, depth, _ = pieces.shape
+        width = 2 * W // rows
+        part = width // shares
+        slabs = jnp.concatenate(
+            [lax.dynamic_slice_in_dim(pieces, starts[n] * 128, W, 2) for n in range(2)], axis=2
+        )
+        sent = slabs.reshape(held, depth, rows, shares, part).transpose(3, 2, 0, 1, 4)
+        got = lax.all_to_all(sent, "share", split_axis=0, concat_axis=0, tiled=True)
+        mixed = jnp.einsum(
+            "qtsi,soirc->qotrc",
+            weights.reshape(shares, K // shares, shares, held),
+            got,
+            precision=lax.Precision.HIGHEST,
+        )
+        flat = mixed.reshape(shares * rows, K // shares, depth, part)
+        back = lax.all_to_all(flat, ("share", "row"), split_axis=0, concat_axis=0, tiled=True)
+        back = back.reshape(shares, rows, K // shares, depth, part).transpose(2, 1, 3, 0, 4)
+        return back.reshape(K // shares, rows * depth, width)
 
-def solution(mesh):
     placed = (P("share", "row", None), P(), P())
     return jax.shard_map(
         body, mesh=mesh, in_specs=placed, out_specs=P("share", None, "row"), check_vma=False

time: 123 us -> 72.8 us (0.59)
  local copies, waits for them, and re-layouts: 38.7 us -> 7.52 us
  blocking collectives: 48 us -> 29.7 us
  other arithmetic: 3.89 us -> 0.84 us
  starting transfers between devices: 4.87 us -> 6.35 us
    all_to_all x2 -> x1, blocking collectives: 48 us -> 29.7 us  [body(): lax.all_to_all(flat, ('share', 'row'), split_axis=0, concat_axis=0, tiled...]
    unnamed x4 -> x2, local copies, waits for them, and re-layouts: 18.3 us -> 0.01 us
    all_to_all x7 -> x0, local copies, waits for them, and re-layouts: 11.3 us -> none  [the longest x3 8.84 us: body(): lax.all_to_all(slabs, 'row', split_axis=2, concat_axis=1, tiled=True)]
    concatenate x1 -> x0, local copies, waits for them, and re-layouts: 5.88 us -> none  [body(): slabs = jnp.concatenate([first, second], axis=2)]
    all_to_all x1 -> x0, other arithmetic: 3.13 us -> none  [body(): lax.all_to_all(slabs, 'row', split_axis=2, concat_axis=1, tiled=True)]
    transpose x0 -> x3, local copies, waits for them, and re-layouts: none -> 2.66 us  [the longest x1 1.65 us: body(): slabs.reshape(held, depth, rows, shares, part).transpose(3, 2, 0, 1, 4)]
    reshape x0 -> x2, local copies, waits for them, and re-layouts: none -> 2.1 us  [the longest x1 1.39 us: body(): return back.reshape(K // shares, rows * depth, width)]
    all_to_all x1, starting transfers between devices: 4.87 us -> 6.35 us  [body(): got = lax.all_to_all(sent, 'share', split_axis=0, concat_axis=0, tiled=True)]
where the time goes in v1:
time: 72.8 us; the launch traced here: 72.6 us
  blocking collectives  29.7 us (41%)
  waiting for transfers between devices  24.8 us (34%)
  local copies, waits for them, and re-layouts  7.52 us (10%)
  starting transfers between devices  6.35 us (9%)
  matrix products  1.89 us (3%)
  between operations  1.46 us (2%)
  other arithmetic  0.84 us (1%)
    all_to_all x1, blocking collectives, body(): lax.all_to_all(flat, ('share', 'row'), split_axis=0, concat_axis=0, tiled...  29.7 us
    all_to_all x1, waiting for transfers between devices, body(): got = lax.all_to_all(sent, 'share', split_axis=0, concat_axis=0, tiled=True)  24.8 us
    all_to_all x1, starting transfers between devices, body(): got = lax.all_to_all(sent, 'share', split_axis=0, concat_axis=0, tiled=True)  6.35 us
    dot_general x1, matrix products, body(): jnp.einsum('qtsi,soirc->qotrc', weights.reshape(shares, K // shares, shar...  1.89 us
    transpose x1, local copies, waits for them, and re-layouts, body(): slabs.reshape(held, depth, rows, shares, part).transpose(3, 2, 0, 1, 4)  1.65 us
  transfers between devices with their start and end apart: 1, of which 1 were waited for; matrix products, arithmetic and copies ran while one was open for 1% of the time, Pallas kernels for 0%

profile of v1, /device:TPU:0, one launch (start us, length us, event | category | flops | bytes accessed | tf_op | source)
XLA Modules:
  0.0 72.6 jit_solution(13628708284004049995)
XLA Ops:
  0.0 1.4 %fusion.4 = (s32[1]{0:T(128)}, s32[1]{0:T(128)}) fusion(s32[2]{0:T(128)} %param.5), kind=kLoop, calls=%fused_computation.21 | loop fusion | bytes 16 | tf_op jit(solution)/shard_map/slice | solution.py:40
  2.7 1.3 %constant_dynamic-slice_fusion.1 = (f32[4,16,2048]{2,1,0:T(8,128)S(1)}, f32[4,16,2048]{2,1,0:T(8,128)S(1)}) fusion(f32[4,16,8192]{2,1,0:T(8,128)} %param.3, s32[]{:T(128)S(6)} %select_n.27, s32[]{:T(128)S(6)} %select_n.28), kind=kLoop, calls=%fused_computation.19 | loop fusion | bytes 2097160 | tf_op jit(solution)/shard_map/dynamic_slice | solution.py:40
  4.0 0.1 pad_maximum_fusion
  4.1 0.7 reshape.148
  4.8 0.0 copy-start
  4.8 1.6 %copy.16 = f32[4,8,4,16,128]{4,2,3,1,0:T(4,128)} copy(f32[4,8,4,16,128]{4,0,1,3,2:T(4,128)S(1)} %bitcast.18) | data formatting | bytes 2097152 | tf_op jit(solution)/shard_map/transpose | solution.py:42
  6.5 6.3 %all-to-all-start = ((f32[4,8,4,16,128]{4,2,3,1,0:T(4,128)}), f32[4,8,4,16,128]{4,2,3,1,0:T(4,128)S(1)}, u32[]{:S(2)}, u32[]{:S(2)}) async-start(f32[4,8,4,16,128]{4,2,3,1,0:T(4,128)} %copy.16), calls=%async_computation | async-start | bytes 2097152 | tf_op jit(solution)/shard_map/all_to_all | solution.py:43
  13.0 0.0 copy-done
  13.0 0.2 select_reduce_fusion
  13.1 0.1 broadcast_subtract_fusion
  13.2 0.1 fusion.1
  13.4 0.1 multiply_cosine_fusion
  13.4 0.1 multiply_reduce_fusion
  13.6 0.1 reduce_sum.22
  13.7 0.1 multiply_bitcast_fusion
  13.7 24.8 %all-to-all-done = f32[4,8,4,16,128]{4,2,3,1,0:T(4,128)S(1)} async-done(((f32[4,8,4,16,128]{4,2,3,1,0:T(4,128)}), f32[4,8,4,16,128]{4,2,3,1,0:T(4,128)S(1)}, u32[]{:S(2)}, u32[]{:S(2)}) %all-to-all-start) | async-done | bytes 1048608 | tf_op jit(solution)/shard_map/all_to_all | solution.py:43
  38.6 1.9 %convolution_bitcast_fusion = f32[4,8,4,16,128]{4,2,0,3,1:T(4,128)S(1)} fusion(f32[4,4,4,4,1,1]{3,2,1,0,5,4:T(4,128)S(1)} %multiply_bitcast_fusion, f32[4,8,4,16,128]{4,2,3,1,0:T(4,128)S(1)} %all-to-all-done), kind=kOutput, calls=%fused_computation | convolution fusion | flops 50331648 | bytes 2098176 | tf_op jit(solution)/shard_map/qtsi,soirc->qotrc/dot_general | solution.py:44
  40.5 0.3 copy.19
  40.8 29.7 %all_to_all.10 = f32[32,4,16,128]{3,2,1,0:T(8,128)S(1)} all-to-all(f32[32,4,16,128]{3,2,1,0:T(8,128)S(1)} %bitcast.19), channel_id=1, replica_groups=mesh['share'=4,'row'=8] {'share','row'}, dimensions={0} | all-to-all | bytes 2097152 | tf_op jit(solution)/shard_map/all_to_all | solution.py:51
  70.5 0.7 copy.20
  71.2 1.4 %reshape.151 = f32[4,128,512]{2,1,0:T(8,128)} reshape(f32[4,8,16,4,128]{4,3,2,1,0:T(4,128)S(1)} %copy.20) | data formatting | bytes 2097152 | tf_op jit(solution)/shard_map/reshape | solution.py:53
  (5 shorter events, 0.1 us)
Async XLA Ops:
  4.8 8.1 %copy-start = (s32[16]{0:T(128)S(1)}, s32[16]{0:T(128)}, u32[]{:S(2)}) copy-start(s32[16]{0:T(128)} %param.4) | copy-start | bytes 196
  6.5 32.1 %all-to-all-start = ((f32[4,8,4,16,128]{4,2,3,1,0:T(4,128)}), f32[4,8,4,16,128]{4,2,3,1,0:T(4,128)S(1)}, u32[]{:S(2)}, u32[]{:S(2)}) async-start(f32[4,8,4,16,128]{4,2,3,1,0:T(4,128)} %copy.16), calls=%async_computation | async-start | bytes 2097152 | tf_op jit(solution)/shard_map/all_to_all | solution.py:43

commit v2 on v0

v2 whole, which is shorter than its diff:
```python
import functools
import math

import jax
import jax.numpy as jnp
from jax import lax
from jax.experimental import pallas as pl
from jax.experimental.pallas import tpu as pltpu
from jax.sharding import PartitionSpec as P

K = 16
CODED_PIECES_ALL = 20
W = 2048

VMEM = pl.BlockSpec(memory_space=pltpu.VMEM)
SMEM = pl.BlockSpec(memory_space=pltpu.SMEM)
ANY = pl.BlockSpec(memory_space=pl.ANY)


def recovery_operator(alive_piece_indices):
    numbers = jnp.arange(CODED_PIECES_ALL, dtype=jnp.float32)
    nodes = jnp.cos(jnp.pi * (2.0 * numbers + 1.0) / (2.0 * CODED_PIECES_ALL))
    chosen_coded_pieces = (
        alive_piece_indices[:, None] == jnp.arange(CODED_PIECES_ALL, dtype=jnp.int32)[None, :]
    ).astype(jnp.float32)
    points = jnp.sum(chosen_coded_pieces * nodes[None, :], axis=1)
    polynomial_degrees = jnp.arange(K, dtype=jnp.float32)
    angles = jnp.pi * (2.0 * polynomial_degrees + 1.0) / (2.0 * K)
    samples = jnp.cos(angles)
    same = jnp.arange(K, dtype=jnp.int32)[:, None] == jnp.arange(K, dtype=jnp.int32)[None, :]
    spacing = jnp.where(same, 1.0, points[:, None] - points[None, :])
    factors = (samples[None, None, :] - points[None, :, None]) / spacing[:, :, None]
    factors = jnp.where(same[:, :, None], 1.0, factors)
    lagrange = jnp.prod(factors, axis=1)
    table = jnp.cos(polynomial_degrees[:, None] * angles[None, :])
    recovery_coefficients = 2.0 / K * jnp.sum(table[:, None, :] * lagrange[None, :, :], axis=2)
    return recovery_coefficients * jnp.where(polynomial_degrees == 0.0, 0.5, 1.0)[:, None]


class Hops:
    def __init__(self, mesh):
        self.shares, self.rows = mesh.shape["share"], mesh.shape["row"]
        self.share = [0, *range(self.shares - 1, 0, -1)]
        hops = range(self.rows)
        self.near = [hop for hop in hops if hop.bit_count() <= 1]
        self.far = [hop for hop in hops if hop.bit_count() > 1]


class Sizes:
    def __init__(self, mesh, pieces):
        self.shares, self.rows = mesh.shape["share"], mesh.shape["row"]
        self.held, self.depth, self.columns = pieces.shape
        self.kept = K // self.shares
        self.width = 2 * W // self.rows
        self.part = self.width // self.shares

    def tiled(self):
        powers = all(n & (n - 1) == 0 for n in (self.shares, self.rows)) and self.rows > 2
        whole = self.depth % 8 == 0 and self.width % (128 * self.shares) == 0
        return powers and whole and W % self.width == 0


def floats(*shape):
    return jax.ShapeDtypeStruct(shape, jnp.float32)


def cut(z, hops, starts, pieces, *refs):
    near, far = refs[: z.shares], refs[z.shares : z.shares + len(hops.far)]
    firsts, columns, sems = refs[z.shares + len(hops.far) :]
    share, row = lax.axis_index("share"), lax.axis_index("row")
    copies = [pltpu.make_async_copy(starts, firsts, sems.at[0])]
    for n in range(z.held):
        copies.append(pltpu.make_async_copy(pieces.at[n], columns.at[n], sems.at[n + 1]))
    for copy in copies:
        copy.start()
    copies[0].wait()

    def part(p, m):
        owner = row ^ p
        slab = (owner * z.width) // W
        first = firsts[slab] * 128 + owner * z.width - slab * W + (share ^ m) * z.part
        return columns[:, :, pl.ds(pl.multiple_of(first, 128), z.part)]

    for copy in copies[1:]:
        copy.wait()
    for m, share_hop in enumerate(hops.share):
        for p, row_hop in enumerate(hops.near):
            near[m][p] = part(row_hop, share_hop)
    for p, row_hop in enumerate(hops.far):
        for m, share_hop in enumerate(hops.share):
            far[p][m] = part(row_hop, share_hop)


def regroup(z, hops, *refs):
    outs, ins = refs[-z.shares :], refs[: -z.shares]
    for m in range(z.shares):
        for p, sent in enumerate(ins):
            outs[m][p] = sent[m]


def mix(z, hops, by_row, weights, *refs):
    ins, outs = refs[: z.shares], refs[z.shares :]
    share = lax.axis_index("share")
    for m, target in enumerate(hops.share):
        totals = [None] * z.kept
        for n, source in enumerate(hops.share):
            for i in range(z.held):
                values = ins[n][:, i]
                for k in range(z.kept):
                    weight = weights[(share ^ target) * z.kept + k, (share ^ source) * z.held + i]
                    term = weight * values
                    totals[k] = term if totals[k] is None else totals[k] + term
        for k, total in enumerate(totals):
            if by_row:
                for p, out in enumerate(outs):
                    out[m, k] = total[p]
            else:
                outs[m][:, k] = total


def place(z, hops, rows, *refs):
    ins, out, sems = refs[-z.shares - 2 : -2], refs[-2], refs[-1]
    share, row = lax.axis_index("share"), lax.axis_index("row")
    copies = []
    for m, share_hop in enumerate(hops.share):
        for p, row_hop in enumerate(rows):
            line = pl.multiple_of((row ^ row_hop) * z.depth, 8)
            column = pl.multiple_of((share ^ share_hop) * z.part, 128)
            there = out.at[:, pl.ds(line, z.depth), pl.ds(column, z.part)]
            copies.append(pltpu.make_async_copy(ins[m].at[p], there, sems.at[m, p]))
    for copy in copies:
        copy.start()
    for copy in copies:
        copy.wait()


def exchange(arrays, axis, peers, hops):
    out = []
    for array, hop in zip(arrays, hops, strict=True):
        pairs = [(i, i ^ hop) for i in range(peers)]
        out.append(lax.ppermute(array, axis, pairs) if hop else array)
    return out


def plain_body(z, pieces, alive, starts):
    weights = recovery_operator(alive)
    slabs = jnp.concatenate(
        [lax.dynamic_slice_in_dim(pieces, starts[n] * 128, W, 2) for n in range(2)], axis=2
    )
    sent = slabs.reshape(z.held, z.depth, z.rows, z.shares, z.part).transpose(3, 2, 0, 1, 4)
    got = lax.all_to_all(sent, "share", split_axis=0, concat_axis=0, tiled=True)
    mixed = jnp.einsum(
        "qtsi,soirc->qotrc",
        weights.reshape(z.shares, z.kept, z.shares, z.held),
        got,
        precision=lax.Precision.HIGHEST,
    )
    flat = mixed.reshape(z.shares * z.rows, z.kept, z.depth, z.part)
    back = lax.all_to_all(flat, ("share", "row"), split_axis=0, concat_axis=0, tiled=True)
    back = back.reshape(z.shares, z.rows, z.kept, z.depth, z.part).transpose(2, 1, 3, 0, 4)
    return back.reshape(z.kept, z.rows * z.depth, z.width)


def tiled_body(z, hops, pieces, alive, starts):
    weights = recovery_operator(alive)
    near, far, shares = len(hops.near), len(hops.far), z.shares

    def call(kernel, outs, ins, in_specs, out_specs, scratch=(), flops=0, **more):
        words = sum(math.prod(out.shape) for out in jax.tree.leaves(outs))
        return pl.pallas_call(
            functools.partial(kernel, z, hops),
            out_shape=outs,
            in_specs=in_specs,
            out_specs=out_specs,
            scratch_shapes=scratch,
            compiler_params=pltpu.CompilerParams(vmem_limit_bytes=8 << 20),
            cost_estimate=pl.CostEstimate(
                flops=flops or words, bytes_accessed=8 * words, transcendentals=0
            ),
            **more,
        )(*ins)

    def over_shares(arrays):
        return exchange(arrays, "share", shares, hops.share)

    def over_rows(arrays, rows):
        return exchange(arrays, "row", z.rows, rows)

    def slots(count, lead, blocks):
        return [floats(lead, blocks, z.depth, z.part)] * count

    def regrouped(arrays, blocks):
        outs = slots(shares, len(arrays), blocks)
        return call(regroup, outs, arrays, [VMEM] * len(arrays), [VMEM] * shares)

    def mixed(arrays, rows, by_row):
        outs = slots(rows, shares, z.kept) if by_row else slots(shares, rows, z.kept)
        specs = [SMEM] + [VMEM] * shares
        return call(
            lambda z, hops, *refs: mix(z, hops, by_row, *refs),
            outs,
            (weights, *arrays),
            specs,
            [VMEM] * len(outs),
            flops=2 * K * rows * K * z.depth * z.part,
        )

    def placed(arrays, rows, base=()):
        return call(
            lambda z, hops, *refs: place(z, hops, rows, *refs),
            floats(z.kept, z.rows * z.depth, z.width),
            (*base, *arrays),
            [ANY] * len(base) + [VMEM] * shares,
            ANY,
            [pltpu.SemaphoreType.DMA((shares, len(rows)))],
            input_output_aliases={0: 0} if base else {},
        )

    in_hbm = [pltpu.with_memory_space_constraint(a, pltpu.HBM) for a in (starts, pieces)]
    scratch = [
        pltpu.SMEM((2,), jnp.int32),
        pltpu.VMEM((z.held, z.depth, z.columns), jnp.float32),
        pltpu.SemaphoreType.DMA((z.held + 1,)),
    ]
    parts = slots(shares, near, z.held) + [floats(shares, z.held, z.depth, z.part)] * far
    parts = call(cut, parts, in_hbm, [ANY, ANY], [VMEM] * len(parts), scratch)
    first = over_shares(parts[:shares])
    second = over_rows(parts[shares:], hops.far)
    second = over_shares(regrouped(second, z.held))
    first = over_rows(mixed(first, near, True), hops.near)
    first = over_shares(regrouped(first, z.kept))
    second = over_shares(mixed(second, far, False))
    out = placed(first, hops.near)
    return placed(second, hops.far, (out,))


def solution(mesh):
    hops = Hops(mesh)

    def body(pieces, alive, starts):
        z = Sizes(mesh, pieces)
        if not z.tiled():
            return plain_body(z, pieces, alive, starts)
        return tiled_body(z, hops, pieces, alive, starts)

    placed = (P("share", "row", None), P(), P())
    return jax.shard_map(
        body, mesh=mesh, in_specs=placed, out_specs=P("share", None, "row"), check_vma=False
    )
```

time: 123 us -> 62 us (0.50)
  blocking collectives: 48 us -> 0 us
  local copies, waits for them, and re-layouts: 38.7 us -> 0.01 us
  starting transfers between devices: 4.87 us -> 30.7 us
  Pallas kernels: 0 us -> 6.25 us
  other arithmetic: 3.89 us -> 0.76 us
  between operations: 1.47 us -> 0.1 us
    all_to_all x2 -> x0, blocking collectives: 48 us -> none  [the longest x1 27.7 us: body(): lax.all_to_all(mixed, 'share', split_axis=0, concat_axis=1, tiled=True)]
    ppermute x0 -> x19, starting transfers between devices: none -> 30.7 us  [exchange(): out.append(lax.ppermute(array, axis, pairs) if hop else array)]
    all_to_all x1 -> x0, waiting for transfers between devices: 24.4 us -> none  [body(): lax.all_to_all(spread, 'share', split_axis=1, concat_axis=0, tiled=True)]
    ppermute x0 -> x19, waiting for transfers between devices: none -> 24 us  [exchange(): out.append(lax.ppermute(array, axis, pairs) if hop else array)]
    unnamed x4 -> x2, local copies, waits for them, and re-layouts: 18.3 us -> 0.01 us
    all_to_all x7 -> x0, local copies, waits for them, and re-layouts: 11.3 us -> none  [the longest x3 8.84 us: body(): lax.all_to_all(slabs, 'row', split_axis=2, concat_axis=1, tiled=True)]
    pallas_call x0 -> x7, Pallas kernels: none -> 6.25 us  [call(): pl.pallas_call(functools.partial(kernel, z, hops), out_shape=outs, in_spe...]
    concatenate x1 -> x0, local copies, waits for them, and re-layouts: 5.88 us -> none  [body(): slabs = jnp.concatenate([first, second], axis=2)]
  transfers between devices with their start and end apart: 1 -> 19, of which waited for: 1 -> 7; matrix products, arithmetic and copies ran while one was open for 1% -> 1% of each run, Pallas kernels for 0% -> 6%
where the time goes in v2:
time: 62 us; the launch traced here: 61.8 us
  starting transfers between devices  30.7 us (50%)
  waiting for transfers between devices  24 us (39%)
  Pallas kernels  6.25 us (10%)
  other arithmetic  0.76 us (1%)
    ppermute x19, starting transfers between devices, exchange(): out.append(lax.ppermute(array, axis, pairs) if hop else array)  30.7 us
    ppermute x19, waiting for transfers between devices, exchange(): out.append(lax.ppermute(array, axis, pairs) if hop else array)  24 us
    pallas_call x7, Pallas kernels, call(): pl.pallas_call(functools.partial(kernel, z, hops), out_shape=outs, in_spe...  6.25 us
  transfers between devices with their start and end apart: 19, of which 7 were waited for; matrix products, arithmetic and copies ran while one was open for 1% of the time, Pallas kernels for 6%

profile of v2, /device:TPU:0, one launch (start us, length us, event | category | flops | bytes accessed | tf_op | source)
XLA Modules:
  0.0 61.8 jit_solution(3385701274520098)
XLA Ops:
  0.0 1.7 %shard_map.37 = (f32[4,4,16,128]{3,2,1,0:T(8,128)S(1)}, f32[4,4,16,128]{3,2,1,0:T(8,128)S(1)}, f32[4,4,16,128]{3,2,1,0:T(8,128)S(1)}, f32[4,4,16,128]{3,2,1,0:T(...) custom-call(s32[2]{0:T(128)} %starts.1, ...), custom_call_target="tpu_custom_call" | custom-call | flops 262144 | bytes 2097152 | tf_op jit(solution)/shard_map/pallas_call | solution.py:170
  1.7 5.1 %collective-permute-start = (f32[4,4,16,128]{3,2,1,0:T(8,128)S(1)}, f32[4,4,16,128]{3,2,1,0:T(8,128)S(1)}, u32[]{:S(2)}, u32[]{:S(2)}) collective-permute-start(f32[4,4,16,128]{3,2,1,0:T(8,128)S(1)} %get-tuple-element.30), channel_id=1, source_target_pairs={{0,24},{8,16},{16,8},{24,0},{1,25},{9,17},{17,9},{25,1},{2,26},{10... | collective-permute-start | bytes 393224 | tf_op jit(solution)/shard_map/ppermute | solution.py:141
  6.9 0.6 %collective-permute-start.2 = (f32[4,4,16,128]{3,2,1,0:T(8,128)S(1)}, f32[4,4,16,128]{3,2,1,0:T(8,128)S(1)}, u32[]{:S(2)}, u32[]{:S(2)}) collective-permute-start(f32[4,4,16,128]{3,2,1,0:T(8,128)S(1)} %get-tuple-element.32), channel_id=1, source_target_pairs={{0,8},{8,0},{16,24},{24,16},{1,9},{9,1},{17,25},{25,17},{2,10},{10... | collective-permute-start | bytes 393224 | tf_op jit(solution)/shard_map/ppermute | solution.py:141
  7.5 0.4 collective-permute-start.9
  7.9 2.5 %collective-permute-start.10 = (f32[4,4,16,128]{3,2,1,0:T(8,128)S(1)}, f32[4,4,16,128]{3,2,1,0:T(8,128)S(1)}, u32[]{:S(2)}, u32[]{:S(2)}) collective-permute-start(f32[4,4,16,128]{3,2,1,0:T(8,128)S(1)} %get-tuple-element.42), channel_id=1, source_target_pairs={{0,5},{1,4},{2,7},{3,6},{4,1},{5,0},{6,3},{7,2},{8,13},{9,12},{10,... | collective-permute-start | bytes 393224 | tf_op jit(solution)/shard_map/ppermute | solution.py:141
  10.6 0.2 select_reduce_fusion
  10.8 0.1 broadcast_subtract_fusion
  10.8 0.1 fusion
  11.0 0.1 multiply_reduce_fusion
  11.1 0.1 broadcast_multiply_fusion.refs_0_
  11.2 0.1 collective-permute-done.refs_2_
  11.3 2.6 %collective-permute-start.11 = (f32[4,4,16,128]{3,2,1,0:T(8,128)S(1)}, f32[4,4,16,128]{3,2,1,0:T(8,128)S(1)}, u32[]{:S(2)}, u32[]{:S(2)}) collective-permute-start(f32[4,4,16,128]{3,2,1,0:T(8,128)S(1)} %get-tuple-element.43), channel_id=1, source_target_pairs={{0,6},{1,7},{2,4},{3,5},{4,2},{5,3},{6,0},{7,1},{8,14},{9,15},{10,... | collective-permute-start | bytes 393224 | tf_op jit(solution)/shard_map/ppermute | solution.py:141
  13.9 4.0 %collective-permute-done.1.refs_3_ = f32[4,4,16,128]{3,2,1,0:T(8,128)S(1)} collective-permute-done((f32[4,4,16,128]{3,2,1,0:T(8,128)S(1)}, f32[4,4,16,128]{3,2,1,0:T(8,128)S(1)}, u32[]{:S(2)}, u32[]{:S(2)}) %collective-permute-start.1) | collective-permute-done | bytes 131104 | tf_op jit(solution)/shard_map/ppermute | solution.py:141
  17.9 1.2 %collective-permute-start.12 = (f32[4,4,16,128]{3,2,1,0:T(8,128)S(1)}, f32[4,4,16,128]{3,2,1,0:T(8,128)S(1)}, u32[]{:S(2)}, u32[]{:S(2)}) collective-permute-start(f32[4,4,16,128]{3,2,1,0:T(8,128)S(1)} %get-tuple-element.44), channel_id=1, source_target_pairs={{0,7},{1,6},{2,5},{3,4},{4,3},{5,2},{6,1},{7,0},{8,15},{9,14},{10,... | collective-permute-start | bytes 393224 | tf_op jit(solution)/shard_map/ppermute | solution.py:141
  19.2 1.3 %shard_map.38 = (f32[4,4,16,128]{3,2,1,0:T(8,128)S(1)}, f32[4,4,16,128]{3,2,1,0:T(8,128)S(1)}, f32[4,4,16,128]{3,2,1,0:T(8,128)S(1)}, f32[4,4,16,128]{3,2,1,0:T(8,128)S(1)}) custom-call(f32[16,16]{1,0:T(8,128)S(1)} %broadcast_multiply_fusion.refs_0_, f32[4,4,16,128]{3,2,1,0:T(8,128)S(1)} %get-tuple-element.29.refs_1_, ...), custom_call_target="tpu_custom_call" | custom-call | flops 4194304 | bytes 1048576 | tf_op jit(solution)/shard_map/pallas_call | solution.py:170
  20.5 1.4 %collective-permute-start.3 = (f32[4,4,16,128]{3,2,1,0:T(8,128)S(1)}, f32[4,4,16,128]{3,2,1,0:T(8,128)S(1)}, u32[]{:S(2)}, u32[]{:S(2)}) collective-permute-start(f32[4,4,16,128]{3,2,1,0:T(8,128)S(1)} %get-tuple-element.34), channel_id=1, source_target_pairs={{0,1},{1,0},{2,3},{3,2},{4,5},{5,4},{6,7},{7,6},{8,9},{9,8},{10,11... | collective-permute-start | bytes 393224 | tf_op jit(solution)/shard_map/ppermute | solution.py:141
  21.9 0.5 collective-permute-start.4
  22.4 0.5 collective-permute-start.5
  22.9 1.6 %collective-permute-done.12.refs_3_ = f32[4,4,16,128]{3,2,1,0:T(8,128)S(1)} collective-permute-done((f32[4,4,16,128]{3,2,1,0:T(8,128)S(1)}, f32[4,4,16,128]{3,2,1,0:T(8,128)S(1)}, u32[]{:S(2)}, u32[]{:S(2)}) %collective-permute-start.12) | collective-permute-done | bytes 131104 | tf_op jit(solution)/shard_map/ppermute | solution.py:141
  24.6 2.5 %collective-permute-start.13 = (f32[4,4,16,128]{3,2,1,0:T(8,128)S(1)}, f32[4,4,16,128]{3,2,1,0:T(8,128)S(1)}, u32[]{:S(2)}, u32[]{:S(2)}) collective-permute-start(f32[4,4,16,128]{3,2,1,0:T(8,128)S(1)} %get-tuple-element.46), channel_id=1, source_target_pairs={{0,24},{8,16},{16,8},{24,0},{1,25},{9,17},{17,9},{25,1},{2,26},{10... | collective-permute-start | bytes 393224 | tf_op jit(solution)/shard_map/ppermute | solution.py:141
  27.1 1.9 %collective-permute-start.15 = (f32[4,4,16,128]{3,2,1,0:T(8,128)S(1)}, f32[4,4,16,128]{3,2,1,0:T(8,128)S(1)}, u32[]{:S(2)}, u32[]{:S(2)}) collective-permute-start(f32[4,4,16,128]{3,2,1,0:T(8,128)S(1)} %get-tuple-element.48), channel_id=1, source_target_pairs={{0,8},{8,0},{16,24},{24,16},{1,9},{9,1},{17,25},{25,17},{2,10},{10... | collective-permute-start | bytes 393224 | tf_op jit(solution)/shard_map/ppermute | solution.py:141
  29.1 2.5 %collective-permute-start.6 = (f32[4,4,16,128]{3,2,1,0:T(8,128)S(1)}, f32[4,4,16,128]{3,2,1,0:T(8,128)S(1)}, u32[]{:S(2)}, u32[]{:S(2)}) collective-permute-start(f32[4,4,16,128]{3,2,1,0:T(8,128)S(1)} %get-tuple-element.38), channel_id=1, source_target_pairs={{0,24},{8,16},{16,8},{24,0},{1,25},{9,17},{17,9},{25,1},{2,26},{10... | collective-permute-start | bytes 393224 | tf_op jit(solution)/shard_map/ppermute | solution.py:141
  31.6 1.3 %collective-permute-done.13.refs_2_ = f32[4,4,16,128]{3,2,1,0:T(8,128)S(1)} collective-permute-done((f32[4,4,16,128]{3,2,1,0:T(8,128)S(1)}, f32[4,4,16,128]{3,2,1,0:T(8,128)S(1)}, u32[]{:S(2)}, u32[]{:S(2)}) %collective-permute-start.13) | collective-permute-done | bytes 131104 | tf_op jit(solution)/shard_map/ppermute | solution.py:141
  32.9 3.9 %collective-permute-start.8 = (f32[4,4,16,128]{3,2,1,0:T(8,128)S(1)}, f32[4,4,16,128]{3,2,1,0:T(8,128)S(1)}, u32[]{:S(2)}, u32[]{:S(2)}) collective-permute-start(f32[4,4,16,128]{3,2,1,0:T(8,128)S(1)} %get-tuple-element.40), channel_id=1, source_target_pairs={{0,8},{8,0},{16,24},{24,16},{1,9},{9,1},{17,25},{25,17},{2,10},{10... | collective-permute-start | bytes 393224 | tf_op jit(solution)/shard_map/ppermute | solution.py:141
  36.8 7.9 %collective-permute-done.14.refs_3_ = f32[4,4,16,128]{3,2,1,0:T(8,128)S(1)} collective-permute-done((f32[4,4,16,128]{3,2,1,0:T(8,128)S(1)}, f32[4,4,16,128]{3,2,1,0:T(8,128)S(1)}, u32[]{:S(2)}, u32[]{:S(2)}) %collective-permute-start.14) | collective-permute-done | bytes 131104 | tf_op jit(solution)/shard_map/ppermute | solution.py:141
  44.7 1.3 %shard_map.42 = (f32[4,4,16,128]{3,2,1,0:T(8,128)S(1)}, f32[4,4,16,128]{3,2,1,0:T(8,128)S(1)}, f32[4,4,16,128]{3,2,1,0:T(8,128)S(1)}, f32[4,4,16,128]{3,2,1,0:T(8,128)S(1)}) custom-call(f32[16,16]{1,0:T(8,128)S(1)} %broadcast_multiply_fusion.refs_0_, f32[4,4,16,128]{3,2,1,0:T(8,128)S(1)} %get-tuple-element.45.refs_1_, ...), custom_call_target="tpu_custom_call" | custom-call | flops 4194304 | bytes 1048576 | tf_op jit(solution)/shard_map/pallas_call | solution.py:170
  46.1 3.4 %collective-permute-start.16 = (f32[4,4,16,128]{3,2,1,0:T(8,128)S(1)}, f32[4,4,16,128]{3,2,1,0:T(8,128)S(1)}, u32[]{:S(2)}, u32[]{:S(2)}) collective-permute-start(f32[4,4,16,128]{3,2,1,0:T(8,128)S(1)} %get-tuple-element.50), channel_id=1, source_target_pairs={{0,24},{8,16},{16,8},{24,0},{1,25},{9,17},{17,9},{25,1},{2,26},{10... | collective-permute-start | bytes 393224 | tf_op jit(solution)/shard_map/ppermute | solution.py:141
  49.5 1.4 %collective-permute-start.18 = (f32[4,4,16,128]{3,2,1,0:T(8,128)S(1)}, f32[4,4,16,128]{3,2,1,0:T(8,128)S(1)}, u32[]{:S(2)}, u32[]{:S(2)}) collective-permute-start(f32[4,4,16,128]{3,2,1,0:T(8,128)S(1)} %get-tuple-element.52), channel_id=1, source_target_pairs={{0,8},{8,0},{16,24},{24,16},{1,9},{9,1},{17,25},{25,17},{2,10},{10... | collective-permute-start | bytes 393224 | tf_op jit(solution)/shard_map/ppermute | solution.py:141
  50.9 5.1 %collective-permute-done.7.refs_2_ = f32[4,4,16,128]{3,2,1,0:T(8,128)S(1)} collective-permute-done((f32[4,4,16,128]{3,2,1,0:T(8,128)S(1)}, f32[4,4,16,128]{3,2,1,0:T(8,128)S(1)}, u32[]{:S(2)}, u32[]{:S(2)}) %collective-permute-start.7) | collective-permute-done | bytes 131104 | tf_op jit(solution)/shard_map/ppermute | solution.py:141
  56.0 0.9 %shard_map.40.refs_0_ = f32[4,128,512]{2,1,0:T(8,128)} custom-call(f32[4,4,16,128]{3,2,1,0:T(8,128)S(1)} %get-tuple-element.37.refs_0_, f32[4,4,16,128]{3,2,1,0:T(8,128)S(1)} %collective-permute-done.6.refs_1_, f32[4,4,16,128]{3,2,1,0:T(8,128)S(1)} %collective-permute-done.7.refs_2_, f32[4,4,16,128]{3,2,1,0:T(8,128)S(1)} %collective-permute-done.8.refs_3_), custom_call_target="tpu_custom_call" | custom-call | flops 262144 | bytes 2097152 | tf_op jit(solution)/shard_map/pallas_call | solution.py:170
  56.9 4.0 %collective-permute-done.17.refs_3_ = f32[4,4,16,128]{3,2,1,0:T(8,128)S(1)} collective-permute-done((f32[4,4,16,128]{3,2,1,0:T(8,128)S(1)}, f32[4,4,16,128]{3,2,1,0:T(8,128)S(1)}, u32[]{:S(2)}, u32[]{:S(2)}) %collective-permute-start.17) | collective-permute-done | bytes 131104 | tf_op jit(solution)/shard_map/ppermute | solution.py:141
  60.9 0.9 %shard_map.43 = f32[4,128,512]{2,1,0:T(8,128)} custom-call(f32[4,128,512]{2,1,0:T(8,128)} %shard_map.40.refs_0_, f32[4,4,16,128]{3,2,1,0:T(8,128)S(1)} %get-tuple-element.49.refs_1_, f32[4,4,16,128]{3,2,1,0:T(8,128)S(1)} %collective-permute-done.16.refs_2_, f32[4,4,16,128]{3,2,1,0:T(8,128)S(1)} %collective-permute-done.17.refs_3_, ...), custom_call_target="tpu_custom_call", output_to_operand_aliasing={{}: (0, {})} | custom-call | flops 262144 | bytes 2097152 | tf_op jit(solution)/shard_map/pallas_call | solution.py:170
  (26 shorter events, 0.3 us)
Async XLA Ops:
  0.0 10.6 %copy-start = (s32[16]{0:T(128)S(1)}, s32[16]{0:T(128)}, u32[]{:S(2)}) copy-start(s32[16]{0:T(128)} %param.4) | copy-start | bytes 196
  1.7 9.6 %collective-permute-start = (f32[4,4,16,128]{3,2,1,0:T(8,128)S(1)}, f32[4,4,16,128]{3,2,1,0:T(8,128)S(1)}, u32[]{:S(2)}, u32[]{:S(2)}) collective-permute-start(f32[4,4,16,128]{3,2,1,0:T(8,128)S(1)} %get-tuple-element.30), channel_id=1, source_target_pairs={{0,24},{8,16},{16,8},{24,0},{1,25},{9,17},{17,9},{25,1},{2,26},{10... | collective-permute-start | bytes 393224 | tf_op jit(solution)/shard_map/ppermute | solution.py:141
  6.9 11.1 %collective-permute-start.1 = (f32[4,4,16,128]{3,2,1,0:T(8,128)S(1)}, f32[4,4,16,128]{3,2,1,0:T(8,128)S(1)}, u32[]{:S(2)}, u32[]{:S(2)}) collective-permute-start(f32[4,4,16,128]{3,2,1,0:T(8,128)S(1)} %get-tuple-element.31), channel_id=1, source_target_pairs={{0,16},{8,24},{16,0},{24,8},{1,17},{9,25},{17,1},{25,9},{2,18},{10... | collective-permute-start | bytes 393224 | tf_op jit(solution)/shard_map/ppermute | solution.py:141
  6.9 12.3 %collective-permute-start.2 = (f32[4,4,16,128]{3,2,1,0:T(8,128)S(1)}, f32[4,4,16,128]{3,2,1,0:T(8,128)S(1)}, u32[]{:S(2)}, u32[]{:S(2)}) collective-permute-start(f32[4,4,16,128]{3,2,1,0:T(8,128)S(1)} %get-tuple-element.32), channel_id=1, source_target_pairs={{0,8},{8,0},{16,24},{24,16},{1,9},{9,1},{17,25},{25,17},{2,10},{10... | collective-permute-start | bytes 393224 | tf_op jit(solution)/shard_map/ppermute | solution.py:141
  7.5 14.4 %collective-permute-start.9 = (f32[4,4,16,128]{3,2,1,0:T(8,128)S(1)}, f32[4,4,16,128]{3,2,1,0:T(8,128)S(1)}, u32[]{:S(2)}, u32[]{:S(2)}) collective-permute-start(f32[4,4,16,128]{3,2,1,0:T(8,128)S(1)} %get-tuple-element.41), channel_id=1, source_target_pairs={{0,3},{1,2},{2,1},{3,0},{4,7},{5,6},{6,5},{7,4},{8,11},{9,10},{10,... | collective-permute-start | bytes 393224 | tf_op jit(solution)/shard_map/ppermute | solution.py:141
  7.9 14.6 %collective-permute-start.10 = (f32[4,4,16,128]{3,2,1,0:T(8,128)S(1)}, f32[4,4,16,128]{3,2,1,0:T(8,128)S(1)}, u32[]{:S(2)}, u32[]{:S(2)}) collective-permute-start(f32[4,4,16,128]{3,2,1,0:T(8,128)S(1)} %get-tuple-element.42), channel_id=1, source_target_pairs={{0,5},{1,4},{2,7},{3,6},{4,1},{5,0},{6,3},{7,2},{8,13},{9,12},{10,... | collective-permute-start | bytes 393224 | tf_op jit(solution)/shard_map/ppermute | solution.py:141
  11.3 11.6 %collective-permute-start.11 = (f32[4,4,16,128]{3,2,1,0:T(8,128)S(1)}, f32[4,4,16,128]{3,2,1,0:T(8,128)S(1)}, u32[]{:S(2)}, u32[]{:S(2)}) collective-permute-start(f32[4,4,16,128]{3,2,1,0:T(8,128)S(1)} %get-tuple-element.43), channel_id=1, source_target_pairs={{0,6},{1,7},{2,4},{3,5},{4,2},{5,3},{6,0},{7,1},{8,14},{9,15},{10,... | collective-permute-start | bytes 393224 | tf_op jit(solution)/shard_map/ppermute | solution.py:141
  17.9 6.6 %collective-permute-start.12 = (f32[4,4,16,128]{3,2,1,0:T(8,128)S(1)}, f32[4,4,16,128]{3,2,1,0:T(8,128)S(1)}, u32[]{:S(2)}, u32[]{:S(2)}) collective-permute-start(f32[4,4,16,128]{3,2,1,0:T(8,128)S(1)} %get-tuple-element.44), channel_id=1, source_target_pairs={{0,7},{1,6},{2,5},{3,4},{4,3},{5,2},{6,1},{7,0},{8,15},{9,14},{10,... | collective-permute-start | bytes 393224 | tf_op jit(solution)/shard_map/ppermute | solution.py:141
  20.5 6.6 %collective-permute-start.3 = (f32[4,4,16,128]{3,2,1,0:T(8,128)S(1)}, f32[4,4,16,128]{3,2,1,0:T(8,128)S(1)}, u32[]{:S(2)}, u32[]{:S(2)}) collective-permute-start(f32[4,4,16,128]{3,2,1,0:T(8,128)S(1)} %get-tuple-element.34), channel_id=1, source_target_pairs={{0,1},{1,0},{2,3},{3,2},{4,5},{5,4},{6,7},{7,6},{8,9},{9,8},{10,11... | collective-permute-start | bytes 393224 | tf_op jit(solution)/shard_map/ppermute | solution.py:141
  21.9 7.1 %collective-permute-start.4 = (f32[4,4,16,128]{3,2,1,0:T(8,128)S(1)}, f32[4,4,16,128]{3,2,1,0:T(8,128)S(1)}, u32[]{:S(2)}, u32[]{:S(2)}) collective-permute-start(f32[4,4,16,128]{3,2,1,0:T(8,128)S(1)} %get-tuple-element.35), channel_id=1, source_target_pairs={{0,2},{1,3},{2,0},{3,1},{4,6},{5,7},{6,4},{7,5},{8,10},{9,11},{10,... | collective-permute-start | bytes 393224 | tf_op jit(solution)/shard_map/ppermute | solution.py:141
  22.4 6.6 %collective-permute-start.5 = (f32[4,4,16,128]{3,2,1,0:T(8,128)S(1)}, f32[4,4,16,128]{3,2,1,0:T(8,128)S(1)}, u32[]{:S(2)}, u32[]{:S(2)}) collective-permute-start(f32[4,4,16,128]{3,2,1,0:T(8,128)S(1)} %get-tuple-element.36), channel_id=1, source_target_pairs={{0,4},{1,5},{2,6},{3,7},{4,0},{5,1},{6,2},{7,3},{8,12},{9,13},{10,... | collective-permute-start | bytes 393224 | tf_op jit(solution)/shard_map/ppermute | solution.py:141
  24.6 8.4 %collective-permute-start.13 = (f32[4,4,16,128]{3,2,1,0:T(8,128)S(1)}, f32[4,4,16,128]{3,2,1,0:T(8,128)S(1)}, u32[]{:S(2)}, u32[]{:S(2)}) collective-permute-start(f32[4,4,16,128]{3,2,1,0:T(8,128)S(1)} %get-tuple-element.46), channel_id=1, source_target_pairs={{0,24},{8,16},{16,8},{24,0},{1,25},{9,17},{17,9},{25,1},{2,26},{10... | collective-permute-start | bytes 393224 | tf_op jit(solution)/shard_map/ppermute | solution.py:141
  27.1 17.6 %collective-permute-start.14 = (f32[4,4,16,128]{3,2,1,0:T(8,128)S(1)}, f32[4,4,16,128]{3,2,1,0:T(8,128)S(1)}, u32[]{:S(2)}, u32[]{:S(2)}) collective-permute-start(f32[4,4,16,128]{3,2,1,0:T(8,128)S(1)} %get-tuple-element.47), channel_id=1, source_target_pairs={{0,16},{8,24},{16,0},{24,8},{1,17},{9,25},{17,1},{25,9},{2,18},{10... | collective-permute-start | bytes 393224 | tf_op jit(solution)/shard_map/ppermute | solution.py:141
  27.1 17.6 %collective-permute-start.15 = (f32[4,4,16,128]{3,2,1,0:T(8,128)S(1)}, f32[4,4,16,128]{3,2,1,0:T(8,128)S(1)}, u32[]{:S(2)}, u32[]{:S(2)}) collective-permute-start(f32[4,4,16,128]{3,2,1,0:T(8,128)S(1)} %get-tuple-element.48), channel_id=1, source_target_pairs={{0,8},{8,0},{16,24},{24,16},{1,9},{9,1},{17,25},{25,17},{2,10},{10... | collective-permute-start | bytes 393224 | tf_op jit(solution)/shard_map/ppermute | solution.py:141
  29.1 20.4 %collective-permute-start.6 = (f32[4,4,16,128]{3,2,1,0:T(8,128)S(1)}, f32[4,4,16,128]{3,2,1,0:T(8,128)S(1)}, u32[]{:S(2)}, u32[]{:S(2)}) collective-permute-start(f32[4,4,16,128]{3,2,1,0:T(8,128)S(1)} %get-tuple-element.38), channel_id=1, source_target_pairs={{0,24},{8,16},{16,8},{24,0},{1,25},{9,17},{17,9},{25,1},{2,26},{10... | collective-permute-start | bytes 393224 | tf_op jit(solution)/shard_map/ppermute | solution.py:141
  31.6 24.4 %collective-permute-start.7 = (f32[4,4,16,128]{3,2,1,0:T(8,128)S(1)}, f32[4,4,16,128]{3,2,1,0:T(8,128)S(1)}, u32[]{:S(2)}, u32[]{:S(2)}) collective-permute-start(f32[4,4,16,128]{3,2,1,0:T(8,128)S(1)} %get-tuple-element.39), channel_id=1, source_target_pairs={{0,16},{8,24},{16,0},{24,8},{1,17},{9,25},{17,1},{25,9},{2,18},{10... | collective-permute-start | bytes 393224 | tf_op jit(solution)/shard_map/ppermute | solution.py:141
  32.9 23.1 %collective-permute-start.8 = (f32[4,4,16,128]{3,2,1,0:T(8,128)S(1)}, f32[4,4,16,128]{3,2,1,0:T(8,128)S(1)}, u32[]{:S(2)}, u32[]{:S(2)}) collective-permute-start(f32[4,4,16,128]{3,2,1,0:T(8,128)S(1)} %get-tuple-element.40), channel_id=1, source_target_pairs={{0,8},{8,0},{16,24},{24,16},{1,9},{9,1},{17,25},{25,17},{2,10},{10... | collective-permute-start | bytes 393224 | tf_op jit(solution)/shard_map/ppermute | solution.py:141
  46.1 10.8 %collective-permute-start.16 = (f32[4,4,16,128]{3,2,1,0:T(8,128)S(1)}, f32[4,4,16,128]{3,2,1,0:T(8,128)S(1)}, u32[]{:S(2)}, u32[]{:S(2)}) collective-permute-start(f32[4,4,16,128]{3,2,1,0:T(8,128)S(1)} %get-tuple-element.50), channel_id=1, source_target_pairs={{0,24},{8,16},{16,8},{24,0},{1,25},{9,17},{17,9},{25,1},{2,26},{10... | collective-permute-start | bytes 393224 | tf_op jit(solution)/shard_map/ppermute | solution.py:141
  49.5 11.4 %collective-permute-start.17 = (f32[4,4,16,128]{3,2,1,0:T(8,128)S(1)}, f32[4,4,16,128]{3,2,1,0:T(8,128)S(1)}, u32[]{:S(2)}, u32[]{:S(2)}) collective-permute-start(f32[4,4,16,128]{3,2,1,0:T(8,128)S(1)} %get-tuple-element.51), channel_id=1, source_target_pairs={{0,16},{8,24},{16,0},{24,8},{1,17},{9,25},{17,1},{25,9},{2,18},{10... | collective-permute-start | bytes 393224 | tf_op jit(solution)/shard_map/ppermute | solution.py:141
  49.5 11.4 %collective-permute-start.18 = (f32[4,4,16,128]{3,2,1,0:T(8,128)S(1)}, f32[4,4,16,128]{3,2,1,0:T(8,128)S(1)}, u32[]{:S(2)}, u32[]{:S(2)}) collective-permute-start(f32[4,4,16,128]{3,2,1,0:T(8,128)S(1)} %get-tuple-element.52), channel_id=1, source_target_pairs={{0,8},{8,0},{16,24},{24,16},{1,9},{9,1},{17,25},{25,17},{2,10},{10... | collective-permute-start | bytes 393224 | tf_op jit(solution)/shard_map/ppermute | solution.py:141

commit v3 on v2

--- a/solution.py
+++ b/solution.py
@@ -41,9 +41,10 @@
     def __init__(self, mesh):
         self.shares, self.rows = mesh.shape["share"], mesh.shape["row"]
         self.share = [0, *range(self.shares - 1, 0, -1)]
-        hops = range(self.rows)
-        self.near = [hop for hop in hops if hop.bit_count() <= 1]
-        self.far = [hop for hop in hops if hop.bit_count() > 1]
+        others = range(2, self.rows)
+        self.near = [0, 1]
+        self.middle = [hop for hop in others if hop.bit_count() % 2 == 1]
+        self.far = [hop for hop in others if hop.bit_count() % 2 == 0]
 
 
 class Sizes:
@@ -65,8 +66,9 @@
 
 
 def cut(z, hops, starts, pieces, *refs):
-    near, far = refs[: z.shares], refs[z.shares : z.shares + len(hops.far)]
-    firsts, columns, sems = refs[z.shares + len(hops.far) :]
+    count = 2 * z.shares + len(hops.far)
+    near, middle, far = refs[: z.shares], refs[z.shares : 2 * z.shares], refs[2 * z.shares : count]
+    firsts, columns, sems = refs[count:]
     share, row = lax.axis_index("share"), lax.axis_index("row")
     copies = [pltpu.make_async_copy(starts, firsts, sems.at[0])]
     for n in range(z.held):
@@ -83,9 +85,10 @@
 
     for copy in copies[1:]:
         copy.wait()
-    for m, share_hop in enumerate(hops.share):
-        for p, row_hop in enumerate(hops.near):
-            near[m][p] = part(row_hop, share_hop)
+    for early, rows in ((near, hops.near), (middle, hops.middle)):
+        for m, share_hop in enumerate(hops.share):
+            for p, row_hop in enumerate(rows):
+                early[m][p] = part(row_hop, share_hop)
     for p, row_hop in enumerate(hops.far):
         for m, share_hop in enumerate(hops.share):
             far[p][m] = part(row_hop, share_hop)
@@ -118,16 +121,18 @@
                 outs[m][:, k] = total
 
 
-def place(z, hops, rows, *refs):
-    ins, out, sems = refs[-z.shares - 2 : -2], refs[-2], refs[-1]
+def place(z, hops, chunks, *refs):
+    ins, out, sems = refs[-len(chunks) * z.shares - 2 : -2], refs[-2], refs[-1]
     share, row = lax.axis_index("share"), lax.axis_index("row")
     copies = []
-    for m, share_hop in enumerate(hops.share):
-        for p, row_hop in enumerate(rows):
-            line = pl.multiple_of((row ^ row_hop) * z.depth, 8)
-            column = pl.multiple_of((share ^ share_hop) * z.part, 128)
-            there = out.at[:, pl.ds(line, z.depth), pl.ds(column, z.part)]
-            copies.append(pltpu.make_async_copy(ins[m].at[p], there, sems.at[m, p]))
+    for n, rows in enumerate(chunks):
+        for m, share_hop in enumerate(hops.share):
+            for p, row_hop in enumerate(rows):
+                line = pl.multiple_of((row ^ row_hop) * z.depth, 8)
+                column = pl.multiple_of((share ^ share_hop) * z.part, 128)
+                there = out.at[:, pl.ds(line, z.depth), pl.ds(column, z.part)]
+                here = ins[n * z.shares + m].at[p]
+                copies.append(pltpu.make_async_copy(here, there, sems.at[len(copies)]))
     for copy in copies:
         copy.start()
     for copy in copies:
@@ -163,7 +168,7 @@
 
 def tiled_body(z, hops, pieces, alive, starts):
     weights = recovery_operator(alive)
-    near, far, shares = len(hops.near), len(hops.far), z.shares
+    shares = z.shares
 
     def call(kernel, outs, ins, in_specs, out_specs, scratch=(), flops=0, **more):
         words = sum(math.prod(out.shape) for out in jax.tree.leaves(outs))
@@ -205,16 +210,22 @@
             flops=2 * K * rows * K * z.depth * z.part,
         )
 
-    def placed(arrays, rows, base=()):
+    def placed(arrays, chunks, base=()):
+        copies = shares * sum(len(rows) for rows in chunks)
         return call(
-            lambda z, hops, *refs: place(z, hops, rows, *refs),
+            lambda z, hops, *refs: place(z, hops, chunks, *refs),
             floats(z.kept, z.rows * z.depth, z.width),
             (*base, *arrays),
-            [ANY] * len(base) + [VMEM] * shares,
+            [ANY] * len(base) + [VMEM] * len(arrays),
             ANY,
-            [pltpu.SemaphoreType.DMA((shares, len(rows)))],
+            [pltpu.SemaphoreType.DMA((copies,))],
             input_output_aliases={0: 0} if base else {},
         )
+
+    def mixed_and_crossed(arrays, rows):
+        arrays = mixed(arrays, len(rows), True)
+        arrays = over_rows(arrays, rows)
+        return regrouped(arrays, z.kept)
 
     in_hbm = [pltpu.with_memory_space_constraint(a, pltpu.HBM) for a in (starts, pieces)]
     scratch = [
@@ -222,16 +233,18 @@
         pltpu.VMEM((z.held, z.depth, z.columns), jnp.float32),
         pltpu.SemaphoreType.DMA((z.held + 1,)),
     ]
-    parts = slots(shares, near, z.held) + [floats(shares, z.held, z.depth, z.part)] * far
+    parts = slots(shares, len(hops.near), z.held) + slots(shares, len(hops.middle), z.held)
+    parts += slots(len(hops.far), shares, z.held)
     parts = call(cut, parts, in_hbm, [ANY, ANY], [VMEM] * len(parts), scratch)
-    first = over_shares(parts[:shares])
-    second = over_rows(parts[shares:], hops.far)
-    second = over_shares(regrouped(second, z.held))
-    first = over_rows(mixed(first, near, True), hops.near)
-    first = over_shares(regrouped(first, z.kept))
-    second = over_shares(mixed(second, far, False))
-    out = placed(first, hops.near)
-    return placed(second, hops.far, (out,))
+    near = over_shares(parts[:shares])
+    middle = over_shares(parts[shares : 2 * shares])
+    far = over_rows(parts[2 * shares :], hops.far)
+    near = over_shares(mixed_and_crossed(near, hops.near))
+    far = over_shares(regrouped(far, z.held))
+    middle = over_shares(mixed_and_crossed(middle, hops.middle))
+    far = over_shares(mixed(far, len(hops.far), False))
+    out = placed(near + middle, [hops.near, hops.middle])
+    return placed(far, [hops.far], (out,))
 
 
 def solution(mesh):

time: 62 us -> 64.4 us (1.039)
  starting transfers between devices: 30.7 us -> 34.9 us
  waiting for transfers between devices: 24 us -> 21.4 us
  Pallas kernels: 6.25 us -> 7.12 us
    ppermute x19 -> x25, starting transfers between devices: 30.7 us -> 34.9 us  [exchange(): out.append(lax.ppermute(array, axis, pairs) if hop else array)]
    ppermute x19 -> x25, waiting for transfers between devices: 24 us -> 21.4 us  [exchange(): out.append(lax.ppermute(array, axis, pairs) if hop else array)]
    pallas_call x7 -> x9, Pallas kernels: 6.25 us -> 7.12 us  [call(): pl.pallas_call(functools.partial(kernel, z, hops), out_shape=outs, in_spe...]
  transfers between devices with their start and end apart: 19 -> 25, of which waited for: 7 -> 9; matrix products, arithmetic and copies ran while one was open for 1% -> 1% of each run, Pallas kernels for 6% -> 7%
where the time goes in v3:
time: 64.4 us; the launch traced here: 64.3 us
  starting transfers between devices  34.9 us (54%)
  waiting for transfers between devices  21.4 us (33%)
  Pallas kernels  7.12 us (11%)
  other arithmetic  0.76 us (1%)
    ppermute x25, starting transfers between devices, exchange(): out.append(lax.ppermute(array, axis, pairs) if hop else array)  34.9 us
    ppermute x25, waiting for transfers between devices, exchange(): out.append(lax.ppermute(array, axis, pairs) if hop else array)  21.4 us
    pallas_call x9, Pallas kernels, call(): pl.pallas_call(functools.partial(kernel, z, hops), out_shape=outs, in_spe...  7.12 us
  transfers between devices with their start and end apart: 25, of which 9 were waited for; matrix products, arithmetic and copies ran while one was open for 1% of the time, Pallas kernels for 7%

profile of v3, /device:TPU:0, one launch (start us, length us, event | category | flops | bytes accessed | tf_op | source)
XLA Modules:
  0.0 64.3 jit_solution(687958077398992720)
XLA Ops:
  0.0 1.7 %shard_map.37 = (f32[2,4,16,128]{3,2,1,0:T(8,128)S(1)}, f32[2,4,16,128]{3,2,1,0:T(8,128)S(1)}, f32[2,4,16,128]{3,2,1,0:T(8,128)S(1)}, f32[2,4,16,128]{3,2,1,0:T(...) custom-call(s32[2]{0:T(128)} %starts.1, ...), custom_call_target="tpu_custom_call" | custom-call | flops 262144 | bytes 2097152 | tf_op jit(solution)/shard_map/pallas_call | solution.py:175
  1.7 5.1 %collective-permute-start = (f32[2,4,16,128]{3,2,1,0:T(8,128)S(1)}, f32[2,4,16,128]{3,2,1,0:T(8,128)S(1)}, u32[]{:S(2)}, u32[]{:S(2)}) collective-permute-start(f32[2,4,16,128]{3,2,1,0:T(8,128)S(1)} %get-tuple-element.38), channel_id=1, source_target_pairs={{0,24},{8,16},{16,8},{24,0},{1,25},{9,17},{17,9},{25,1},{2,26},{10... | collective-permute-start | bytes 196616 | tf_op jit(solution)/shard_map/ppermute | solution.py:146
  7.5 3.7 %collective-permute-start.7 = (f32[3,4,16,128]{3,2,1,0:T(8,128)S(1)}, f32[3,4,16,128]{3,2,1,0:T(8,128)S(1)}, u32[]{:S(2)}, u32[]{:S(2)}) collective-permute-start(f32[3,4,16,128]{3,2,1,0:T(8,128)S(1)} %get-tuple-element.48), channel_id=1, source_target_pairs={{0,24},{8,16},{16,8},{24,0},{1,25},{9,17},{17,9},{25,1},{2,26},{10... | collective-permute-start | bytes 294920 | tf_op jit(solution)/shard_map/ppermute | solution.py:146
  12.0 0.7 %collective-permute-start.9 = (f32[3,4,16,128]{3,2,1,0:T(8,128)S(1)}, f32[3,4,16,128]{3,2,1,0:T(8,128)S(1)}, u32[]{:S(2)}, u32[]{:S(2)}) collective-permute-start(f32[3,4,16,128]{3,2,1,0:T(8,128)S(1)} %get-tuple-element.50), channel_id=1, source_target_pairs={{0,8},{8,0},{16,24},{24,16},{1,9},{9,1},{17,25},{25,17},{2,10},{10... | collective-permute-start | bytes 294920 | tf_op jit(solution)/shard_map/ppermute | solution.py:146
  12.7 3.3 %collective-permute-done.7.refs_2_ = f32[3,4,16,128]{3,2,1,0:T(8,128)S(1)} collective-permute-done((f32[3,4,16,128]{3,2,1,0:T(8,128)S(1)}, f32[3,4,16,128]{3,2,1,0:T(8,128)S(1)}, u32[]{:S(2)}, u32[]{:S(2)}) %collective-permute-start.7) | collective-permute-done | bytes 98336 | tf_op jit(solution)/shard_map/ppermute | solution.py:146
  16.0 4.9 %collective-permute-done.8.refs_3_ = f32[3,4,16,128]{3,2,1,0:T(8,128)S(1)} collective-permute-done((f32[3,4,16,128]{3,2,1,0:T(8,128)S(1)}, f32[3,4,16,128]{3,2,1,0:T(8,128)S(1)}, u32[]{:S(2)}, u32[]{:S(2)}) %collective-permute-start.8) | collective-permute-done | bytes 98336 | tf_op jit(solution)/shard_map/ppermute | solution.py:146
  20.9 0.9 %collective-permute-start.17 = (f32[4,4,16,128]{3,2,1,0:T(8,128)S(1)}, f32[4,4,16,128]{3,2,1,0:T(8,128)S(1)}, u32[]{:S(2)}, u32[]{:S(2)}) collective-permute-start(f32[4,4,16,128]{3,2,1,0:T(8,128)S(1)} %get-tuple-element.59), channel_id=1, source_target_pairs={{0,5},{1,4},{2,7},{3,6},{4,1},{5,0},{6,3},{7,2},{8,13},{9,12},{10,... | collective-permute-start | bytes 393224 | tf_op jit(solution)/shard_map/ppermute | solution.py:146
  21.9 1.6 %collective-permute-start.18 = (f32[4,4,16,128]{3,2,1,0:T(8,128)S(1)}, f32[4,4,16,128]{3,2,1,0:T(8,128)S(1)}, u32[]{:S(2)}, u32[]{:S(2)}) collective-permute-start(f32[4,4,16,128]{3,2,1,0:T(8,128)S(1)} %get-tuple-element.60), channel_id=1, source_target_pairs={{0,6},{1,7},{2,4},{3,5},{4,2},{5,3},{6,0},{7,1},{8,14},{9,15},{10,... | collective-permute-start | bytes 393224 | tf_op jit(solution)/shard_map/ppermute | solution.py:146
  23.4 1.2 %shard_map.40 = (f32[4,4,16,128]{3,2,1,0:T(8,128)S(1)}, f32[4,4,16,128]{3,2,1,0:T(8,128)S(1)}, f32[4,4,16,128]{3,2,1,0:T(8,128)S(1)}) custom-call(f32[16,16]{1,0:T(8,128)S(1)} %broadcast_multiply_fusion.refs_0_, f32[3,4,16,128]{3,2,1,0:T(8,128)S(1)} %get-tuple-element.47.refs_1_, f32[3,4,16,128]{3,2,1,0:T(8,128)S(1)} %collective-permute-done.7.refs_2_, ...), custom_call_target="tpu_custom_call" | custom-call | flops 3145728 | bytes 786432 | tf_op jit(solution)/shard_map/pallas_call | solution.py:175
  25.2 1.4 %collective-permute-start.11 = (f32[4,4,16,128]{3,2,1,0:T(8,128)S(1)}, f32[4,4,16,128]{3,2,1,0:T(8,128)S(1)}, u32[]{:S(2)}, u32[]{:S(2)}) collective-permute-start(f32[4,4,16,128]{3,2,1,0:T(8,128)S(1)} %get-tuple-element.52), channel_id=1, source_target_pairs={{0,4},{1,5},{2,6},{3,7},{4,0},{5,1},{6,2},{7,3},{8,12},{9,13},{10,... | collective-permute-start | bytes 393224 | tf_op jit(solution)/shard_map/ppermute | solution.py:146
  26.7 0.9 %collective-permute-start.12 = (f32[4,4,16,128]{3,2,1,0:T(8,128)S(1)}, f32[4,4,16,128]{3,2,1,0:T(8,128)S(1)}, u32[]{:S(2)}, u32[]{:S(2)}) collective-permute-start(f32[4,4,16,128]{3,2,1,0:T(8,128)S(1)} %get-tuple-element.53), channel_id=1, source_target_pairs={{0,7},{1,6},{2,5},{3,4},{4,3},{5,2},{6,1},{7,0},{8,15},{9,14},{10,... | collective-permute-start | bytes 393224 | tf_op jit(solution)/shard_map/ppermute | solution.py:146
  27.6 1.1 %shard_map.38 = (f32[4,4,16,128]{3,2,1,0:T(8,128)S(1)}, f32[4,4,16,128]{3,2,1,0:T(8,128)S(1)}) custom-call(f32[16,16]{1,0:T(8,128)S(1)} %broadcast_multiply_fusion.refs_0_, f32[2,4,16,128]{3,2,1,0:T(8,128)S(1)} %get-tuple-element.37.refs_1_, f32[2,4,16,128]{3,2,1,0:T(8,128)S(1)} %collective-permute-done.refs_2_, ...), custom_call_target="tpu_custom_call" | custom-call | flops 2097152 | bytes 524288 | tf_op jit(solution)/shard_map/pallas_call | solution.py:175
  28.7 0.7 %collective-permute-done.17.refs_1_ = f32[4,4,16,128]{3,2,1,0:T(8,128)S(1)} collective-permute-done((f32[4,4,16,128]{3,2,1,0:T(8,128)S(1)}, f32[4,4,16,128]{3,2,1,0:T(8,128)S(1)}, u32[]{:S(2)}, u32[]{:S(2)}) %collective-permute-start.17) | collective-permute-done | bytes 131104 | tf_op jit(solution)/shard_map/ppermute | solution.py:146
  29.7 2.8 %collective-permute-start.19 = (f32[3,4,16,128]{3,2,1,0:T(8,128)S(1)}, f32[3,4,16,128]{3,2,1,0:T(8,128)S(1)}, u32[]{:S(2)}, u32[]{:S(2)}) collective-permute-start(f32[3,4,16,128]{3,2,1,0:T(8,128)S(1)} %get-tuple-element.62), channel_id=1, source_target_pairs={{0,24},{8,16},{16,8},{24,0},{1,25},{9,17},{17,9},{25,1},{2,26},{10... | collective-permute-start | bytes 294920 | tf_op jit(solution)/shard_map/ppermute | solution.py:146
  32.5 0.8 %collective-permute-start.20 = (f32[3,4,16,128]{3,2,1,0:T(8,128)S(1)}, f32[3,4,16,128]{3,2,1,0:T(8,128)S(1)}, u32[]{:S(2)}, u32[]{:S(2)}) collective-permute-start(f32[3,4,16,128]{3,2,1,0:T(8,128)S(1)} %get-tuple-element.63), channel_id=1, source_target_pairs={{0,16},{8,24},{16,0},{24,8},{1,17},{9,25},{17,1},{25,9},{2,18},{10... | collective-permute-start | bytes 294920 | tf_op jit(solution)/shard_map/ppermute | solution.py:146
  33.3 1.8 %collective-permute-done.11.refs_1_ = f32[4,4,16,128]{3,2,1,0:T(8,128)S(1)} collective-permute-done((f32[4,4,16,128]{3,2,1,0:T(8,128)S(1)}, f32[4,4,16,128]{3,2,1,0:T(8,128)S(1)}, u32[]{:S(2)}, u32[]{:S(2)}) %collective-permute-start.11) | collective-permute-done | bytes 131104 | tf_op jit(solution)/shard_map/ppermute | solution.py:146
  35.2 2.8 %collective-permute-start.13 = (f32[3,4,16,128]{3,2,1,0:T(8,128)S(1)}, f32[3,4,16,128]{3,2,1,0:T(8,128)S(1)}, u32[]{:S(2)}, u32[]{:S(2)}) collective-permute-start(f32[3,4,16,128]{3,2,1,0:T(8,128)S(1)} %get-tuple-element.55), channel_id=1, source_target_pairs={{0,24},{8,16},{16,8},{24,0},{1,25},{9,17},{17,9},{25,1},{2,26},{10... | collective-permute-start | bytes 294920 | tf_op jit(solution)/shard_map/ppermute | solution.py:146
  38.0 1.2 %collective-permute-start.4 = (f32[2,4,16,128]{3,2,1,0:T(8,128)S(1)}, f32[2,4,16,128]{3,2,1,0:T(8,128)S(1)}, u32[]{:S(2)}, u32[]{:S(2)}) collective-permute-start(f32[2,4,16,128]{3,2,1,0:T(8,128)S(1)} %get-tuple-element.44), channel_id=1, source_target_pairs={{0,24},{8,16},{16,8},{24,0},{1,25},{9,17},{17,9},{25,1},{2,26},{10... | collective-permute-start | bytes 196616 | tf_op jit(solution)/shard_map/ppermute | solution.py:146
  39.1 1.5 %collective-permute-start.5 = (f32[2,4,16,128]{3,2,1,0:T(8,128)S(1)}, f32[2,4,16,128]{3,2,1,0:T(8,128)S(1)}, u32[]{:S(2)}, u32[]{:S(2)}) collective-permute-start(f32[2,4,16,128]{3,2,1,0:T(8,128)S(1)} %get-tuple-element.45), channel_id=1, source_target_pairs={{0,16},{8,24},{16,0},{24,8},{1,17},{9,25},{17,1},{25,9},{2,18},{10... | collective-permute-start | bytes 196616 | tf_op jit(solution)/shard_map/ppermute | solution.py:146
  40.6 0.9 %collective-permute-done.20.refs_3_ = f32[3,4,16,128]{3,2,1,0:T(8,128)S(1)} collective-permute-done((f32[3,4,16,128]{3,2,1,0:T(8,128)S(1)}, f32[3,4,16,128]{3,2,1,0:T(8,128)S(1)}, u32[]{:S(2)}, u32[]{:S(2)}) %collective-permute-start.20) | collective-permute-done | bytes 98336 | tf_op jit(solution)/shard_map/ppermute | solution.py:146
  41.5 0.9 %collective-permute-start.6 = (f32[2,4,16,128]{3,2,1,0:T(8,128)S(1)}, f32[2,4,16,128]{3,2,1,0:T(8,128)S(1)}, u32[]{:S(2)}, u32[]{:S(2)}) collective-permute-start(f32[2,4,16,128]{3,2,1,0:T(8,128)S(1)} %get-tuple-element.46), channel_id=1, source_target_pairs={{0,8},{8,0},{16,24},{24,16},{1,9},{9,1},{17,25},{25,17},{2,10},{10... | collective-permute-start | bytes 196616 | tf_op jit(solution)/shard_map/ppermute | solution.py:146
  42.4 3.7 %collective-permute-done.21.refs_4_ = f32[3,4,16,128]{3,2,1,0:T(8,128)S(1)} collective-permute-done((f32[3,4,16,128]{3,2,1,0:T(8,128)S(1)}, f32[3,4,16,128]{3,2,1,0:T(8,128)S(1)}, u32[]{:S(2)}, u32[]{:S(2)}) %collective-permute-start.21) | collective-permute-done | bytes 98336 | tf_op jit(solution)/shard_map/ppermute | solution.py:146
  46.1 2.4 %collective-permute-start.14 = (f32[3,4,16,128]{3,2,1,0:T(8,128)S(1)}, f32[3,4,16,128]{3,2,1,0:T(8,128)S(1)}, u32[]{:S(2)}, u32[]{:S(2)}) collective-permute-start(f32[3,4,16,128]{3,2,1,0:T(8,128)S(1)} %get-tuple-element.56), channel_id=1, source_target_pairs={{0,16},{8,24},{16,0},{24,8},{1,17},{9,25},{17,1},{25,9},{2,18},{10... | collective-permute-start | bytes 294920 | tf_op jit(solution)/shard_map/ppermute | solution.py:146
  48.5 1.2 %shard_map.44 = (f32[3,4,16,128]{3,2,1,0:T(8,128)S(1)}, f32[3,4,16,128]{3,2,1,0:T(8,128)S(1)}, f32[3,4,16,128]{3,2,1,0:T(8,128)S(1)}, f32[3,4,16,128]{3,2,1,0:T(8,128)S(1)}) custom-call(f32[16,16]{1,0:T(8,128)S(1)} %broadcast_multiply_fusion.refs_0_, f32[3,4,16,128]{3,2,1,0:T(8,128)S(1)} %get-tuple-element.61.refs_1_, ...), custom_call_target="tpu_custom_call" | custom-call | flops 3145728 | bytes 786432 | tf_op jit(solution)/shard_map/pallas_call | solution.py:175
  49.7 2.3 %collective-permute-start.15 = (f32[3,4,16,128]{3,2,1,0:T(8,128)S(1)}, f32[3,4,16,128]{3,2,1,0:T(8,128)S(1)}, u32[]{:S(2)}, u32[]{:S(2)}) collective-permute-start(f32[3,4,16,128]{3,2,1,0:T(8,128)S(1)} %get-tuple-element.57), channel_id=1, source_target_pairs={{0,8},{8,0},{16,24},{24,16},{1,9},{9,1},{17,25},{25,17},{2,10},{10... | collective-permute-start | bytes 294920 | tf_op jit(solution)/shard_map/ppermute | solution.py:146
  52.0 0.9 %collective-permute-done.5.refs_2_ = f32[2,4,16,128]{3,2,1,0:T(8,128)S(1)} collective-permute-done((f32[2,4,16,128]{3,2,1,0:T(8,128)S(1)}, f32[2,4,16,128]{3,2,1,0:T(8,128)S(1)}, u32[]{:S(2)}, u32[]{:S(2)}) %collective-permute-start.5) | collective-permute-done | bytes 65568 | tf_op jit(solution)/shard_map/ppermute | solution.py:146
  52.9 2.7 %collective-permute-start.22 = (f32[3,4,16,128]{3,2,1,0:T(8,128)S(1)}, f32[3,4,16,128]{3,2,1,0:T(8,128)S(1)}, u32[]{:S(2)}, u32[]{:S(2)}) collective-permute-start(f32[3,4,16,128]{3,2,1,0:T(8,128)S(1)} %get-tuple-element.66), channel_id=1, source_target_pairs={{0,24},{8,16},{16,8},{24,0},{1,25},{9,17},{17,9},{25,1},{2,26},{10... | collective-permute-start | bytes 294920 | tf_op jit(solution)/shard_map/ppermute | solution.py:146
  55.7 1.7 %collective-permute-start.24 = (f32[3,4,16,128]{3,2,1,0:T(8,128)S(1)}, f32[3,4,16,128]{3,2,1,0:T(8,128)S(1)}, u32[]{:S(2)}, u32[]{:S(2)}) collective-permute-start(f32[3,4,16,128]{3,2,1,0:T(8,128)S(1)} %get-tuple-element.68), channel_id=1, source_target_pairs={{0,8},{8,0},{16,24},{24,16},{1,9},{9,1},{17,25},{25,17},{2,10},{10... | collective-permute-start | bytes 294920 | tf_op jit(solution)/shard_map/ppermute | solution.py:146
  57.3 1.0 %shard_map.42.refs_0_ = f32[4,128,512]{2,1,0:T(8,128)} custom-call(f32[2,4,16,128]{3,2,1,0:T(8,128)S(1)} %get-tuple-element.43.refs_0_, f32[2,4,16,128]{3,2,1,0:T(8,128)S(1)} %collective-permute-done.4.refs_1_, f32[2,4,16,128]{3,2,1,0:T(8,128)S(1)} %collective-permute-done.5.refs_2_, f32[2,4,16,128]{3,2,1,0:T(8,128)S(1)} %collective-permute-done.6.refs_3_, ...), custom_call_target="tpu_custom_call" | custom-call | flops 262144 | bytes 2097152 | tf_op jit(solution)/shard_map/pallas_call | solution.py:175
  58.3 2.1 %collective-permute-done.22.refs_2_ = f32[3,4,16,128]{3,2,1,0:T(8,128)S(1)} collective-permute-done((f32[3,4,16,128]{3,2,1,0:T(8,128)S(1)}, f32[3,4,16,128]{3,2,1,0:T(8,128)S(1)}, u32[]{:S(2)}, u32[]{:S(2)}) %collective-permute-start.22) | collective-permute-done | bytes 98336 | tf_op jit(solution)/shard_map/ppermute | solution.py:146
  60.4 3.0 %collective-permute-done.23.refs_3_ = f32[3,4,16,128]{3,2,1,0:T(8,128)S(1)} collective-permute-done((f32[3,4,16,128]{3,2,1,0:T(8,128)S(1)}, f32[3,4,16,128]{3,2,1,0:T(8,128)S(1)}, u32[]{:S(2)}, u32[]{:S(2)}) %collective-permute-start.23) | collective-permute-done | bytes 98336 | tf_op jit(solution)/shard_map/ppermute | solution.py:146
  63.5 0.8 %shard_map.45 = f32[4,128,512]{2,1,0:T(8,128)} custom-call(f32[4,128,512]{2,1,0:T(8,128)} %shard_map.42.refs_0_, f32[3,4,16,128]{3,2,1,0:T(8,128)S(1)} %get-tuple-element.65.refs_1_, f32[3,4,16,128]{3,2,1,0:T(8,128)S(1)} %collective-permute-done.22.refs_2_, f32[3,4,16,128]{3,2,1,0:T(8,128)S(1)} %collective-permute-done.23.refs_3_, ...), custom_call_target="tpu_custom_call", output_to_operand_aliasing={{}: (0, {})} | custom-call | flops 262144 | bytes 2097152 | tf_op jit(solution)/shard_map/pallas_call | solution.py:175
  (40 shorter events, 2.4 us)
Async XLA Ops:
  0.0 11.4 %copy-start = (s32[16]{0:T(128)S(1)}, s32[16]{0:T(128)}, u32[]{:S(2)}) copy-start(s32[16]{0:T(128)} %param.4) | copy-start | bytes 196
  1.7 10.3 %collective-permute-start = (f32[2,4,16,128]{3,2,1,0:T(8,128)S(1)}, f32[2,4,16,128]{3,2,1,0:T(8,128)S(1)}, u32[]{:S(2)}, u32[]{:S(2)}) collective-permute-start(f32[2,4,16,128]{3,2,1,0:T(8,128)S(1)} %get-tuple-element.38), channel_id=1, source_target_pairs={{0,24},{8,16},{16,8},{24,0},{1,25},{9,17},{17,9},{25,1},{2,26},{10... | collective-permute-start | bytes 196616 | tf_op jit(solution)/shard_map/ppermute | solution.py:146
  6.9 17.8 %collective-permute-start.1 = (f32[2,4,16,128]{3,2,1,0:T(8,128)S(1)}, f32[2,4,16,128]{3,2,1,0:T(8,128)S(1)}, u32[]{:S(2)}, u32[]{:S(2)}) collective-permute-start(f32[2,4,16,128]{3,2,1,0:T(8,128)S(1)} %get-tuple-element.39), channel_id=1, source_target_pairs={{0,16},{8,24},{16,0},{24,8},{1,17},{9,25},{17,1},{25,9},{2,18},{10... | collective-permute-start | bytes 196616 | tf_op jit(solution)/shard_map/ppermute | solution.py:146
  6.9 18.4 %collective-permute-start.2 = (f32[2,4,16,128]{3,2,1,0:T(8,128)S(1)}, f32[2,4,16,128]{3,2,1,0:T(8,128)S(1)}, u32[]{:S(2)}, u32[]{:S(2)}) collective-permute-start(f32[2,4,16,128]{3,2,1,0:T(8,128)S(1)} %get-tuple-element.40), channel_id=1, source_target_pairs={{0,8},{8,0},{16,24},{24,16},{1,9},{9,1},{17,25},{25,17},{2,10},{10... | collective-permute-start | bytes 196616 | tf_op jit(solution)/shard_map/ppermute | solution.py:146
  7.5 8.5 %collective-permute-start.7 = (f32[3,4,16,128]{3,2,1,0:T(8,128)S(1)}, f32[3,4,16,128]{3,2,1,0:T(8,128)S(1)}, u32[]{:S(2)}, u32[]{:S(2)}) collective-permute-start(f32[3,4,16,128]{3,2,1,0:T(8,128)S(1)} %get-tuple-element.48), channel_id=1, source_target_pairs={{0,24},{8,16},{16,8},{24,0},{1,25},{9,17},{17,9},{25,1},{2,26},{10... | collective-permute-start | bytes 294920 | tf_op jit(solution)/shard_map/ppermute | solution.py:146
  11.3 9.6 %collective-permute-start.8 = (f32[3,4,16,128]{3,2,1,0:T(8,128)S(1)}, f32[3,4,16,128]{3,2,1,0:T(8,128)S(1)}, u32[]{:S(2)}, u32[]{:S(2)}) collective-permute-start(f32[3,4,16,128]{3,2,1,0:T(8,128)S(1)} %get-tuple-element.49), channel_id=1, source_target_pairs={{0,16},{8,24},{16,0},{24,8},{1,17},{9,25},{17,1},{25,9},{2,18},{10... | collective-permute-start | bytes 294920 | tf_op jit(solution)/shard_map/ppermute | solution.py:146
  12.0 9.9 %collective-permute-start.9 = (f32[3,4,16,128]{3,2,1,0:T(8,128)S(1)}, f32[3,4,16,128]{3,2,1,0:T(8,128)S(1)}, u32[]{:S(2)}, u32[]{:S(2)}) collective-permute-start(f32[3,4,16,128]{3,2,1,0:T(8,128)S(1)} %get-tuple-element.50), channel_id=1, source_target_pairs={{0,8},{8,0},{16,24},{24,16},{1,9},{9,1},{17,25},{25,17},{2,10},{10... | collective-permute-start | bytes 294920 | tf_op jit(solution)/shard_map/ppermute | solution.py:146
  16.0 10.7 %collective-permute-start.16 = (f32[4,4,16,128]{3,2,1,0:T(8,128)S(1)}, f32[4,4,16,128]{3,2,1,0:T(8,128)S(1)}, u32[]{:S(2)}, u32[]{:S(2)}) collective-permute-start(f32[4,4,16,128]{3,2,1,0:T(8,128)S(1)} %get-tuple-element.58), channel_id=1, source_target_pairs={{0,3},{1,2},{2,1},{3,0},{4,7},{5,6},{6,5},{7,4},{8,11},{9,10},{10,... | collective-permute-start | bytes 393224 | tf_op jit(solution)/shard_map/ppermute | solution.py:146
  20.9 8.5 %collective-permute-start.17 = (f32[4,4,16,128]{3,2,1,0:T(8,128)S(1)}, f32[4,4,16,128]{3,2,1,0:T(8,128)S(1)}, u32[]{:S(2)}, u32[]{:S(2)}) collective-permute-start(f32[4,4,16,128]{3,2,1,0:T(8,128)S(1)} %get-tuple-element.59), channel_id=1, source_target_pairs={{0,5},{1,4},{2,7},{3,6},{4,1},{5,0},{6,3},{7,2},{8,13},{9,12},{10,... | collective-permute-start | bytes 393224 | tf_op jit(solution)/shard_map/ppermute | solution.py:146
  21.9 7.8 %collective-permute-start.18 = (f32[4,4,16,128]{3,2,1,0:T(8,128)S(1)}, f32[4,4,16,128]{3,2,1,0:T(8,128)S(1)}, u32[]{:S(2)}, u32[]{:S(2)}) collective-permute-start(f32[4,4,16,128]{3,2,1,0:T(8,128)S(1)} %get-tuple-element.60), channel_id=1, source_target_pairs={{0,6},{1,7},{2,4},{3,5},{4,2},{5,3},{6,0},{7,1},{8,14},{9,15},{10,... | collective-permute-start | bytes 393224 | tf_op jit(solution)/shard_map/ppermute | solution.py:146
  24.6 7.9 %collective-permute-start.10 = (f32[4,4,16,128]{3,2,1,0:T(8,128)S(1)}, f32[4,4,16,128]{3,2,1,0:T(8,128)S(1)}, u32[]{:S(2)}, u32[]{:S(2)}) collective-permute-start(f32[4,4,16,128]{3,2,1,0:T(8,128)S(1)} %get-tuple-element.51), channel_id=1, source_target_pairs={{0,2},{1,3},{2,0},{3,1},{4,6},{5,7},{6,4},{7,5},{8,10},{9,11},{10,... | collective-permute-start | bytes 393224 | tf_op jit(solution)/shard_map/ppermute | solution.py:146
  25.2 9.9 %collective-permute-start.11 = (f32[4,4,16,128]{3,2,1,0:T(8,128)S(1)}, f32[4,4,16,128]{3,2,1,0:T(8,128)S(1)}, u32[]{:S(2)}, u32[]{:S(2)}) collective-permute-start(f32[4,4,16,128]{3,2,1,0:T(8,128)S(1)} %get-tuple-element.52), channel_id=1, source_target_pairs={{0,4},{1,5},{2,6},{3,7},{4,0},{5,1},{6,2},{7,3},{8,12},{9,13},{10,... | collective-permute-start | bytes 393224 | tf_op jit(solution)/shard_map/ppermute | solution.py:146
  26.7 8.5 %collective-permute-start.12 = (f32[4,4,16,128]{3,2,1,0:T(8,128)S(1)}, f32[4,4,16,128]{3,2,1,0:T(8,128)S(1)}, u32[]{:S(2)}, u32[]{:S(2)}) collective-permute-start(f32[4,4,16,128]{3,2,1,0:T(8,128)S(1)} %get-tuple-element.53), channel_id=1, source_target_pairs={{0,7},{1,6},{2,5},{3,4},{4,3},{5,2},{6,1},{7,0},{8,15},{9,14},{10,... | collective-permute-start | bytes 393224 | tf_op jit(solution)/shard_map/ppermute | solution.py:146
  29.4 8.5 %collective-permute-start.3 = (f32[4,4,16,128]{3,2,1,0:T(8,128)S(1)}, f32[4,4,16,128]{3,2,1,0:T(8,128)S(1)}, u32[]{:S(2)}, u32[]{:S(2)}) collective-permute-start(f32[4,4,16,128]{3,2,1,0:T(8,128)S(1)} %get-tuple-element.42), channel_id=1, source_target_pairs={{0,1},{1,0},{2,3},{3,2},{4,5},{5,4},{6,7},{7,6},{8,9},{9,8},{10,11... | collective-permute-start | bytes 393224 | tf_op jit(solution)/shard_map/ppermute | solution.py:146
  29.7 9.4 %collective-permute-start.19 = (f32[3,4,16,128]{3,2,1,0:T(8,128)S(1)}, f32[3,4,16,128]{3,2,1,0:T(8,128)S(1)}, u32[]{:S(2)}, u32[]{:S(2)}) collective-permute-start(f32[3,4,16,128]{3,2,1,0:T(8,128)S(1)} %get-tuple-element.62), channel_id=1, source_target_pairs={{0,24},{8,16},{16,8},{24,0},{1,25},{9,17},{17,9},{25,1},{2,26},{10... | collective-permute-start | bytes 294920 | tf_op jit(solution)/shard_map/ppermute | solution.py:146
  32.5 9.0 %collective-permute-start.20 = (f32[3,4,16,128]{3,2,1,0:T(8,128)S(1)}, f32[3,4,16,128]{3,2,1,0:T(8,128)S(1)}, u32[]{:S(2)}, u32[]{:S(2)}) collective-permute-start(f32[3,4,16,128]{3,2,1,0:T(8,128)S(1)} %get-tuple-element.63), channel_id=1, source_target_pairs={{0,16},{8,24},{16,0},{24,8},{1,17},{9,25},{17,1},{25,9},{2,18},{10... | collective-permute-start | bytes 294920 | tf_op jit(solution)/shard_map/ppermute | solution.py:146
  35.1 11.0 %collective-permute-start.21 = (f32[3,4,16,128]{3,2,1,0:T(8,128)S(1)}, f32[3,4,16,128]{3,2,1,0:T(8,128)S(1)}, u32[]{:S(2)}, u32[]{:S(2)}) collective-permute-start(f32[3,4,16,128]{3,2,1,0:T(8,128)S(1)} %get-tuple-element.64), channel_id=1, source_target_pairs={{0,8},{8,0},{16,24},{24,16},{1,9},{9,1},{17,25},{25,17},{2,10},{10... | collective-permute-start | bytes 294920 | tf_op jit(solution)/shard_map/ppermute | solution.py:146
  35.2 20.5 %collective-permute-start.13 = (f32[3,4,16,128]{3,2,1,0:T(8,128)S(1)}, f32[3,4,16,128]{3,2,1,0:T(8,128)S(1)}, u32[]{:S(2)}, u32[]{:S(2)}) collective-permute-start(f32[3,4,16,128]{3,2,1,0:T(8,128)S(1)} %get-tuple-element.55), channel_id=1, source_target_pairs={{0,24},{8,16},{16,8},{24,0},{1,25},{9,17},{17,9},{25,1},{2,26},{10... | collective-permute-start | bytes 294920 | tf_op jit(solution)/shard_map/ppermute | solution.py:146
  38.0 11.7 %collective-permute-start.4 = (f32[2,4,16,128]{3,2,1,0:T(8,128)S(1)}, f32[2,4,16,128]{3,2,1,0:T(8,128)S(1)}, u32[]{:S(2)}, u32[]{:S(2)}) collective-permute-start(f32[2,4,16,128]{3,2,1,0:T(8,128)S(1)} %get-tuple-element.44), channel_id=1, source_target_pairs={{0,24},{8,16},{16,8},{24,0},{1,25},{9,17},{17,9},{25,1},{2,26},{10... | collective-permute-start | bytes 196616 | tf_op jit(solution)/shard_map/ppermute | solution.py:146
  39.1 13.8 %collective-permute-start.5 = (f32[2,4,16,128]{3,2,1,0:T(8,128)S(1)}, f32[2,4,16,128]{3,2,1,0:T(8,128)S(1)}, u32[]{:S(2)}, u32[]{:S(2)}) collective-permute-start(f32[2,4,16,128]{3,2,1,0:T(8,128)S(1)} %get-tuple-element.45), channel_id=1, source_target_pairs={{0,16},{8,24},{16,0},{24,8},{1,17},{9,25},{17,1},{25,9},{2,18},{10... | collective-permute-start | bytes 196616 | tf_op jit(solution)/shard_map/ppermute | solution.py:146
  41.5 14.1 %collective-permute-start.6 = (f32[2,4,16,128]{3,2,1,0:T(8,128)S(1)}, f32[2,4,16,128]{3,2,1,0:T(8,128)S(1)}, u32[]{:S(2)}, u32[]{:S(2)}) collective-permute-start(f32[2,4,16,128]{3,2,1,0:T(8,128)S(1)} %get-tuple-element.46), channel_id=1, source_target_pairs={{0,8},{8,0},{16,24},{24,16},{1,9},{9,1},{17,25},{25,17},{2,10},{10... | collective-permute-start | bytes 196616 | tf_op jit(solution)/shard_map/ppermute | solution.py:146
  46.1 11.2 %collective-permute-start.14 = (f32[3,4,16,128]{3,2,1,0:T(8,128)S(1)}, f32[3,4,16,128]{3,2,1,0:T(8,128)S(1)}, u32[]{:S(2)}, u32[]{:S(2)}) collective-permute-start(f32[3,4,16,128]{3,2,1,0:T(8,128)S(1)} %get-tuple-element.56), channel_id=1, source_target_pairs={{0,16},{8,24},{16,0},{24,8},{1,17},{9,25},{17,1},{25,9},{2,18},{10... | collective-permute-start | bytes 294920 | tf_op jit(solution)/shard_map/ppermute | solution.py:146
  49.7 7.7 %collective-permute-start.15 = (f32[3,4,16,128]{3,2,1,0:T(8,128)S(1)}, f32[3,4,16,128]{3,2,1,0:T(8,128)S(1)}, u32[]{:S(2)}, u32[]{:S(2)}) collective-permute-start(f32[3,4,16,128]{3,2,1,0:T(8,128)S(1)} %get-tuple-element.57), channel_id=1, source_target_pairs={{0,8},{8,0},{16,24},{24,16},{1,9},{9,1},{17,25},{25,17},{2,10},{10... | collective-permute-start | bytes 294920 | tf_op jit(solution)/shard_map/ppermute | solution.py:146
  52.9 7.5 %collective-permute-start.22 = (f32[3,4,16,128]{3,2,1,0:T(8,128)S(1)}, f32[3,4,16,128]{3,2,1,0:T(8,128)S(1)}, u32[]{:S(2)}, u32[]{:S(2)}) collective-permute-start(f32[3,4,16,128]{3,2,1,0:T(8,128)S(1)} %get-tuple-element.66), channel_id=1, source_target_pairs={{0,24},{8,16},{16,8},{24,0},{1,25},{9,17},{17,9},{25,1},{2,26},{10... | collective-permute-start | bytes 294920 | tf_op jit(solution)/shard_map/ppermute | solution.py:146
  55.7 7.8 %collective-permute-start.23 = (f32[3,4,16,128]{3,2,1,0:T(8,128)S(1)}, f32[3,4,16,128]{3,2,1,0:T(8,128)S(1)}, u32[]{:S(2)}, u32[]{:S(2)}) collective-permute-start(f32[3,4,16,128]{3,2,1,0:T(8,128)S(1)} %get-tuple-element.67), channel_id=1, source_target_pairs={{0,16},{8,24},{16,0},{24,8},{1,17},{9,25},{17,1},{25,9},{2,18},{10... | collective-permute-start | bytes 294920 | tf_op jit(solution)/shard_map/ppermute | solution.py:146
  55.7 7.8 %collective-permute-start.24 = (f32[3,4,16,128]{3,2,1,0:T(8,128)S(1)}, f32[3,4,16,128]{3,2,1,0:T(8,128)S(1)}, u32[]{:S(2)}, u32[]{:S(2)}) collective-permute-start(f32[3,4,16,128]{3,2,1,0:T(8,128)S(1)} %get-tuple-element.68), channel_id=1, source_target_pairs={{0,8},{8,0},{16,24},{24,16},{1,9},{9,1},{17,25},{25,17},{2,10},{10... | collective-permute-start | bytes 294920 | tf_op jit(solution)/shard_map/ppermute | solution.py:146

commit v4 on v3

--- a/solution.py
+++ b/solution.py
@@ -41,8 +41,8 @@
     def __init__(self, mesh):
         self.shares, self.rows = mesh.shape["share"], mesh.shape["row"]
         self.share = [0, *range(self.shares - 1, 0, -1)]
-        others = range(2, self.rows)
-        self.near = [0, 1]
+        others = range(3, self.rows)
+        self.near = [0, 1, 2]
         self.middle = [hop for hop in others if hop.bit_count() % 2 == 1]
         self.far = [hop for hop in others if hop.bit_count() % 2 == 0]
 
@@ -56,8 +56,8 @@
         self.part = self.width // self.shares
 
     def tiled(self):
-        powers = all(n & (n - 1) == 0 for n in (self.shares, self.rows)) and self.rows > 2
-        whole = self.depth % 8 == 0 and self.width % (128 * self.shares) == 0
+        powers = all(n & (n - 1) == 0 for n in (self.shares, self.rows)) and self.rows > 4
+        whole = self.depth % 8 == 0 and self.width == 128 * self.shares
         return powers and whole and W % self.width == 0
 
 
@@ -102,16 +102,19 @@
 
 
 def mix(z, hops, by_row, weights, *refs):
-    ins, outs = refs[: z.shares], refs[z.shares :]
+    ins, outs, spread = refs[: z.shares], refs[z.shares : -1], refs[-1]
     share = lax.axis_index("share")
+    table = weights[...]
+    for i in range(K):
+        spread[i] = jnp.broadcast_to(table[:, i : i + 1], (K, 128))
     for m, target in enumerate(hops.share):
         totals = [None] * z.kept
         for n, source in enumerate(hops.share):
             for i in range(z.held):
                 values = ins[n][:, i]
                 for k in range(z.kept):
-                    weight = weights[(share ^ target) * z.kept + k, (share ^ source) * z.held + i]
-                    term = weight * values
+                    line = pl.ds((share ^ target) * z.kept + k, 1)
+                    term = spread[(share ^ source) * z.held + i, line] * values
                     totals[k] = term if totals[k] is None else totals[k] + term
         for k, total in enumerate(totals):
             if by_row:
@@ -200,13 +203,14 @@
 
     def mixed(arrays, rows, by_row):
         outs = slots(rows, shares, z.kept) if by_row else slots(shares, rows, z.kept)
-        specs = [SMEM] + [VMEM] * shares
+        specs = [VMEM] * (1 + shares)
         return call(
             lambda z, hops, *refs: mix(z, hops, by_row, *refs),
             outs,
             (weights, *arrays),
             specs,
             [VMEM] * len(outs),
+            [pltpu.VMEM((K, K, 128), jnp.float32)],
             flops=2 * K * rows * K * z.depth * z.part,
         )
 
@@ -239,12 +243,12 @@
     near = over_shares(parts[:shares])
     middle = over_shares(parts[shares : 2 * shares])
     far = over_rows(parts[2 * shares :], hops.far)
+    far = over_shares(regrouped(far, z.held))
     near = over_shares(mixed_and_crossed(near, hops.near))
-    far = over_shares(regrouped(far, z.held))
+    far = over_shares(mixed(far, len(hops.far), False))
     middle = over_shares(mixed_and_crossed(middle, hops.middle))
-    far = over_shares(mixed(far, len(hops.far), False))
-    out = placed(near + middle, [hops.near, hops.middle])
-    return placed(far, [hops.far], (out,))
+    out = placed(near + far, [hops.near, hops.far])
+    return placed(middle, [hops.middle], (out,))
 
 
 def solution(mesh):

time: 64.4 us -> 58.2 us (0.904)
  waiting for transfers between devices: 21.4 us -> 10.9 us
  starting transfers between devices: 34.9 us -> 41.1 us
  Pallas kernels: 7.12 us -> 5.06 us
    ppermute x25, waiting for transfers between devices: 21.4 us -> 10.9 us  [exchange(): out.append(lax.ppermute(array, axis, pairs) if hop else array)]
    ppermute x25, starting transfers between devices: 34.9 us -> 41.1 us  [exchange(): out.append(lax.ppermute(array, axis, pairs) if hop else array)]
    pallas_call x9, Pallas kernels: 7.12 us -> 5.06 us  [call(): pl.pallas_call(functools.partial(kernel, z, hops), out_shape=outs, in_spe...]
  transfers between devices with their start and end apart: 25 -> 25, of which waited for: 9 -> 7; matrix products, arithmetic and copies ran while one was open for 1% -> 1% of each run, Pallas kernels for 7% -> 4%
where the time goes in v4:
time: 58.2 us; the launch traced here: 58 us
  starting transfers between devices  41.1 us (71%)
  waiting for transfers between devices  10.9 us (19%)
  Pallas kernels  5.06 us (9%)
  other arithmetic  0.76 us (1%)
    ppermute x25, starting transfers between devices, exchange(): out.append(lax.ppermute(array, axis, pairs) if hop else array)  41.1 us
    ppermute x25, waiting for transfers between devices, exchange(): out.append(lax.ppermute(array, axis, pairs) if hop else array)  10.9 us
    pallas_call x9, Pallas kernels, call(): pl.pallas_call(functools.partial(kernel, z, hops), out_shape=outs, in_spe...  5.06 us
  transfers between devices with their start and end apart: 25, of which 7 were waited for; matrix products, arithmetic and copies ran while one was open for 1% of the time, Pallas kernels for 4%

profile of v4, /device:TPU:0, one launch (start us, length us, event | category | flops | bytes accessed | tf_op | source)
XLA Modules:
  0.0 58.0 jit_solution(4104928178250771380)
XLA Ops:
  0.0 1.7 %shard_map.37 = (f32[3,4,16,128]{3,2,1,0:T(8,128)S(1)}, f32[3,4,16,128]{3,2,1,0:T(8,128)S(1)}, f32[3,4,16,128]{3,2,1,0:T(8,128)S(1)}, f32[3,4,16,128]{3,2,1,0:T(...) custom-call(s32[2]{0:T(128)} %starts.1, ...), custom_call_target="tpu_custom_call" | custom-call | flops 262144 | bytes 2097152 | tf_op jit(solution)/shard_map/pallas_call | solution.py:178
  1.7 5.1 %collective-permute-start = (f32[3,4,16,128]{3,2,1,0:T(8,128)S(1)}, f32[3,4,16,128]{3,2,1,0:T(8,128)S(1)}, u32[]{:S(2)}, u32[]{:S(2)}) collective-permute-start(f32[3,4,16,128]{3,2,1,0:T(8,128)S(1)} %get-tuple-element.38), channel_id=1, source_target_pairs={{0,24},{8,16},{16,8},{24,0},{1,25},{9,17},{17,9},{25,1},{2,26},{10... | collective-permute-start | bytes 294920 | tf_op jit(solution)/shard_map/ppermute | solution.py:149
  6.9 0.6 %collective-permute-start.2 = (f32[3,4,16,128]{3,2,1,0:T(8,128)S(1)}, f32[3,4,16,128]{3,2,1,0:T(8,128)S(1)}, u32[]{:S(2)}, u32[]{:S(2)}) collective-permute-start(f32[3,4,16,128]{3,2,1,0:T(8,128)S(1)} %get-tuple-element.40), channel_id=1, source_target_pairs={{0,8},{8,0},{16,24},{24,16},{1,9},{9,1},{17,25},{25,17},{2,10},{10... | collective-permute-start | bytes 294920 | tf_op jit(solution)/shard_map/ppermute | solution.py:149
  7.5 0.4 collective-permute-start.8
  7.9 2.5 %collective-permute-start.9 = (f32[4,4,16,128]{3,2,1,0:T(8,128)S(1)}, f32[4,4,16,128]{3,2,1,0:T(8,128)S(1)}, u32[]{:S(2)}, u32[]{:S(2)}) collective-permute-start(f32[4,4,16,128]{3,2,1,0:T(8,128)S(1)} %get-tuple-element.49), channel_id=1, source_target_pairs={{0,5},{1,4},{2,7},{3,6},{4,1},{5,0},{6,3},{7,2},{8,13},{9,12},{10,... | collective-permute-start | bytes 393224 | tf_op jit(solution)/shard_map/ppermute | solution.py:149
  10.6 0.2 select_reduce_fusion
  11.1 1.9 %collective-permute-start.10 = (f32[4,4,16,128]{3,2,1,0:T(8,128)S(1)}, f32[4,4,16,128]{3,2,1,0:T(8,128)S(1)}, u32[]{:S(2)}, u32[]{:S(2)}) collective-permute-start(f32[4,4,16,128]{3,2,1,0:T(8,128)S(1)} %get-tuple-element.50), channel_id=1, source_target_pairs={{0,6},{1,7},{2,4},{3,5},{4,2},{5,3},{6,0},{7,1},{8,14},{9,15},{10,... | collective-permute-start | bytes 393224 | tf_op jit(solution)/shard_map/ppermute | solution.py:149
  13.1 2.0 %collective-permute-done.1.refs_3_ = f32[3,4,16,128]{3,2,1,0:T(8,128)S(1)} collective-permute-done((f32[3,4,16,128]{3,2,1,0:T(8,128)S(1)}, f32[3,4,16,128]{3,2,1,0:T(8,128)S(1)}, u32[]{:S(2)}, u32[]{:S(2)}) %collective-permute-start.1) | collective-permute-done | bytes 98336 | tf_op jit(solution)/shard_map/ppermute | solution.py:149
  15.1 0.5 shard_map.38
  15.7 2.6 %collective-permute-start.17 = (f32[2,4,16,128]{3,2,1,0:T(8,128)S(1)}, f32[2,4,16,128]{3,2,1,0:T(8,128)S(1)}, u32[]{:S(2)}, u32[]{:S(2)}) collective-permute-start(f32[2,4,16,128]{3,2,1,0:T(8,128)S(1)} %get-tuple-element.60), channel_id=1, source_target_pairs={{0,24},{8,16},{16,8},{24,0},{1,25},{9,17},{17,9},{25,1},{2,26},{10... | collective-permute-start | bytes 196616 | tf_op jit(solution)/shard_map/ppermute | solution.py:149
  18.3 0.9 %collective-permute-start.18 = (f32[2,4,16,128]{3,2,1,0:T(8,128)S(1)}, f32[2,4,16,128]{3,2,1,0:T(8,128)S(1)}, u32[]{:S(2)}, u32[]{:S(2)}) collective-permute-start(f32[2,4,16,128]{3,2,1,0:T(8,128)S(1)} %get-tuple-element.61), channel_id=1, source_target_pairs={{0,16},{8,24},{16,0},{24,8},{1,17},{9,25},{17,1},{25,9},{2,18},{10... | collective-permute-start | bytes 196616 | tf_op jit(solution)/shard_map/ppermute | solution.py:149
  19.2 0.7 %collective-permute-start.4 = (f32[4,4,16,128]{3,2,1,0:T(8,128)S(1)}, f32[4,4,16,128]{3,2,1,0:T(8,128)S(1)}, u32[]{:S(2)}, u32[]{:S(2)}) collective-permute-start(f32[4,4,16,128]{3,2,1,0:T(8,128)S(1)} %get-tuple-element.43), channel_id=1, source_target_pairs={{0,2},{1,3},{2,0},{3,1},{4,6},{5,7},{6,4},{7,5},{8,10},{9,11},{10,... | collective-permute-start | bytes 393224 | tf_op jit(solution)/shard_map/ppermute | solution.py:149
  19.9 1.8 %collective-permute-start.19 = (f32[2,4,16,128]{3,2,1,0:T(8,128)S(1)}, f32[2,4,16,128]{3,2,1,0:T(8,128)S(1)}, u32[]{:S(2)}, u32[]{:S(2)}) collective-permute-start(f32[2,4,16,128]{3,2,1,0:T(8,128)S(1)} %get-tuple-element.62), channel_id=1, source_target_pairs={{0,8},{8,0},{16,24},{24,16},{1,9},{9,1},{17,25},{25,17},{2,10},{10... | collective-permute-start | bytes 196616 | tf_op jit(solution)/shard_map/ppermute | solution.py:149
  21.7 0.4 collective-permute-done.17.refs_2_
  22.1 3.1 %collective-permute-start.11 = (f32[3,4,16,128]{3,2,1,0:T(8,128)S(1)}, f32[3,4,16,128]{3,2,1,0:T(8,128)S(1)}, u32[]{:S(2)}, u32[]{:S(2)}) collective-permute-start(f32[3,4,16,128]{3,2,1,0:T(8,128)S(1)} %get-tuple-element.52), channel_id=1, source_target_pairs={{0,24},{8,16},{16,8},{24,0},{1,25},{9,17},{17,9},{25,1},{2,26},{10... | collective-permute-start | bytes 294920 | tf_op jit(solution)/shard_map/ppermute | solution.py:149
  25.2 0.6 %collective-permute-done.18.refs_3_ = f32[2,4,16,128]{3,2,1,0:T(8,128)S(1)} collective-permute-done((f32[2,4,16,128]{3,2,1,0:T(8,128)S(1)}, f32[2,4,16,128]{3,2,1,0:T(8,128)S(1)}, u32[]{:S(2)}, u32[]{:S(2)}) %collective-permute-start.18) | collective-permute-done | bytes 65568 | tf_op jit(solution)/shard_map/ppermute | solution.py:149
  25.8 0.4 shard_map.43
  26.2 1.2 %collective-permute-start.20 = (f32[4,4,16,128]{3,2,1,0:T(8,128)S(1)}, f32[4,4,16,128]{3,2,1,0:T(8,128)S(1)}, u32[]{:S(2)}, u32[]{:S(2)}) collective-permute-start(f32[4,4,16,128]{3,2,1,0:T(8,128)S(1)} %get-tuple-element.63), channel_id=1, source_target_pairs={{0,4},{1,5},{2,6},{3,7},{4,0},{5,1},{6,2},{7,3},{8,12},{9,13},{10,... | collective-permute-start | bytes 393224 | tf_op jit(solution)/shard_map/ppermute | solution.py:149
  27.5 2.0 %collective-permute-start.12 = (f32[3,4,16,128]{3,2,1,0:T(8,128)S(1)}, f32[3,4,16,128]{3,2,1,0:T(8,128)S(1)}, u32[]{:S(2)}, u32[]{:S(2)}) collective-permute-start(f32[3,4,16,128]{3,2,1,0:T(8,128)S(1)} %get-tuple-element.53), channel_id=1, source_target_pairs={{0,16},{8,24},{16,0},{24,8},{1,17},{9,25},{17,1},{25,9},{2,18},{10... | collective-permute-start | bytes 294920 | tf_op jit(solution)/shard_map/ppermute | solution.py:149
  29.5 0.9 %collective-permute-start.13 = (f32[3,4,16,128]{3,2,1,0:T(8,128)S(1)}, f32[3,4,16,128]{3,2,1,0:T(8,128)S(1)}, u32[]{:S(2)}, u32[]{:S(2)}) collective-permute-start(f32[3,4,16,128]{3,2,1,0:T(8,128)S(1)} %get-tuple-element.54), channel_id=1, source_target_pairs={{0,8},{8,0},{16,24},{24,16},{1,9},{9,1},{17,25},{25,17},{2,10},{10... | collective-permute-start | bytes 294920 | tf_op jit(solution)/shard_map/ppermute | solution.py:149
  30.4 1.5 %collective-permute-start.5 = (f32[3,4,16,128]{3,2,1,0:T(8,128)S(1)}, f32[3,4,16,128]{3,2,1,0:T(8,128)S(1)}, u32[]{:S(2)}, u32[]{:S(2)}) collective-permute-start(f32[3,4,16,128]{3,2,1,0:T(8,128)S(1)} %get-tuple-element.45), channel_id=1, source_target_pairs={{0,24},{8,16},{16,8},{24,0},{1,25},{9,17},{17,9},{25,1},{2,26},{10... | collective-permute-start | bytes 294920 | tf_op jit(solution)/shard_map/ppermute | solution.py:149
  32.0 3.1 %collective-permute-done.12.refs_3_ = f32[3,4,16,128]{3,2,1,0:T(8,128)S(1)} collective-permute-done((f32[3,4,16,128]{3,2,1,0:T(8,128)S(1)}, f32[3,4,16,128]{3,2,1,0:T(8,128)S(1)}, u32[]{:S(2)}, u32[]{:S(2)}) %collective-permute-start.12) | collective-permute-done | bytes 98336 | tf_op jit(solution)/shard_map/ppermute | solution.py:149
  35.3 6.4 %collective-permute-start.7 = (f32[3,4,16,128]{3,2,1,0:T(8,128)S(1)}, f32[3,4,16,128]{3,2,1,0:T(8,128)S(1)}, u32[]{:S(2)}, u32[]{:S(2)}) collective-permute-start(f32[3,4,16,128]{3,2,1,0:T(8,128)S(1)} %get-tuple-element.47), channel_id=1, source_target_pairs={{0,8},{8,0},{16,24},{24,16},{1,9},{9,1},{17,25},{25,17},{2,10},{10... | collective-permute-start | bytes 294920 | tf_op jit(solution)/shard_map/ppermute | solution.py:149
  41.8 0.5 shard_map.41
  42.4 1.4 %collective-permute-start.15 = (f32[3,4,16,128]{3,2,1,0:T(8,128)S(1)}, f32[3,4,16,128]{3,2,1,0:T(8,128)S(1)}, u32[]{:S(2)}, u32[]{:S(2)}) collective-permute-start(f32[3,4,16,128]{3,2,1,0:T(8,128)S(1)} %get-tuple-element.57), channel_id=1, source_target_pairs={{0,16},{8,24},{16,0},{24,8},{1,17},{9,25},{17,1},{25,9},{2,18},{10... | collective-permute-start | bytes 294920 | tf_op jit(solution)/shard_map/ppermute | solution.py:149
  43.8 2.9 %collective-permute-start.16 = (f32[3,4,16,128]{3,2,1,0:T(8,128)S(1)}, f32[3,4,16,128]{3,2,1,0:T(8,128)S(1)}, u32[]{:S(2)}, u32[]{:S(2)}) collective-permute-start(f32[3,4,16,128]{3,2,1,0:T(8,128)S(1)} %get-tuple-element.58), channel_id=1, source_target_pairs={{0,8},{8,0},{16,24},{24,16},{1,9},{9,1},{17,25},{25,17},{2,10},{10... | collective-permute-start | bytes 294920 | tf_op jit(solution)/shard_map/ppermute | solution.py:149
  46.8 3.6 %collective-permute-start.22 = (f32[2,4,16,128]{3,2,1,0:T(8,128)S(1)}, f32[2,4,16,128]{3,2,1,0:T(8,128)S(1)}, u32[]{:S(2)}, u32[]{:S(2)}) collective-permute-start(f32[2,4,16,128]{3,2,1,0:T(8,128)S(1)} %get-tuple-element.66), channel_id=1, source_target_pairs={{0,24},{8,16},{16,8},{24,0},{1,25},{9,17},{17,9},{25,1},{2,26},{10... | collective-permute-start | bytes 196616 | tf_op jit(solution)/shard_map/ppermute | solution.py:149
  50.4 1.2 %collective-permute-start.24 = (f32[2,4,16,128]{3,2,1,0:T(8,128)S(1)}, f32[2,4,16,128]{3,2,1,0:T(8,128)S(1)}, u32[]{:S(2)}, u32[]{:S(2)}) collective-permute-start(f32[2,4,16,128]{3,2,1,0:T(8,128)S(1)} %get-tuple-element.68), channel_id=1, source_target_pairs={{0,8},{8,0},{16,24},{24,16},{1,9},{9,1},{17,25},{25,17},{2,10},{10... | collective-permute-start | bytes 196616 | tf_op jit(solution)/shard_map/ppermute | solution.py:149
  51.6 3.5 %collective-permute-done.15.refs_6_ = f32[3,4,16,128]{3,2,1,0:T(8,128)S(1)} collective-permute-done((f32[3,4,16,128]{3,2,1,0:T(8,128)S(1)}, f32[3,4,16,128]{3,2,1,0:T(8,128)S(1)}, u32[]{:S(2)}, u32[]{:S(2)}) %collective-permute-start.15) | collective-permute-done | bytes 98336 | tf_op jit(solution)/shard_map/ppermute | solution.py:149
  55.0 1.1 %shard_map.42.refs_0_ = f32[4,128,512]{2,1,0:T(8,128)} custom-call(f32[3,4,16,128]{3,2,1,0:T(8,128)S(1)} %get-tuple-element.44.refs_0_, f32[3,4,16,128]{3,2,1,0:T(8,128)S(1)} %collective-permute-done.5.refs_1_, f32[3,4,16,128]{3,2,1,0:T(8,128)S(1)} %collective-permute-done.6.refs_2_, f32[3,4,16,128]{3,2,1,0:T(8,128)S(1)} %collective-permute-done.7.refs_3_, ...), custom_call_target="tpu_custom_call" | custom-call | flops 262144 | bytes 2097152 | tf_op jit(solution)/shard_map/pallas_call | solution.py:178
  56.1 1.1 %collective-permute-done.23.refs_3_ = f32[2,4,16,128]{3,2,1,0:T(8,128)S(1)} collective-permute-done((f32[2,4,16,128]{3,2,1,0:T(8,128)S(1)}, f32[2,4,16,128]{3,2,1,0:T(8,128)S(1)}, u32[]{:S(2)}, u32[]{:S(2)}) %collective-permute-start.23) | collective-permute-done | bytes 65568 | tf_op jit(solution)/shard_map/ppermute | solution.py:149
  57.3 0.8 %shard_map.45 = f32[4,128,512]{2,1,0:T(8,128)} custom-call(f32[4,128,512]{2,1,0:T(8,128)} %shard_map.42.refs_0_, f32[2,4,16,128]{3,2,1,0:T(8,128)S(1)} %get-tuple-element.65.refs_1_, f32[2,4,16,128]{3,2,1,0:T(8,128)S(1)} %collective-permute-done.22.refs_2_, f32[2,4,16,128]{3,2,1,0:T(8,128)S(1)} %collective-permute-done.23.refs_3_, ...), custom_call_target="tpu_custom_call", output_to_operand_aliasing={{}: (0, {})} | custom-call | flops 262144 | bytes 2097152 | tf_op jit(solution)/shard_map/pallas_call | solution.py:178
  (40 shorter events, 1.1 us)
Async XLA Ops:
  0.0 10.6 %copy-start = (s32[16]{0:T(128)S(1)}, s32[16]{0:T(128)}, u32[]{:S(2)}) copy-start(s32[16]{0:T(128)} %param.4) | copy-start | bytes 196
  1.7 9.4 %collective-permute-start = (f32[3,4,16,128]{3,2,1,0:T(8,128)S(1)}, f32[3,4,16,128]{3,2,1,0:T(8,128)S(1)}, u32[]{:S(2)}, u32[]{:S(2)}) collective-permute-start(f32[3,4,16,128]{3,2,1,0:T(8,128)S(1)} %get-tuple-element.38), channel_id=1, source_target_pairs={{0,24},{8,16},{16,8},{24,0},{1,25},{9,17},{17,9},{25,1},{2,26},{10... | collective-permute-start | bytes 294920 | tf_op jit(solution)/shard_map/ppermute | solution.py:149
  6.9 8.3 %collective-permute-start.1 = (f32[3,4,16,128]{3,2,1,0:T(8,128)S(1)}, f32[3,4,16,128]{3,2,1,0:T(8,128)S(1)}, u32[]{:S(2)}, u32[]{:S(2)}) collective-permute-start(f32[3,4,16,128]{3,2,1,0:T(8,128)S(1)} %get-tuple-element.39), channel_id=1, source_target_pairs={{0,16},{8,24},{16,0},{24,8},{1,17},{9,25},{17,1},{25,9},{2,18},{10... | collective-permute-start | bytes 294920 | tf_op jit(solution)/shard_map/ppermute | solution.py:149
  6.9 8.3 %collective-permute-start.2 = (f32[3,4,16,128]{3,2,1,0:T(8,128)S(1)}, f32[3,4,16,128]{3,2,1,0:T(8,128)S(1)}, u32[]{:S(2)}, u32[]{:S(2)}) collective-permute-start(f32[3,4,16,128]{3,2,1,0:T(8,128)S(1)} %get-tuple-element.40), channel_id=1, source_target_pairs={{0,8},{8,0},{16,24},{24,16},{1,9},{9,1},{17,25},{25,17},{2,10},{10... | collective-permute-start | bytes 294920 | tf_op jit(solution)/shard_map/ppermute | solution.py:149
  7.5 10.8 %collective-permute-start.8 = (f32[4,4,16,128]{3,2,1,0:T(8,128)S(1)}, f32[4,4,16,128]{3,2,1,0:T(8,128)S(1)}, u32[]{:S(2)}, u32[]{:S(2)}) collective-permute-start(f32[4,4,16,128]{3,2,1,0:T(8,128)S(1)} %get-tuple-element.48), channel_id=1, source_target_pairs={{0,3},{1,2},{2,1},{3,0},{4,7},{5,6},{6,5},{7,4},{8,11},{9,10},{10,... | collective-permute-start | bytes 393224 | tf_op jit(solution)/shard_map/ppermute | solution.py:149
  7.9 11.3 %collective-permute-start.9 = (f32[4,4,16,128]{3,2,1,0:T(8,128)S(1)}, f32[4,4,16,128]{3,2,1,0:T(8,128)S(1)}, u32[]{:S(2)}, u32[]{:S(2)}) collective-permute-start(f32[4,4,16,128]{3,2,1,0:T(8,128)S(1)} %get-tuple-element.49), channel_id=1, source_target_pairs={{0,5},{1,4},{2,7},{3,6},{4,1},{5,0},{6,3},{7,2},{8,13},{9,12},{10,... | collective-permute-start | bytes 393224 | tf_op jit(solution)/shard_map/ppermute | solution.py:149
  11.1 8.8 %collective-permute-start.10 = (f32[4,4,16,128]{3,2,1,0:T(8,128)S(1)}, f32[4,4,16,128]{3,2,1,0:T(8,128)S(1)}, u32[]{:S(2)}, u32[]{:S(2)}) collective-permute-start(f32[4,4,16,128]{3,2,1,0:T(8,128)S(1)} %get-tuple-element.50), channel_id=1, source_target_pairs={{0,6},{1,7},{2,4},{3,5},{4,2},{5,3},{6,0},{7,1},{8,14},{9,15},{10,... | collective-permute-start | bytes 393224 | tf_op jit(solution)/shard_map/ppermute | solution.py:149
  15.7 13.8 %collective-permute-start.3 = (f32[4,4,16,128]{3,2,1,0:T(8,128)S(1)}, f32[4,4,16,128]{3,2,1,0:T(8,128)S(1)}, u32[]{:S(2)}, u32[]{:S(2)}) collective-permute-start(f32[4,4,16,128]{3,2,1,0:T(8,128)S(1)} %get-tuple-element.42), channel_id=1, source_target_pairs={{0,1},{1,0},{2,3},{3,2},{4,5},{5,4},{6,7},{7,6},{8,9},{9,8},{10,11... | collective-permute-start | bytes 393224 | tf_op jit(solution)/shard_map/ppermute | solution.py:149
  15.7 6.4 %collective-permute-start.17 = (f32[2,4,16,128]{3,2,1,0:T(8,128)S(1)}, f32[2,4,16,128]{3,2,1,0:T(8,128)S(1)}, u32[]{:S(2)}, u32[]{:S(2)}) collective-permute-start(f32[2,4,16,128]{3,2,1,0:T(8,128)S(1)} %get-tuple-element.60), channel_id=1, source_target_pairs={{0,24},{8,16},{16,8},{24,0},{1,25},{9,17},{17,9},{25,1},{2,26},{10... | collective-permute-start | bytes 196616 | tf_op jit(solution)/shard_map/ppermute | solution.py:149
  18.3 7.5 %collective-permute-start.18 = (f32[2,4,16,128]{3,2,1,0:T(8,128)S(1)}, f32[2,4,16,128]{3,2,1,0:T(8,128)S(1)}, u32[]{:S(2)}, u32[]{:S(2)}) collective-permute-start(f32[2,4,16,128]{3,2,1,0:T(8,128)S(1)} %get-tuple-element.61), channel_id=1, source_target_pairs={{0,16},{8,24},{16,0},{24,8},{1,17},{9,25},{17,1},{25,9},{2,18},{10... | collective-permute-start | bytes 196616 | tf_op jit(solution)/shard_map/ppermute | solution.py:149
  19.2 11.2 %collective-permute-start.4 = (f32[4,4,16,128]{3,2,1,0:T(8,128)S(1)}, f32[4,4,16,128]{3,2,1,0:T(8,128)S(1)}, u32[]{:S(2)}, u32[]{:S(2)}) collective-permute-start(f32[4,4,16,128]{3,2,1,0:T(8,128)S(1)} %get-tuple-element.43), channel_id=1, source_target_pairs={{0,2},{1,3},{2,0},{3,1},{4,6},{5,7},{6,4},{7,5},{8,10},{9,11},{10,... | collective-permute-start | bytes 393224 | tf_op jit(solution)/shard_map/ppermute | solution.py:149
  19.9 5.9 %collective-permute-start.19 = (f32[2,4,16,128]{3,2,1,0:T(8,128)S(1)}, f32[2,4,16,128]{3,2,1,0:T(8,128)S(1)}, u32[]{:S(2)}, u32[]{:S(2)}) collective-permute-start(f32[2,4,16,128]{3,2,1,0:T(8,128)S(1)} %get-tuple-element.62), channel_id=1, source_target_pairs={{0,8},{8,0},{16,24},{24,16},{1,9},{9,1},{17,25},{25,17},{2,10},{10... | collective-permute-start | bytes 196616 | tf_op jit(solution)/shard_map/ppermute | solution.py:149
  22.1 8.3 %collective-permute-start.11 = (f32[3,4,16,128]{3,2,1,0:T(8,128)S(1)}, f32[3,4,16,128]{3,2,1,0:T(8,128)S(1)}, u32[]{:S(2)}, u32[]{:S(2)}) collective-permute-start(f32[3,4,16,128]{3,2,1,0:T(8,128)S(1)} %get-tuple-element.52), channel_id=1, source_target_pairs={{0,24},{8,16},{16,8},{24,0},{1,25},{9,17},{17,9},{25,1},{2,26},{10... | collective-permute-start | bytes 294920 | tf_op jit(solution)/shard_map/ppermute | solution.py:149
  26.2 16.1 %collective-permute-start.20 = (f32[4,4,16,128]{3,2,1,0:T(8,128)S(1)}, f32[4,4,16,128]{3,2,1,0:T(8,128)S(1)}, u32[]{:S(2)}, u32[]{:S(2)}) collective-permute-start(f32[4,4,16,128]{3,2,1,0:T(8,128)S(1)} %get-tuple-element.63), channel_id=1, source_target_pairs={{0,4},{1,5},{2,6},{3,7},{4,0},{5,1},{6,2},{7,3},{8,12},{9,13},{10,... | collective-permute-start | bytes 393224 | tf_op jit(solution)/shard_map/ppermute | solution.py:149
  27.5 7.6 %collective-permute-start.12 = (f32[3,4,16,128]{3,2,1,0:T(8,128)S(1)}, f32[3,4,16,128]{3,2,1,0:T(8,128)S(1)}, u32[]{:S(2)}, u32[]{:S(2)}) collective-permute-start(f32[3,4,16,128]{3,2,1,0:T(8,128)S(1)} %get-tuple-element.53), channel_id=1, source_target_pairs={{0,16},{8,24},{16,0},{24,8},{1,17},{9,25},{17,1},{25,9},{2,18},{10... | collective-permute-start | bytes 294920 | tf_op jit(solution)/shard_map/ppermute | solution.py:149
  29.5 5.9 %collective-permute-start.13 = (f32[3,4,16,128]{3,2,1,0:T(8,128)S(1)}, f32[3,4,16,128]{3,2,1,0:T(8,128)S(1)}, u32[]{:S(2)}, u32[]{:S(2)}) collective-permute-start(f32[3,4,16,128]{3,2,1,0:T(8,128)S(1)} %get-tuple-element.54), channel_id=1, source_target_pairs={{0,8},{8,0},{16,24},{24,16},{1,9},{9,1},{17,25},{25,17},{2,10},{10... | collective-permute-start | bytes 294920 | tf_op jit(solution)/shard_map/ppermute | solution.py:149
  30.4 12.0 %collective-permute-start.21 = (f32[4,4,16,128]{3,2,1,0:T(8,128)S(1)}, f32[4,4,16,128]{3,2,1,0:T(8,128)S(1)}, u32[]{:S(2)}, u32[]{:S(2)}) collective-permute-start(f32[4,4,16,128]{3,2,1,0:T(8,128)S(1)} %get-tuple-element.64), channel_id=1, source_target_pairs={{0,7},{1,6},{2,5},{3,4},{4,3},{5,2},{6,1},{7,0},{8,15},{9,14},{10,... | collective-permute-start | bytes 393224 | tf_op jit(solution)/shard_map/ppermute | solution.py:149
  30.4 13.4 %collective-permute-start.5 = (f32[3,4,16,128]{3,2,1,0:T(8,128)S(1)}, f32[3,4,16,128]{3,2,1,0:T(8,128)S(1)}, u32[]{:S(2)}, u32[]{:S(2)}) collective-permute-start(f32[3,4,16,128]{3,2,1,0:T(8,128)S(1)} %get-tuple-element.45), channel_id=1, source_target_pairs={{0,24},{8,16},{16,8},{24,0},{1,25},{9,17},{17,9},{25,1},{2,26},{10... | collective-permute-start | bytes 294920 | tf_op jit(solution)/shard_map/ppermute | solution.py:149
  35.1 11.7 %collective-permute-start.6 = (f32[3,4,16,128]{3,2,1,0:T(8,128)S(1)}, f32[3,4,16,128]{3,2,1,0:T(8,128)S(1)}, u32[]{:S(2)}, u32[]{:S(2)}) collective-permute-start(f32[3,4,16,128]{3,2,1,0:T(8,128)S(1)} %get-tuple-element.46), channel_id=1, source_target_pairs={{0,16},{8,24},{16,0},{24,8},{1,17},{9,25},{17,1},{25,9},{2,18},{10... | collective-permute-start | bytes 294920 | tf_op jit(solution)/shard_map/ppermute | solution.py:149
  35.3 15.1 %collective-permute-start.7 = (f32[3,4,16,128]{3,2,1,0:T(8,128)S(1)}, f32[3,4,16,128]{3,2,1,0:T(8,128)S(1)}, u32[]{:S(2)}, u32[]{:S(2)}) collective-permute-start(f32[3,4,16,128]{3,2,1,0:T(8,128)S(1)} %get-tuple-element.47), channel_id=1, source_target_pairs={{0,8},{8,0},{16,24},{24,16},{1,9},{9,1},{17,25},{25,17},{2,10},{10... | collective-permute-start | bytes 294920 | tf_op jit(solution)/shard_map/ppermute | solution.py:149
  42.3 8.1 %collective-permute-start.14 = (f32[3,4,16,128]{3,2,1,0:T(8,128)S(1)}, f32[3,4,16,128]{3,2,1,0:T(8,128)S(1)}, u32[]{:S(2)}, u32[]{:S(2)}) collective-permute-start(f32[3,4,16,128]{3,2,1,0:T(8,128)S(1)} %get-tuple-element.56), channel_id=1, source_target_pairs={{0,24},{8,16},{16,8},{24,0},{1,25},{9,17},{17,9},{25,1},{2,26},{10... | collective-permute-start | bytes 294920 | tf_op jit(solution)/shard_map/ppermute | solution.py:149
  42.4 12.7 %collective-permute-start.15 = (f32[3,4,16,128]{3,2,1,0:T(8,128)S(1)}, f32[3,4,16,128]{3,2,1,0:T(8,128)S(1)}, u32[]{:S(2)}, u32[]{:S(2)}) collective-permute-start(f32[3,4,16,128]{3,2,1,0:T(8,128)S(1)} %get-tuple-element.57), channel_id=1, source_target_pairs={{0,16},{8,24},{16,0},{24,8},{1,17},{9,25},{17,1},{25,9},{2,18},{10... | collective-permute-start | bytes 294920 | tf_op jit(solution)/shard_map/ppermute | solution.py:149
  43.8 11.2 %collective-permute-start.16 = (f32[3,4,16,128]{3,2,1,0:T(8,128)S(1)}, f32[3,4,16,128]{3,2,1,0:T(8,128)S(1)}, u32[]{:S(2)}, u32[]{:S(2)}) collective-permute-start(f32[3,4,16,128]{3,2,1,0:T(8,128)S(1)} %get-tuple-element.58), channel_id=1, source_target_pairs={{0,8},{8,0},{16,24},{24,16},{1,9},{9,1},{17,25},{25,17},{2,10},{10... | collective-permute-start | bytes 294920 | tf_op jit(solution)/shard_map/ppermute | solution.py:149
  46.8 9.3 %collective-permute-start.22 = (f32[2,4,16,128]{3,2,1,0:T(8,128)S(1)}, f32[2,4,16,128]{3,2,1,0:T(8,128)S(1)}, u32[]{:S(2)}, u32[]{:S(2)}) collective-permute-start(f32[2,4,16,128]{3,2,1,0:T(8,128)S(1)} %get-tuple-element.66), channel_id=1, source_target_pairs={{0,24},{8,16},{16,8},{24,0},{1,25},{9,17},{17,9},{25,1},{2,26},{10... | collective-permute-start | bytes 196616 | tf_op jit(solution)/shard_map/ppermute | solution.py:149
  50.4 6.9 %collective-permute-start.23 = (f32[2,4,16,128]{3,2,1,0:T(8,128)S(1)}, f32[2,4,16,128]{3,2,1,0:T(8,128)S(1)}, u32[]{:S(2)}, u32[]{:S(2)}) collective-permute-start(f32[2,4,16,128]{3,2,1,0:T(8,128)S(1)} %get-tuple-element.67), channel_id=1, source_target_pairs={{0,16},{8,24},{16,0},{24,8},{1,17},{9,25},{17,1},{25,9},{2,18},{10... | collective-permute-start | bytes 196616 | tf_op jit(solution)/shard_map/ppermute | solution.py:149
  50.4 6.9 %collective-permute-start.24 = (f32[2,4,16,128]{3,2,1,0:T(8,128)S(1)}, f32[2,4,16,128]{3,2,1,0:T(8,128)S(1)}, u32[]{:S(2)}, u32[]{:S(2)}) collective-permute-start(f32[2,4,16,128]{3,2,1,0:T(8,128)S(1)} %get-tuple-element.68), channel_id=1, source_target_pairs={{0,8},{8,0},{16,24},{24,16},{1,9},{9,1},{17,25},{25,17},{2,10},{10... | collective-permute-start | bytes 196616 | tf_op jit(solution)/shard_map/ppermute | solution.py:149

commit v5 on v4

--- a/solution.py
+++ b/solution.py
@@ -41,10 +41,10 @@
     def __init__(self, mesh):
         self.shares, self.rows = mesh.shape["share"], mesh.shape["row"]
         self.share = [0, *range(self.shares - 1, 0, -1)]
-        others = range(3, self.rows)
-        self.near = [0, 1, 2]
-        self.middle = [hop for hop in others if hop.bit_count() % 2 == 1]
-        self.far = [hop for hop in others if hop.bit_count() % 2 == 0]
+        others = range(2, self.rows)
+        self.near = [0, 1]
+        self.middle = [hop for hop in others if hop % 2 == 1]
+        self.far = [hop for hop in others if hop % 2 == 0]
 
 
 class Sizes:
@@ -56,7 +56,7 @@
         self.part = self.width // self.shares
 
     def tiled(self):
-        powers = all(n & (n - 1) == 0 for n in (self.shares, self.rows)) and self.rows > 4
+        powers = all(n & (n - 1) == 0 for n in (self.shares, self.rows)) and self.rows > 2
         whole = self.depth % 8 == 0 and self.width == 128 * self.shares
         return powers and whole and W % self.width == 0
 

time: 58.2 us -> 63.4 us (1.089)
  waiting for transfers between devices: 10.9 us -> 22.8 us
  starting transfers between devices: 41.1 us -> 34.5 us
    ppermute x25, waiting for transfers between devices: 10.9 us -> 22.8 us  [exchange(): out.append(lax.ppermute(array, axis, pairs) if hop else array)]
    ppermute x25, starting transfers between devices: 41.1 us -> 34.5 us  [exchange(): out.append(lax.ppermute(array, axis, pairs) if hop else array)]
  transfers between devices with their start and end apart: 25 -> 25, of which waited for: 7 -> 11; matrix products, arithmetic and copies ran while one was open for 1% -> 1% of each run, Pallas kernels for 4% -> 4%
where the time goes in v5:
time: 63.4 us; the launch traced here: 63.2 us
  starting transfers between devices  34.5 us (54%)
  waiting for transfers between devices  22.8 us (36%)
  Pallas kernels  5.05 us (8%)
  other arithmetic  0.76 us (1%)
    ppermute x25, starting transfers between devices, exchange(): out.append(lax.ppermute(array, axis, pairs) if hop else array)  34.5 us
    ppermute x25, waiting for transfers between devices, exchange(): out.append(lax.ppermute(array, axis, pairs) if hop else array)  22.8 us
    pallas_call x9, Pallas kernels, call(): pl.pallas_call(functools.partial(kernel, z, hops), out_shape=outs, in_spe...  5.05 us
  transfers between devices with their start and end apart: 25, of which 11 were waited for; matrix products, arithmetic and copies ran while one was open for 1% of the time, Pallas kernels for 4%

profile of v5, /device:TPU:0, one launch (start us, length us, event | category | flops | bytes accessed | tf_op | source)
XLA Modules:
  0.0 63.2 jit_solution(12023722703525128960)
XLA Ops:
  0.0 1.7 %shard_map.37 = (f32[2,4,16,128]{3,2,1,0:T(8,128)S(1)}, f32[2,4,16,128]{3,2,1,0:T(8,128)S(1)}, f32[2,4,16,128]{3,2,1,0:T(8,128)S(1)}, f32[2,4,16,128]{3,2,1,0:T(...) custom-call(s32[2]{0:T(128)} %starts.1, ...), custom_call_target="tpu_custom_call" | custom-call | flops 262144 | bytes 2097152 | tf_op jit(solution)/shard_map/pallas_call | solution.py:178
  1.7 5.1 %collective-permute-start = (f32[2,4,16,128]{3,2,1,0:T(8,128)S(1)}, f32[2,4,16,128]{3,2,1,0:T(8,128)S(1)}, u32[]{:S(2)}, u32[]{:S(2)}) collective-permute-start(f32[2,4,16,128]{3,2,1,0:T(8,128)S(1)} %get-tuple-element.38), channel_id=1, source_target_pairs={{0,24},{8,16},{16,8},{24,0},{1,25},{9,17},{17,9},{25,1},{2,26},{10... | collective-permute-start | bytes 196616 | tf_op jit(solution)/shard_map/ppermute | solution.py:149
  6.9 1.5 %collective-permute-start.7 = (f32[4,4,16,128]{3,2,1,0:T(8,128)S(1)}, f32[4,4,16,128]{3,2,1,0:T(8,128)S(1)}, u32[]{:S(2)}, u32[]{:S(2)}) collective-permute-start(f32[4,4,16,128]{3,2,1,0:T(8,128)S(1)} %get-tuple-element.47), channel_id=1, source_target_pairs={{0,2},{1,3},{2,0},{3,1},{4,6},{5,7},{6,4},{7,5},{8,10},{9,11},{10,... | collective-permute-start | bytes 393224 | tf_op jit(solution)/shard_map/ppermute | solution.py:149
  8.4 1.5 %collective-permute-start.8 = (f32[4,4,16,128]{3,2,1,0:T(8,128)S(1)}, f32[4,4,16,128]{3,2,1,0:T(8,128)S(1)}, u32[]{:S(2)}, u32[]{:S(2)}) collective-permute-start(f32[4,4,16,128]{3,2,1,0:T(8,128)S(1)} %get-tuple-element.48), channel_id=1, source_target_pairs={{0,4},{1,5},{2,6},{3,7},{4,0},{5,1},{6,2},{7,3},{8,12},{9,13},{10,... | collective-permute-start | bytes 393224 | tf_op jit(solution)/shard_map/ppermute | solution.py:149
  9.9 0.5 collective-permute-start.9
  11.1 1.2 %collective-permute-done.7.refs_0_ = f32[4,4,16,128]{3,2,1,0:T(8,128)S(1)} collective-permute-done((f32[4,4,16,128]{3,2,1,0:T(8,128)S(1)}, f32[4,4,16,128]{3,2,1,0:T(8,128)S(1)}, u32[]{:S(2)}, u32[]{:S(2)}) %collective-permute-start.7) | collective-permute-done | bytes 131104 | tf_op jit(solution)/shard_map/ppermute | solution.py:149
  12.3 0.7 %collective-permute-start.2 = (f32[2,4,16,128]{3,2,1,0:T(8,128)S(1)}, f32[2,4,16,128]{3,2,1,0:T(8,128)S(1)}, u32[]{:S(2)}, u32[]{:S(2)}) collective-permute-start(f32[2,4,16,128]{3,2,1,0:T(8,128)S(1)} %get-tuple-element.40), channel_id=1, source_target_pairs={{0,8},{8,0},{16,24},{24,16},{1,9},{9,1},{17,25},{25,17},{2,10},{10... | collective-permute-start | bytes 196616 | tf_op jit(solution)/shard_map/ppermute | solution.py:149
  12.9 3.2 %collective-permute-done.8.refs_1_ = f32[4,4,16,128]{3,2,1,0:T(8,128)S(1)} collective-permute-done((f32[4,4,16,128]{3,2,1,0:T(8,128)S(1)}, f32[4,4,16,128]{3,2,1,0:T(8,128)S(1)}, u32[]{:S(2)}, u32[]{:S(2)}) %collective-permute-start.8) | collective-permute-done | bytes 131104 | tf_op jit(solution)/shard_map/ppermute | solution.py:149
  16.1 1.9 %collective-permute-start.16 = (f32[3,4,16,128]{3,2,1,0:T(8,128)S(1)}, f32[3,4,16,128]{3,2,1,0:T(8,128)S(1)}, u32[]{:S(2)}, u32[]{:S(2)}) collective-permute-start(f32[3,4,16,128]{3,2,1,0:T(8,128)S(1)} %get-tuple-element.59), channel_id=1, source_target_pairs={{0,24},{8,16},{16,8},{24,0},{1,25},{9,17},{17,9},{25,1},{2,26},{10... | collective-permute-start | bytes 294920 | tf_op jit(solution)/shard_map/ppermute | solution.py:149
  18.1 1.0 %collective-permute-start.17 = (f32[3,4,16,128]{3,2,1,0:T(8,128)S(1)}, f32[3,4,16,128]{3,2,1,0:T(8,128)S(1)}, u32[]{:S(2)}, u32[]{:S(2)}) collective-permute-start(f32[3,4,16,128]{3,2,1,0:T(8,128)S(1)} %get-tuple-element.60), channel_id=1, source_target_pairs={{0,16},{8,24},{16,0},{24,8},{1,17},{9,25},{17,1},{25,9},{2,18},{10... | collective-permute-start | bytes 294920 | tf_op jit(solution)/shard_map/ppermute | solution.py:149
  19.1 1.5 %collective-permute-start.18 = (f32[3,4,16,128]{3,2,1,0:T(8,128)S(1)}, f32[3,4,16,128]{3,2,1,0:T(8,128)S(1)}, u32[]{:S(2)}, u32[]{:S(2)}) collective-permute-start(f32[3,4,16,128]{3,2,1,0:T(8,128)S(1)} %get-tuple-element.61), channel_id=1, source_target_pairs={{0,8},{8,0},{16,24},{24,16},{1,9},{9,1},{17,25},{25,17},{2,10},{10... | collective-permute-start | bytes 294920 | tf_op jit(solution)/shard_map/ppermute | solution.py:149
  20.6 1.9 %collective-permute-start.10 = (f32[3,4,16,128]{3,2,1,0:T(8,128)S(1)}, f32[3,4,16,128]{3,2,1,0:T(8,128)S(1)}, u32[]{:S(2)}, u32[]{:S(2)}) collective-permute-start(f32[3,4,16,128]{3,2,1,0:T(8,128)S(1)} %get-tuple-element.51), channel_id=1, source_target_pairs={{0,24},{8,16},{16,8},{24,0},{1,25},{9,17},{17,9},{25,1},{2,26},{10... | collective-permute-start | bytes 294920 | tf_op jit(solution)/shard_map/ppermute | solution.py:149
  22.8 0.4 shard_map.38
  23.2 0.5 collective-permute-done.16.refs_2_
  23.7 7.4 %collective-permute-done.17.refs_3_ = f32[3,4,16,128]{3,2,1,0:T(8,128)S(1)} collective-permute-done((f32[3,4,16,128]{3,2,1,0:T(8,128)S(1)}, f32[3,4,16,128]{3,2,1,0:T(8,128)S(1)}, u32[]{:S(2)}, u32[]{:S(2)}) %collective-permute-start.17) | collective-permute-done | bytes 98336 | tf_op jit(solution)/shard_map/ppermute | solution.py:149
  31.1 0.5 shard_map.43
  31.8 1.3 %collective-permute-start.20 = (f32[4,4,16,128]{3,2,1,0:T(8,128)S(1)}, f32[4,4,16,128]{3,2,1,0:T(8,128)S(1)}, u32[]{:S(2)}, u32[]{:S(2)}) collective-permute-start(f32[4,4,16,128]{3,2,1,0:T(8,128)S(1)} %get-tuple-element.63), channel_id=1, source_target_pairs={{0,5},{1,4},{2,7},{3,6},{4,1},{5,0},{6,3},{7,2},{8,13},{9,12},{10,... | collective-permute-start | bytes 393224 | tf_op jit(solution)/shard_map/ppermute | solution.py:149
  33.3 0.4 collective-permute-start.21
  33.8 2.5 %collective-permute-done.12.refs_4_ = f32[3,4,16,128]{3,2,1,0:T(8,128)S(1)} collective-permute-done((f32[3,4,16,128]{3,2,1,0:T(8,128)S(1)}, f32[3,4,16,128]{3,2,1,0:T(8,128)S(1)}, u32[]{:S(2)}, u32[]{:S(2)}) %collective-permute-start.12) | collective-permute-done | bytes 98336 | tf_op jit(solution)/shard_map/ppermute | solution.py:149
  36.3 0.5 shard_map.41
  36.8 2.0 %collective-permute-start.13 = (f32[3,4,16,128]{3,2,1,0:T(8,128)S(1)}, f32[3,4,16,128]{3,2,1,0:T(8,128)S(1)}, u32[]{:S(2)}, u32[]{:S(2)}) collective-permute-start(f32[3,4,16,128]{3,2,1,0:T(8,128)S(1)} %get-tuple-element.55), channel_id=1, source_target_pairs={{0,24},{8,16},{16,8},{24,0},{1,25},{9,17},{17,9},{25,1},{2,26},{10... | collective-permute-start | bytes 294920 | tf_op jit(solution)/shard_map/ppermute | solution.py:149
  38.9 1.9 %collective-permute-start.4 = (f32[2,4,16,128]{3,2,1,0:T(8,128)S(1)}, f32[2,4,16,128]{3,2,1,0:T(8,128)S(1)}, u32[]{:S(2)}, u32[]{:S(2)}) collective-permute-start(f32[2,4,16,128]{3,2,1,0:T(8,128)S(1)} %get-tuple-element.44), channel_id=1, source_target_pairs={{0,24},{8,16},{16,8},{24,0},{1,25},{9,17},{17,9},{25,1},{2,26},{10... | collective-permute-start | bytes 196616 | tf_op jit(solution)/shard_map/ppermute | solution.py:149
  40.8 2.5 %collective-permute-start.6 = (f32[2,4,16,128]{3,2,1,0:T(8,128)S(1)}, f32[2,4,16,128]{3,2,1,0:T(8,128)S(1)}, u32[]{:S(2)}, u32[]{:S(2)}) collective-permute-start(f32[2,4,16,128]{3,2,1,0:T(8,128)S(1)} %get-tuple-element.46), channel_id=1, source_target_pairs={{0,8},{8,0},{16,24},{24,16},{1,9},{9,1},{17,25},{25,17},{2,10},{10... | collective-permute-start | bytes 196616 | tf_op jit(solution)/shard_map/ppermute | solution.py:149
  43.4 1.9 %collective-permute-start.22 = (f32[3,4,16,128]{3,2,1,0:T(8,128)S(1)}, f32[3,4,16,128]{3,2,1,0:T(8,128)S(1)}, u32[]{:S(2)}, u32[]{:S(2)}) collective-permute-start(f32[3,4,16,128]{3,2,1,0:T(8,128)S(1)} %get-tuple-element.66), channel_id=1, source_target_pairs={{0,24},{8,16},{16,8},{24,0},{1,25},{9,17},{17,9},{25,1},{2,26},{10... | collective-permute-start | bytes 294920 | tf_op jit(solution)/shard_map/ppermute | solution.py:149
  45.3 0.4 collective-permute-done.4.refs_1_
  45.7 5.8 %collective-permute-start.14 = (f32[3,4,16,128]{3,2,1,0:T(8,128)S(1)}, f32[3,4,16,128]{3,2,1,0:T(8,128)S(1)}, u32[]{:S(2)}, u32[]{:S(2)}) collective-permute-start(f32[3,4,16,128]{3,2,1,0:T(8,128)S(1)} %get-tuple-element.56), channel_id=1, source_target_pairs={{0,16},{8,24},{16,0},{24,8},{1,17},{9,25},{17,1},{25,9},{2,18},{10... | collective-permute-start | bytes 294920 | tf_op jit(solution)/shard_map/ppermute | solution.py:149
  51.5 0.3 collective-permute-done.5.refs_2_
  51.8 2.6 %collective-permute-start.23 = (f32[3,4,16,128]{3,2,1,0:T(8,128)S(1)}, f32[3,4,16,128]{3,2,1,0:T(8,128)S(1)}, u32[]{:S(2)}, u32[]{:S(2)}) collective-permute-start(f32[3,4,16,128]{3,2,1,0:T(8,128)S(1)} %get-tuple-element.67), channel_id=1, source_target_pairs={{0,16},{8,24},{16,0},{24,8},{1,17},{9,25},{17,1},{25,9},{2,18},{10... | collective-permute-start | bytes 294920 | tf_op jit(solution)/shard_map/ppermute | solution.py:149
  54.4 4.9 %collective-permute-done.14.refs_6_ = f32[3,4,16,128]{3,2,1,0:T(8,128)S(1)} collective-permute-done((f32[3,4,16,128]{3,2,1,0:T(8,128)S(1)}, f32[3,4,16,128]{3,2,1,0:T(8,128)S(1)}, u32[]{:S(2)}, u32[]{:S(2)}) %collective-permute-start.14) | collective-permute-done | bytes 98336 | tf_op jit(solution)/shard_map/ppermute | solution.py:149
  59.3 1.0 %shard_map.42.refs_0_ = f32[4,128,512]{2,1,0:T(8,128)} custom-call(f32[2,4,16,128]{3,2,1,0:T(8,128)S(1)} %get-tuple-element.43.refs_0_, f32[2,4,16,128]{3,2,1,0:T(8,128)S(1)} %collective-permute-done.4.refs_1_, f32[2,4,16,128]{3,2,1,0:T(8,128)S(1)} %collective-permute-done.5.refs_2_, f32[2,4,16,128]{3,2,1,0:T(8,128)S(1)} %collective-permute-done.6.refs_3_, ...), custom_call_target="tpu_custom_call" | custom-call | flops 262144 | bytes 2097152 | tf_op jit(solution)/shard_map/pallas_call | solution.py:178
  60.3 1.8 %collective-permute-done.23.refs_3_ = f32[3,4,16,128]{3,2,1,0:T(8,128)S(1)} collective-permute-done((f32[3,4,16,128]{3,2,1,0:T(8,128)S(1)}, f32[3,4,16,128]{3,2,1,0:T(8,128)S(1)}, u32[]{:S(2)}, u32[]{:S(2)}) %collective-permute-start.23) | collective-permute-done | bytes 98336 | tf_op jit(solution)/shard_map/ppermute | solution.py:149
  62.4 0.8 %shard_map.45 = f32[4,128,512]{2,1,0:T(8,128)} custom-call(f32[4,128,512]{2,1,0:T(8,128)} %shard_map.42.refs_0_, f32[3,4,16,128]{3,2,1,0:T(8,128)S(1)} %get-tuple-element.65.refs_1_, f32[3,4,16,128]{3,2,1,0:T(8,128)S(1)} %collective-permute-done.22.refs_2_, f32[3,4,16,128]{3,2,1,0:T(8,128)S(1)} %collective-permute-done.23.refs_3_, ...), custom_call_target="tpu_custom_call", output_to_operand_aliasing={{}: (0, {})} | custom-call | flops 262144 | bytes 2097152 | tf_op jit(solution)/shard_map/pallas_call | solution.py:178
  (40 shorter events, 1.7 us)
Async XLA Ops:
  0.0 10.5 %copy-start = (s32[16]{0:T(128)S(1)}, s32[16]{0:T(128)}, u32[]{:S(2)}) copy-start(s32[16]{0:T(128)} %param.4) | copy-start | bytes 196
  1.7 17.4 %collective-permute-start = (f32[2,4,16,128]{3,2,1,0:T(8,128)S(1)}, f32[2,4,16,128]{3,2,1,0:T(8,128)S(1)}, u32[]{:S(2)}, u32[]{:S(2)}) collective-permute-start(f32[2,4,16,128]{3,2,1,0:T(8,128)S(1)} %get-tuple-element.38), channel_id=1, source_target_pairs={{0,24},{8,16},{16,8},{24,0},{1,25},{9,17},{17,9},{25,1},{2,26},{10... | collective-permute-start | bytes 196616 | tf_op jit(solution)/shard_map/ppermute | solution.py:149
  6.9 13.8 %collective-permute-start.1 = (f32[2,4,16,128]{3,2,1,0:T(8,128)S(1)}, f32[2,4,16,128]{3,2,1,0:T(8,128)S(1)}, u32[]{:S(2)}, u32[]{:S(2)}) collective-permute-start(f32[2,4,16,128]{3,2,1,0:T(8,128)S(1)} %get-tuple-element.39), channel_id=1, source_target_pairs={{0,16},{8,24},{16,0},{24,8},{1,17},{9,25},{17,1},{25,9},{2,18},{10... | collective-permute-start | bytes 196616 | tf_op jit(solution)/shard_map/ppermute | solution.py:149
  6.9 5.4 %collective-permute-start.7 = (f32[4,4,16,128]{3,2,1,0:T(8,128)S(1)}, f32[4,4,16,128]{3,2,1,0:T(8,128)S(1)}, u32[]{:S(2)}, u32[]{:S(2)}) collective-permute-start(f32[4,4,16,128]{3,2,1,0:T(8,128)S(1)} %get-tuple-element.47), channel_id=1, source_target_pairs={{0,2},{1,3},{2,0},{3,1},{4,6},{5,7},{6,4},{7,5},{8,10},{9,11},{10,... | collective-permute-start | bytes 393224 | tf_op jit(solution)/shard_map/ppermute | solution.py:149
  8.4 7.8 %collective-permute-start.8 = (f32[4,4,16,128]{3,2,1,0:T(8,128)S(1)}, f32[4,4,16,128]{3,2,1,0:T(8,128)S(1)}, u32[]{:S(2)}, u32[]{:S(2)}) collective-permute-start(f32[4,4,16,128]{3,2,1,0:T(8,128)S(1)} %get-tuple-element.48), channel_id=1, source_target_pairs={{0,4},{1,5},{2,6},{3,7},{4,0},{5,1},{6,2},{7,3},{8,12},{9,13},{10,... | collective-permute-start | bytes 393224 | tf_op jit(solution)/shard_map/ppermute | solution.py:149
  9.9 8.2 %collective-permute-start.9 = (f32[4,4,16,128]{3,2,1,0:T(8,128)S(1)}, f32[4,4,16,128]{3,2,1,0:T(8,128)S(1)}, u32[]{:S(2)}, u32[]{:S(2)}) collective-permute-start(f32[4,4,16,128]{3,2,1,0:T(8,128)S(1)} %get-tuple-element.49), channel_id=1, source_target_pairs={{0,6},{1,7},{2,4},{3,5},{4,2},{5,3},{6,0},{7,1},{8,14},{9,15},{10,... | collective-permute-start | bytes 393224 | tf_op jit(solution)/shard_map/ppermute | solution.py:149
  12.3 10.3 %collective-permute-start.2 = (f32[2,4,16,128]{3,2,1,0:T(8,128)S(1)}, f32[2,4,16,128]{3,2,1,0:T(8,128)S(1)}, u32[]{:S(2)}, u32[]{:S(2)}) collective-permute-start(f32[2,4,16,128]{3,2,1,0:T(8,128)S(1)} %get-tuple-element.40), channel_id=1, source_target_pairs={{0,8},{8,0},{16,24},{24,16},{1,9},{9,1},{17,25},{25,17},{2,10},{10... | collective-permute-start | bytes 196616 | tf_op jit(solution)/shard_map/ppermute | solution.py:149
  16.1 7.6 %collective-permute-start.16 = (f32[3,4,16,128]{3,2,1,0:T(8,128)S(1)}, f32[3,4,16,128]{3,2,1,0:T(8,128)S(1)}, u32[]{:S(2)}, u32[]{:S(2)}) collective-permute-start(f32[3,4,16,128]{3,2,1,0:T(8,128)S(1)} %get-tuple-element.59), channel_id=1, source_target_pairs={{0,24},{8,16},{16,8},{24,0},{1,25},{9,17},{17,9},{25,1},{2,26},{10... | collective-permute-start | bytes 294920 | tf_op jit(solution)/shard_map/ppermute | solution.py:149
  18.1 13.0 %collective-permute-start.17 = (f32[3,4,16,128]{3,2,1,0:T(8,128)S(1)}, f32[3,4,16,128]{3,2,1,0:T(8,128)S(1)}, u32[]{:S(2)}, u32[]{:S(2)}) collective-permute-start(f32[3,4,16,128]{3,2,1,0:T(8,128)S(1)} %get-tuple-element.60), channel_id=1, source_target_pairs={{0,16},{8,24},{16,0},{24,8},{1,17},{9,25},{17,1},{25,9},{2,18},{10... | collective-permute-start | bytes 294920 | tf_op jit(solution)/shard_map/ppermute | solution.py:149
  19.1 12.0 %collective-permute-start.18 = (f32[3,4,16,128]{3,2,1,0:T(8,128)S(1)}, f32[3,4,16,128]{3,2,1,0:T(8,128)S(1)}, u32[]{:S(2)}, u32[]{:S(2)}) collective-permute-start(f32[3,4,16,128]{3,2,1,0:T(8,128)S(1)} %get-tuple-element.61), channel_id=1, source_target_pairs={{0,8},{8,0},{16,24},{24,16},{1,9},{9,1},{17,25},{25,17},{2,10},{10... | collective-permute-start | bytes 294920 | tf_op jit(solution)/shard_map/ppermute | solution.py:149
  20.6 11.1 %collective-permute-start.10 = (f32[3,4,16,128]{3,2,1,0:T(8,128)S(1)}, f32[3,4,16,128]{3,2,1,0:T(8,128)S(1)}, u32[]{:S(2)}, u32[]{:S(2)}) collective-permute-start(f32[3,4,16,128]{3,2,1,0:T(8,128)S(1)} %get-tuple-element.51), channel_id=1, source_target_pairs={{0,24},{8,16},{16,8},{24,0},{1,25},{9,17},{17,9},{25,1},{2,26},{10... | collective-permute-start | bytes 294920 | tf_op jit(solution)/shard_map/ppermute | solution.py:149
  22.6 10.8 %collective-permute-start.11 = (f32[3,4,16,128]{3,2,1,0:T(8,128)S(1)}, f32[3,4,16,128]{3,2,1,0:T(8,128)S(1)}, u32[]{:S(2)}, u32[]{:S(2)}) collective-permute-start(f32[3,4,16,128]{3,2,1,0:T(8,128)S(1)} %get-tuple-element.52), channel_id=1, source_target_pairs={{0,16},{8,24},{16,0},{24,8},{1,17},{9,25},{17,1},{25,9},{2,18},{10... | collective-permute-start | bytes 294920 | tf_op jit(solution)/shard_map/ppermute | solution.py:149
  23.7 15.1 %collective-permute-start.3 = (f32[4,4,16,128]{3,2,1,0:T(8,128)S(1)}, f32[4,4,16,128]{3,2,1,0:T(8,128)S(1)}, u32[]{:S(2)}, u32[]{:S(2)}) collective-permute-start(f32[4,4,16,128]{3,2,1,0:T(8,128)S(1)} %get-tuple-element.42), channel_id=1, source_target_pairs={{0,1},{1,0},{2,3},{3,2},{4,5},{5,4},{6,7},{7,6},{8,9},{9,8},{10,11... | collective-permute-start | bytes 393224 | tf_op jit(solution)/shard_map/ppermute | solution.py:149
  31.6 4.7 %collective-permute-start.12 = (f32[3,4,16,128]{3,2,1,0:T(8,128)S(1)}, f32[3,4,16,128]{3,2,1,0:T(8,128)S(1)}, u32[]{:S(2)}, u32[]{:S(2)}) collective-permute-start(f32[3,4,16,128]{3,2,1,0:T(8,128)S(1)} %get-tuple-element.53), channel_id=1, source_target_pairs={{0,8},{8,0},{16,24},{24,16},{1,9},{9,1},{17,25},{25,17},{2,10},{10... | collective-permute-start | bytes 294920 | tf_op jit(solution)/shard_map/ppermute | solution.py:149
  31.7 9.1 %collective-permute-start.19 = (f32[4,4,16,128]{3,2,1,0:T(8,128)S(1)}, f32[4,4,16,128]{3,2,1,0:T(8,128)S(1)}, u32[]{:S(2)}, u32[]{:S(2)}) collective-permute-start(f32[4,4,16,128]{3,2,1,0:T(8,128)S(1)} %get-tuple-element.62), channel_id=1, source_target_pairs={{0,3},{1,2},{2,1},{3,0},{4,7},{5,6},{6,5},{7,4},{8,11},{9,10},{10,... | collective-permute-start | bytes 393224 | tf_op jit(solution)/shard_map/ppermute | solution.py:149
  31.8 9.0 %collective-permute-start.20 = (f32[4,4,16,128]{3,2,1,0:T(8,128)S(1)}, f32[4,4,16,128]{3,2,1,0:T(8,128)S(1)}, u32[]{:S(2)}, u32[]{:S(2)}) collective-permute-start(f32[4,4,16,128]{3,2,1,0:T(8,128)S(1)} %get-tuple-element.63), channel_id=1, source_target_pairs={{0,5},{1,4},{2,7},{3,6},{4,1},{5,0},{6,3},{7,2},{8,13},{9,12},{10,... | collective-permute-start | bytes 393224 | tf_op jit(solution)/shard_map/ppermute | solution.py:149
  33.3 10.0 %collective-permute-start.21 = (f32[4,4,16,128]{3,2,1,0:T(8,128)S(1)}, f32[4,4,16,128]{3,2,1,0:T(8,128)S(1)}, u32[]{:S(2)}, u32[]{:S(2)}) collective-permute-start(f32[4,4,16,128]{3,2,1,0:T(8,128)S(1)} %get-tuple-element.64), channel_id=1, source_target_pairs={{0,7},{1,6},{2,5},{3,4},{4,3},{5,2},{6,1},{7,0},{8,15},{9,14},{10,... | collective-permute-start | bytes 393224 | tf_op jit(solution)/shard_map/ppermute | solution.py:149
  36.8 17.6 %collective-permute-start.13 = (f32[3,4,16,128]{3,2,1,0:T(8,128)S(1)}, f32[3,4,16,128]{3,2,1,0:T(8,128)S(1)}, u32[]{:S(2)}, u32[]{:S(2)}) collective-permute-start(f32[3,4,16,128]{3,2,1,0:T(8,128)S(1)} %get-tuple-element.55), channel_id=1, source_target_pairs={{0,24},{8,16},{16,8},{24,0},{1,25},{9,17},{17,9},{25,1},{2,26},{10... | collective-permute-start | bytes 294920 | tf_op jit(solution)/shard_map/ppermute | solution.py:149
  38.9 6.9 %collective-permute-start.4 = (f32[2,4,16,128]{3,2,1,0:T(8,128)S(1)}, f32[2,4,16,128]{3,2,1,0:T(8,128)S(1)}, u32[]{:S(2)}, u32[]{:S(2)}) collective-permute-start(f32[2,4,16,128]{3,2,1,0:T(8,128)S(1)} %get-tuple-element.44), channel_id=1, source_target_pairs={{0,24},{8,16},{16,8},{24,0},{1,25},{9,17},{17,9},{25,1},{2,26},{10... | collective-permute-start | bytes 196616 | tf_op jit(solution)/shard_map/ppermute | solution.py:149
  40.8 11.0 %collective-permute-start.5 = (f32[2,4,16,128]{3,2,1,0:T(8,128)S(1)}, f32[2,4,16,128]{3,2,1,0:T(8,128)S(1)}, u32[]{:S(2)}, u32[]{:S(2)}) collective-permute-start(f32[2,4,16,128]{3,2,1,0:T(8,128)S(1)} %get-tuple-element.45), channel_id=1, source_target_pairs={{0,16},{8,24},{16,0},{24,8},{1,17},{9,25},{17,1},{25,9},{2,18},{10... | collective-permute-start | bytes 196616 | tf_op jit(solution)/shard_map/ppermute | solution.py:149
  40.8 11.0 %collective-permute-start.6 = (f32[2,4,16,128]{3,2,1,0:T(8,128)S(1)}, f32[2,4,16,128]{3,2,1,0:T(8,128)S(1)}, u32[]{:S(2)}, u32[]{:S(2)}) collective-permute-start(f32[2,4,16,128]{3,2,1,0:T(8,128)S(1)} %get-tuple-element.46), channel_id=1, source_target_pairs={{0,8},{8,0},{16,24},{24,16},{1,9},{9,1},{17,25},{25,17},{2,10},{10... | collective-permute-start | bytes 196616 | tf_op jit(solution)/shard_map/ppermute | solution.py:149
  43.4 17.0 %collective-permute-start.22 = (f32[3,4,16,128]{3,2,1,0:T(8,128)S(1)}, f32[3,4,16,128]{3,2,1,0:T(8,128)S(1)}, u32[]{:S(2)}, u32[]{:S(2)}) collective-permute-start(f32[3,4,16,128]{3,2,1,0:T(8,128)S(1)} %get-tuple-element.66), channel_id=1, source_target_pairs={{0,24},{8,16},{16,8},{24,0},{1,25},{9,17},{17,9},{25,1},{2,26},{10... | collective-permute-start | bytes 294920 | tf_op jit(solution)/shard_map/ppermute | solution.py:149
  45.7 13.6 %collective-permute-start.14 = (f32[3,4,16,128]{3,2,1,0:T(8,128)S(1)}, f32[3,4,16,128]{3,2,1,0:T(8,128)S(1)}, u32[]{:S(2)}, u32[]{:S(2)}) collective-permute-start(f32[3,4,16,128]{3,2,1,0:T(8,128)S(1)} %get-tuple-element.56), channel_id=1, source_target_pairs={{0,16},{8,24},{16,0},{24,8},{1,17},{9,25},{17,1},{25,9},{2,18},{10... | collective-permute-start | bytes 294920 | tf_op jit(solution)/shard_map/ppermute | solution.py:149
  51.8 7.5 %collective-permute-start.15 = (f32[3,4,16,128]{3,2,1,0:T(8,128)S(1)}, f32[3,4,16,128]{3,2,1,0:T(8,128)S(1)}, u32[]{:S(2)}, u32[]{:S(2)}) collective-permute-start(f32[3,4,16,128]{3,2,1,0:T(8,128)S(1)} %get-tuple-element.57), channel_id=1, source_target_pairs={{0,8},{8,0},{16,24},{24,16},{1,9},{9,1},{17,25},{25,17},{2,10},{10... | collective-permute-start | bytes 294920 | tf_op jit(solution)/shard_map/ppermute | solution.py:149
  51.8 10.3 %collective-permute-start.23 = (f32[3,4,16,128]{3,2,1,0:T(8,128)S(1)}, f32[3,4,16,128]{3,2,1,0:T(8,128)S(1)}, u32[]{:S(2)}, u32[]{:S(2)}) collective-permute-start(f32[3,4,16,128]{3,2,1,0:T(8,128)S(1)} %get-tuple-element.67), channel_id=1, source_target_pairs={{0,16},{8,24},{16,0},{24,8},{1,17},{9,25},{17,1},{25,9},{2,18},{10... | collective-permute-start | bytes 294920 | tf_op jit(solution)/shard_map/ppermute | solution.py:149
  54.4 8.0 %collective-permute-start.24 = (f32[3,4,16,128]{3,2,1,0:T(8,128)S(1)}, f32[3,4,16,128]{3,2,1,0:T(8,128)S(1)}, u32[]{:S(2)}, u32[]{:S(2)}) collective-permute-start(f32[3,4,16,128]{3,2,1,0:T(8,128)S(1)} %get-tuple-element.68), channel_id=1, source_target_pairs={{0,8},{8,0},{16,24},{24,16},{1,9},{9,1},{17,25},{25,17},{2,10},{10... | collective-permute-start | bytes 294920 | tf_op jit(solution)/shard_map/ppermute | solution.py:149

commit v6 on v5

--- a/solution.py
+++ b/solution.py
@@ -41,6 +41,7 @@
     def __init__(self, mesh):
         self.shares, self.rows = mesh.shape["share"], mesh.shape["row"]
         self.share = [0, *range(self.shares - 1, 0, -1)]
+        self.apart = self.shares - (self.shares - 1) // 3
         others = range(2, self.rows)
         self.near = [0, 1]
         self.middle = [hop for hop in others if hop % 2 == 1]
@@ -66,8 +67,9 @@
 
 
 def cut(z, hops, starts, pieces, *refs):
-    count = 2 * z.shares + len(hops.far)
-    near, middle, far = refs[: z.shares], refs[z.shares : 2 * z.shares], refs[2 * z.shares : count]
+    count = z.shares + hops.apart + len(hops.far)
+    near, middle = refs[: z.shares], refs[z.shares : z.shares + hops.apart]
+    far = refs[z.shares + hops.apart : count]
     firsts, columns, sems = refs[count:]
     share, row = lax.axis_index("share"), lax.axis_index("row")
     copies = [pltpu.make_async_copy(starts, firsts, sems.at[0])]
@@ -85,10 +87,14 @@
 
     for copy in copies[1:]:
         copy.wait()
-    for early, rows in ((near, hops.near), (middle, hops.middle)):
-        for m, share_hop in enumerate(hops.share):
-            for p, row_hop in enumerate(rows):
-                early[m][p] = part(row_hop, share_hop)
+    for m, share_hop in enumerate(hops.share):
+        for p, row_hop in enumerate(hops.near):
+            near[m][p] = part(row_hop, share_hop)
+        for p, row_hop in enumerate(hops.middle):
+            if m < hops.apart:
+                middle[m][p] = part(row_hop, share_hop)
+            else:
+                near[m][len(hops.near) + p] = part(row_hop, share_hop)
     for p, row_hop in enumerate(hops.far):
         for m, share_hop in enumerate(hops.share):
             far[p][m] = part(row_hop, share_hop)
@@ -101,7 +107,7 @@
             outs[m][p] = sent[m]
 
 
-def mix(z, hops, by_row, weights, *refs):
+def mix(z, hops, rows, skip, by_row, weights, *refs):
     ins, outs, spread = refs[: z.shares], refs[z.shares : -1], refs[-1]
     share = lax.axis_index("share")
     table = weights[...]
@@ -111,7 +117,8 @@
         totals = [None] * z.kept
         for n, source in enumerate(hops.share):
             for i in range(z.held):
-                values = ins[n][:, i]
+                first = skip if n >= hops.apart else 0
+                values = ins[n][first : first + rows, i]
                 for k in range(z.kept):
                     line = pl.ds((share ^ target) * z.kept + k, 1)
                     term = spread[(share ^ source) * z.held + i, line] * values
@@ -201,11 +208,11 @@
         outs = slots(shares, len(arrays), blocks)
         return call(regroup, outs, arrays, [VMEM] * len(arrays), [VMEM] * shares)
 
-    def mixed(arrays, rows, by_row):
+    def mixed(arrays, rows, by_row, skip=0):
         outs = slots(rows, shares, z.kept) if by_row else slots(shares, rows, z.kept)
         specs = [VMEM] * (1 + shares)
         return call(
-            lambda z, hops, *refs: mix(z, hops, by_row, *refs),
+            lambda z, hops, *refs: mix(z, hops, rows, skip, by_row, *refs),
             outs,
             (weights, *arrays),
             specs,
@@ -226,8 +233,8 @@
             input_output_aliases={0: 0} if base else {},
         )
 
-    def mixed_and_crossed(arrays, rows):
-        arrays = mixed(arrays, len(rows), True)
+    def mixed_and_crossed(arrays, rows, skip=0):
+        arrays = mixed(arrays, len(rows), True, skip)
         arrays = over_rows(arrays, rows)
         return regrouped(arrays, z.kept)
 
@@ -237,16 +244,20 @@
         pltpu.VMEM((z.held, z.depth, z.columns), jnp.float32),
         pltpu.SemaphoreType.DMA((z.held + 1,)),
     ]
-    parts = slots(shares, len(hops.near), z.held) + slots(shares, len(hops.middle), z.held)
-    parts += slots(len(hops.far), shares, z.held)
+    count_near, count_middle = len(hops.near), len(hops.middle)
+    parts = slots(hops.apart, count_near, z.held)
+    parts += slots(shares - hops.apart, count_near + count_middle, z.held)
+    parts += slots(hops.apart, count_middle, z.held) + slots(len(hops.far), shares, z.held)
     parts = call(cut, parts, in_hbm, [ANY, ANY], [VMEM] * len(parts), scratch)
-    near = over_shares(parts[:shares])
-    middle = over_shares(parts[shares : 2 * shares])
-    far = over_rows(parts[2 * shares :], hops.far)
+    near, parts = over_shares(parts[:shares]), parts[shares:]
+    middle, far = parts[: hops.apart], parts[hops.apart :]
+    middle = exchange(middle, "share", shares, hops.share[: hops.apart])
+    middle += near[hops.apart :]
+    far = over_rows(far, hops.far)
     far = over_shares(regrouped(far, z.held))
     near = over_shares(mixed_and_crossed(near, hops.near))
     far = over_shares(mixed(far, len(hops.far), False))
-    middle = over_shares(mixed_and_crossed(middle, hops.middle))
+    middle = over_shares(mixed_and_crossed(middle, hops.middle, count_near))
     out = placed(near + far, [hops.near, hops.far])
     return placed(middle, [hops.middle], (out,))
 

time: 63.4 us -> 60.6 us (0.956)
  waiting for transfers between devices: 22.8 us -> 17 us
  starting transfers between devices: 34.5 us -> 37.4 us
    ppermute x25 -> x24, waiting for transfers between devices: 22.8 us -> 17 us  [exchange(): out.append(lax.ppermute(array, axis, pairs) if hop else array)]
    ppermute x25 -> x24, starting transfers between devices: 34.5 us -> 37.4 us  [exchange(): out.append(lax.ppermute(array, axis, pairs) if hop else array)]
  transfers between devices with their start and end apart: 25 -> 24, of which waited for: 11 -> 7; matrix products, arithmetic and copies ran while one was open for 1% -> 1% of each run, Pallas kernels for 4% -> 4%
where the time goes in v6:
time: 60.6 us; the launch traced here: 60.4 us
  starting transfers between devices  37.4 us (62%)
  waiting for transfers between devices  17 us (28%)
  Pallas kernels  5.06 us (8%)
  other arithmetic  0.76 us (1%)
    ppermute x24, starting transfers between devices, exchange(): out.append(lax.ppermute(array, axis, pairs) if hop else array)  37.4 us
    ppermute x24, waiting for transfers between devices, exchange(): out.append(lax.ppermute(array, axis, pairs) if hop else array)  17 us
    pallas_call x9, Pallas kernels, call(): pl.pallas_call(functools.partial(kernel, z, hops), out_shape=outs, in_spe...  5.06 us
  transfers between devices with their start and end apart: 24, of which 7 were waited for; matrix products, arithmetic and copies ran while one was open for 1% of the time, Pallas kernels for 4%

profile of v6, /device:TPU:0, one launch (start us, length us, event | category | flops | bytes accessed | tf_op | source)
XLA Modules:
  0.0 60.4 jit_solution(13906605795389081516)
XLA Ops:
  0.0 1.7 %shard_map.37 = (f32[2,4,16,128]{3,2,1,0:T(8,128)S(1)}, f32[2,4,16,128]{3,2,1,0:T(8,128)S(1)}, f32[2,4,16,128]{3,2,1,0:T(8,128)S(1)}, f32[5,4,16,128]{3,2,1,0:T(...) custom-call(s32[2]{0:T(128)} %starts.1, ...), custom_call_target="tpu_custom_call" | custom-call | flops 262144 | bytes 2097152 | tf_op jit(solution)/shard_map/pallas_call | solution.py:185
  1.7 5.1 %collective-permute-start = (f32[2,4,16,128]{3,2,1,0:T(8,128)S(1)}, f32[2,4,16,128]{3,2,1,0:T(8,128)S(1)}, u32[]{:S(2)}, u32[]{:S(2)}) collective-permute-start(f32[2,4,16,128]{3,2,1,0:T(8,128)S(1)} %get-tuple-element.37), channel_id=1, source_target_pairs={{0,24},{8,16},{16,8},{24,0},{1,25},{9,17},{17,9},{25,1},{2,26},{10... | collective-permute-start | bytes 196616 | tf_op jit(solution)/shard_map/ppermute | solution.py:156
  6.9 1.5 %collective-permute-start.7 = (f32[4,4,16,128]{3,2,1,0:T(8,128)S(1)}, f32[4,4,16,128]{3,2,1,0:T(8,128)S(1)}, u32[]{:S(2)}, u32[]{:S(2)}) collective-permute-start(f32[4,4,16,128]{3,2,1,0:T(8,128)S(1)} %get-tuple-element.46), channel_id=1, source_target_pairs={{0,2},{1,3},{2,0},{3,1},{4,6},{5,7},{6,4},{7,5},{8,10},{9,11},{10,... | collective-permute-start | bytes 393224 | tf_op jit(solution)/shard_map/ppermute | solution.py:156
  8.4 1.5 %collective-permute-start.8 = (f32[4,4,16,128]{3,2,1,0:T(8,128)S(1)}, f32[4,4,16,128]{3,2,1,0:T(8,128)S(1)}, u32[]{:S(2)}, u32[]{:S(2)}) collective-permute-start(f32[4,4,16,128]{3,2,1,0:T(8,128)S(1)} %get-tuple-element.47), channel_id=1, source_target_pairs={{0,4},{1,5},{2,6},{3,7},{4,0},{5,1},{6,2},{7,3},{8,12},{9,13},{10,... | collective-permute-start | bytes 393224 | tf_op jit(solution)/shard_map/ppermute | solution.py:156
  9.9 0.5 collective-permute-start.9
  10.6 0.2 select_reduce_fusion
  11.1 1.2 %collective-permute-done.7.refs_0_ = f32[4,4,16,128]{3,2,1,0:T(8,128)S(1)} collective-permute-done((f32[4,4,16,128]{3,2,1,0:T(8,128)S(1)}, f32[4,4,16,128]{3,2,1,0:T(8,128)S(1)}, u32[]{:S(2)}, u32[]{:S(2)}) %collective-permute-start.7) | collective-permute-done | bytes 131104 | tf_op jit(solution)/shard_map/ppermute | solution.py:156
  12.3 2.2 %collective-permute-start.16 = (f32[3,4,16,128]{3,2,1,0:T(8,128)S(1)}, f32[3,4,16,128]{3,2,1,0:T(8,128)S(1)}, u32[]{:S(2)}, u32[]{:S(2)}) collective-permute-start(f32[3,4,16,128]{3,2,1,0:T(8,128)S(1)} %get-tuple-element.58), channel_id=1, source_target_pairs={{0,24},{8,16},{16,8},{24,0},{1,25},{9,17},{17,9},{25,1},{2,26},{10... | collective-permute-start | bytes 294920 | tf_op jit(solution)/shard_map/ppermute | solution.py:156
  14.5 1.7 %collective-permute-done.8.refs_1_ = f32[4,4,16,128]{3,2,1,0:T(8,128)S(1)} collective-permute-done((f32[4,4,16,128]{3,2,1,0:T(8,128)S(1)}, f32[4,4,16,128]{3,2,1,0:T(8,128)S(1)}, u32[]{:S(2)}, u32[]{:S(2)}) %collective-permute-start.8) | collective-permute-done | bytes 131104 | tf_op jit(solution)/shard_map/ppermute | solution.py:156
  16.1 2.9 %collective-permute-start.17 = (f32[3,4,16,128]{3,2,1,0:T(8,128)S(1)}, f32[3,4,16,128]{3,2,1,0:T(8,128)S(1)}, u32[]{:S(2)}, u32[]{:S(2)}) collective-permute-start(f32[3,4,16,128]{3,2,1,0:T(8,128)S(1)} %get-tuple-element.59), channel_id=1, source_target_pairs={{0,16},{8,24},{16,0},{24,8},{1,17},{9,25},{17,1},{25,9},{2,18},{10... | collective-permute-start | bytes 294920 | tf_op jit(solution)/shard_map/ppermute | solution.py:156
  19.1 1.5 %collective-permute-start.10 = (f32[3,4,16,128]{3,2,1,0:T(8,128)S(1)}, f32[3,4,16,128]{3,2,1,0:T(8,128)S(1)}, u32[]{:S(2)}, u32[]{:S(2)}) collective-permute-start(f32[3,4,16,128]{3,2,1,0:T(8,128)S(1)} %get-tuple-element.50), channel_id=1, source_target_pairs={{0,24},{8,16},{16,8},{24,0},{1,25},{9,17},{17,9},{25,1},{2,26},{10... | collective-permute-start | bytes 294920 | tf_op jit(solution)/shard_map/ppermute | solution.py:156
  20.7 2.0 %collective-permute-start.11 = (f32[3,4,16,128]{3,2,1,0:T(8,128)S(1)}, f32[3,4,16,128]{3,2,1,0:T(8,128)S(1)}, u32[]{:S(2)}, u32[]{:S(2)}) collective-permute-start(f32[3,4,16,128]{3,2,1,0:T(8,128)S(1)} %get-tuple-element.51), channel_id=1, source_target_pairs={{0,16},{8,24},{16,0},{24,8},{1,17},{9,25},{17,1},{25,9},{2,18},{10... | collective-permute-start | bytes 294920 | tf_op jit(solution)/shard_map/ppermute | solution.py:156
  22.7 2.4 %collective-permute-done.2.refs_4_ = f32[5,4,16,128]{3,2,1,0:T(8,128)S(1)} collective-permute-done((f32[5,4,16,128]{3,2,1,0:T(8,128)S(1)}, f32[5,4,16,128]{3,2,1,0:T(8,128)S(1)}, u32[]{:S(2)}, u32[]{:S(2)}) %collective-permute-start.2) | collective-permute-done | bytes 163872 | tf_op jit(solution)/shard_map/ppermute | solution.py:156
  25.1 0.4 shard_map.38
  25.6 0.9 %collective-permute-start.12 = (f32[3,4,16,128]{3,2,1,0:T(8,128)S(1)}, f32[3,4,16,128]{3,2,1,0:T(8,128)S(1)}, u32[]{:S(2)}, u32[]{:S(2)}) collective-permute-start(f32[3,4,16,128]{3,2,1,0:T(8,128)S(1)} %get-tuple-element.52), channel_id=1, source_target_pairs={{0,8},{8,0},{16,24},{24,16},{1,9},{9,1},{17,25},{25,17},{2,10},{10... | collective-permute-start | bytes 294920 | tf_op jit(solution)/shard_map/ppermute | solution.py:156
  26.4 1.7 %collective-permute-done.17.refs_3_ = f32[3,4,16,128]{3,2,1,0:T(8,128)S(1)} collective-permute-done((f32[3,4,16,128]{3,2,1,0:T(8,128)S(1)}, f32[3,4,16,128]{3,2,1,0:T(8,128)S(1)}, u32[]{:S(2)}, u32[]{:S(2)}) %collective-permute-start.17) | collective-permute-done | bytes 98336 | tf_op jit(solution)/shard_map/ppermute | solution.py:156
  28.1 0.5 shard_map.43
  28.7 2.8 %collective-permute-start.19 = (f32[4,4,16,128]{3,2,1,0:T(8,128)S(1)}, f32[4,4,16,128]{3,2,1,0:T(8,128)S(1)}, u32[]{:S(2)}, u32[]{:S(2)}) collective-permute-start(f32[4,4,16,128]{3,2,1,0:T(8,128)S(1)} %get-tuple-element.61), channel_id=1, source_target_pairs={{0,5},{1,4},{2,7},{3,6},{4,1},{5,0},{6,3},{7,2},{8,13},{9,12},{10,... | collective-permute-start | bytes 393224 | tf_op jit(solution)/shard_map/ppermute | solution.py:156
  31.5 0.7 %collective-permute-done.12.refs_4_ = f32[3,4,16,128]{3,2,1,0:T(8,128)S(1)} collective-permute-done((f32[3,4,16,128]{3,2,1,0:T(8,128)S(1)}, f32[3,4,16,128]{3,2,1,0:T(8,128)S(1)}, u32[]{:S(2)}, u32[]{:S(2)}) %collective-permute-start.12) | collective-permute-done | bytes 98336 | tf_op jit(solution)/shard_map/ppermute | solution.py:156
  32.3 0.5 shard_map.41
  32.8 2.1 %collective-permute-start.13 = (f32[3,4,16,128]{3,2,1,0:T(8,128)S(1)}, f32[3,4,16,128]{3,2,1,0:T(8,128)S(1)}, u32[]{:S(2)}, u32[]{:S(2)}) collective-permute-start(f32[3,4,16,128]{3,2,1,0:T(8,128)S(1)} %get-tuple-element.54), channel_id=1, source_target_pairs={{0,24},{8,16},{16,8},{24,0},{1,25},{9,17},{17,9},{25,1},{2,26},{10... | collective-permute-start | bytes 294920 | tf_op jit(solution)/shard_map/ppermute | solution.py:156
  34.9 0.2 collective-permute-start.14
  35.1 2.1 %collective-permute-start.15 = (f32[3,4,16,128]{3,2,1,0:T(8,128)S(1)}, f32[3,4,16,128]{3,2,1,0:T(8,128)S(1)}, u32[]{:S(2)}, u32[]{:S(2)}) collective-permute-start(f32[3,4,16,128]{3,2,1,0:T(8,128)S(1)} %get-tuple-element.56), channel_id=1, source_target_pairs={{0,8},{8,0},{16,24},{24,16},{1,9},{9,1},{17,25},{25,17},{2,10},{10... | collective-permute-start | bytes 294920 | tf_op jit(solution)/shard_map/ppermute | solution.py:156
  37.3 2.3 %collective-permute-start.4 = (f32[2,4,16,128]{3,2,1,0:T(8,128)S(1)}, f32[2,4,16,128]{3,2,1,0:T(8,128)S(1)}, u32[]{:S(2)}, u32[]{:S(2)}) collective-permute-start(f32[2,4,16,128]{3,2,1,0:T(8,128)S(1)} %get-tuple-element.43), channel_id=1, source_target_pairs={{0,24},{8,16},{16,8},{24,0},{1,25},{9,17},{17,9},{25,1},{2,26},{10... | collective-permute-start | bytes 196616 | tf_op jit(solution)/shard_map/ppermute | solution.py:156
  39.6 1.6 %collective-permute-start.21 = (f32[3,4,16,128]{3,2,1,0:T(8,128)S(1)}, f32[3,4,16,128]{3,2,1,0:T(8,128)S(1)}, u32[]{:S(2)}, u32[]{:S(2)}) collective-permute-start(f32[3,4,16,128]{3,2,1,0:T(8,128)S(1)} %get-tuple-element.64), channel_id=1, source_target_pairs={{0,24},{8,16},{16,8},{24,0},{1,25},{9,17},{17,9},{25,1},{2,26},{10... | collective-permute-start | bytes 294920 | tf_op jit(solution)/shard_map/ppermute | solution.py:156
  41.3 0.6 collective-permute-start.22
  41.8 2.8 %collective-permute-done.14.refs_6_ = f32[3,4,16,128]{3,2,1,0:T(8,128)S(1)} collective-permute-done((f32[3,4,16,128]{3,2,1,0:T(8,128)S(1)}, f32[3,4,16,128]{3,2,1,0:T(8,128)S(1)}, u32[]{:S(2)}, u32[]{:S(2)}) %collective-permute-start.14) | collective-permute-done | bytes 98336 | tf_op jit(solution)/shard_map/ppermute | solution.py:156
  44.7 3.0 %collective-permute-start.5 = (f32[2,4,16,128]{3,2,1,0:T(8,128)S(1)}, f32[2,4,16,128]{3,2,1,0:T(8,128)S(1)}, u32[]{:S(2)}, u32[]{:S(2)}) collective-permute-start(f32[2,4,16,128]{3,2,1,0:T(8,128)S(1)} %get-tuple-element.44), channel_id=1, source_target_pairs={{0,16},{8,24},{16,0},{24,8},{1,17},{9,25},{17,1},{25,9},{2,18},{10... | collective-permute-start | bytes 196616 | tf_op jit(solution)/shard_map/ppermute | solution.py:156
  47.7 4.4 %collective-permute-start.6 = (f32[2,4,16,128]{3,2,1,0:T(8,128)S(1)}, f32[2,4,16,128]{3,2,1,0:T(8,128)S(1)}, u32[]{:S(2)}, u32[]{:S(2)}) collective-permute-start(f32[2,4,16,128]{3,2,1,0:T(8,128)S(1)} %get-tuple-element.45), channel_id=1, source_target_pairs={{0,8},{8,0},{16,24},{24,16},{1,9},{9,1},{17,25},{25,17},{2,10},{10... | collective-permute-start | bytes 196616 | tf_op jit(solution)/shard_map/ppermute | solution.py:156
  52.1 6.5 %collective-permute-done.5.refs_2_ = f32[2,4,16,128]{3,2,1,0:T(8,128)S(1)} collective-permute-done((f32[2,4,16,128]{3,2,1,0:T(8,128)S(1)}, f32[2,4,16,128]{3,2,1,0:T(8,128)S(1)}, u32[]{:S(2)}, u32[]{:S(2)}) %collective-permute-start.5) | collective-permute-done | bytes 65568 | tf_op jit(solution)/shard_map/ppermute | solution.py:156
  58.6 1.0 %shard_map.42.refs_0_ = f32[4,128,512]{2,1,0:T(8,128)} custom-call(f32[2,4,16,128]{3,2,1,0:T(8,128)S(1)} %get-tuple-element.42.refs_0_, f32[2,4,16,128]{3,2,1,0:T(8,128)S(1)} %collective-permute-done.4.refs_1_, f32[2,4,16,128]{3,2,1,0:T(8,128)S(1)} %collective-permute-done.5.refs_2_, f32[2,4,16,128]{3,2,1,0:T(8,128)S(1)} %collective-permute-done.6.refs_3_, ...), custom_call_target="tpu_custom_call" | custom-call | flops 262144 | bytes 2097152 | tf_op jit(solution)/shard_map/pallas_call | solution.py:185
  59.6 0.9 %shard_map.45 = f32[4,128,512]{2,1,0:T(8,128)} custom-call(f32[4,128,512]{2,1,0:T(8,128)} %shard_map.42.refs_0_, f32[3,4,16,128]{3,2,1,0:T(8,128)S(1)} %get-tuple-element.63.refs_1_, f32[3,4,16,128]{3,2,1,0:T(8,128)S(1)} %collective-permute-done.21.refs_2_, f32[3,4,16,128]{3,2,1,0:T(8,128)S(1)} %collective-permute-done.22.refs_3_, ...), custom_call_target="tpu_custom_call", output_to_operand_aliasing={{}: (0, {})} | custom-call | flops 262144 | bytes 2097152 | tf_op jit(solution)/shard_map/pallas_call | solution.py:185
  (38 shorter events, 0.9 us)
Async XLA Ops:
  0.0 10.5 %copy-start = (s32[16]{0:T(128)S(1)}, s32[16]{0:T(128)}, u32[]{:S(2)}) copy-start(s32[16]{0:T(128)} %param.4) | copy-start | bytes 196
  1.7 17.4 %collective-permute-start = (f32[2,4,16,128]{3,2,1,0:T(8,128)S(1)}, f32[2,4,16,128]{3,2,1,0:T(8,128)S(1)}, u32[]{:S(2)}, u32[]{:S(2)}) collective-permute-start(f32[2,4,16,128]{3,2,1,0:T(8,128)S(1)} %get-tuple-element.37), channel_id=1, source_target_pairs={{0,24},{8,16},{16,8},{24,0},{1,25},{9,17},{17,9},{25,1},{2,26},{10... | collective-permute-start | bytes 196616 | tf_op jit(solution)/shard_map/ppermute | solution.py:156
  6.9 13.8 %collective-permute-start.1 = (f32[2,4,16,128]{3,2,1,0:T(8,128)S(1)}, f32[2,4,16,128]{3,2,1,0:T(8,128)S(1)}, u32[]{:S(2)}, u32[]{:S(2)}) collective-permute-start(f32[2,4,16,128]{3,2,1,0:T(8,128)S(1)} %get-tuple-element.38), channel_id=1, source_target_pairs={{0,16},{8,24},{16,0},{24,8},{1,17},{9,25},{17,1},{25,9},{2,18},{10... | collective-permute-start | bytes 196616 | tf_op jit(solution)/shard_map/ppermute | solution.py:156
  6.9 5.4 %collective-permute-start.7 = (f32[4,4,16,128]{3,2,1,0:T(8,128)S(1)}, f32[4,4,16,128]{3,2,1,0:T(8,128)S(1)}, u32[]{:S(2)}, u32[]{:S(2)}) collective-permute-start(f32[4,4,16,128]{3,2,1,0:T(8,128)S(1)} %get-tuple-element.46), channel_id=1, source_target_pairs={{0,2},{1,3},{2,0},{3,1},{4,6},{5,7},{6,4},{7,5},{8,10},{9,11},{10,... | collective-permute-start | bytes 393224 | tf_op jit(solution)/shard_map/ppermute | solution.py:156
  8.4 7.8 %collective-permute-start.8 = (f32[4,4,16,128]{3,2,1,0:T(8,128)S(1)}, f32[4,4,16,128]{3,2,1,0:T(8,128)S(1)}, u32[]{:S(2)}, u32[]{:S(2)}) collective-permute-start(f32[4,4,16,128]{3,2,1,0:T(8,128)S(1)} %get-tuple-element.47), channel_id=1, source_target_pairs={{0,4},{1,5},{2,6},{3,7},{4,0},{5,1},{6,2},{7,3},{8,12},{9,13},{10,... | collective-permute-start | bytes 393224 | tf_op jit(solution)/shard_map/ppermute | solution.py:156
  9.9 9.2 %collective-permute-start.9 = (f32[4,4,16,128]{3,2,1,0:T(8,128)S(1)}, f32[4,4,16,128]{3,2,1,0:T(8,128)S(1)}, u32[]{:S(2)}, u32[]{:S(2)}) collective-permute-start(f32[4,4,16,128]{3,2,1,0:T(8,128)S(1)} %get-tuple-element.48), channel_id=1, source_target_pairs={{0,6},{1,7},{2,4},{3,5},{4,2},{5,3},{6,0},{7,1},{8,14},{9,15},{10,... | collective-permute-start | bytes 393224 | tf_op jit(solution)/shard_map/ppermute | solution.py:156
  12.3 13.3 %collective-permute-start.16 = (f32[3,4,16,128]{3,2,1,0:T(8,128)S(1)}, f32[3,4,16,128]{3,2,1,0:T(8,128)S(1)}, u32[]{:S(2)}, u32[]{:S(2)}) collective-permute-start(f32[3,4,16,128]{3,2,1,0:T(8,128)S(1)} %get-tuple-element.58), channel_id=1, source_target_pairs={{0,24},{8,16},{16,8},{24,0},{1,25},{9,17},{17,9},{25,1},{2,26},{10... | collective-permute-start | bytes 294920 | tf_op jit(solution)/shard_map/ppermute | solution.py:156
  16.1 12.0 %collective-permute-start.17 = (f32[3,4,16,128]{3,2,1,0:T(8,128)S(1)}, f32[3,4,16,128]{3,2,1,0:T(8,128)S(1)}, u32[]{:S(2)}, u32[]{:S(2)}) collective-permute-start(f32[3,4,16,128]{3,2,1,0:T(8,128)S(1)} %get-tuple-element.59), channel_id=1, source_target_pairs={{0,16},{8,24},{16,0},{24,8},{1,17},{9,25},{17,1},{25,9},{2,18},{10... | collective-permute-start | bytes 294920 | tf_op jit(solution)/shard_map/ppermute | solution.py:156
  19.1 6.0 %collective-permute-start.2 = (f32[5,4,16,128]{3,2,1,0:T(8,128)S(1)}, f32[5,4,16,128]{3,2,1,0:T(8,128)S(1)}, u32[]{:S(2)}, u32[]{:S(2)}) collective-permute-start(f32[5,4,16,128]{3,2,1,0:T(8,128)S(1)} %get-tuple-element.39), channel_id=1, source_target_pairs={{0,8},{8,0},{16,24},{24,16},{1,9},{9,1},{17,25},{25,17},{2,10},{10... | collective-permute-start | bytes 491528 | tf_op jit(solution)/shard_map/ppermute | solution.py:156
  19.1 9.6 %collective-permute-start.10 = (f32[3,4,16,128]{3,2,1,0:T(8,128)S(1)}, f32[3,4,16,128]{3,2,1,0:T(8,128)S(1)}, u32[]{:S(2)}, u32[]{:S(2)}) collective-permute-start(f32[3,4,16,128]{3,2,1,0:T(8,128)S(1)} %get-tuple-element.50), channel_id=1, source_target_pairs={{0,24},{8,16},{16,8},{24,0},{1,25},{9,17},{17,9},{25,1},{2,26},{10... | collective-permute-start | bytes 294920 | tf_op jit(solution)/shard_map/ppermute | solution.py:156
  20.7 10.8 %collective-permute-start.11 = (f32[3,4,16,128]{3,2,1,0:T(8,128)S(1)}, f32[3,4,16,128]{3,2,1,0:T(8,128)S(1)}, u32[]{:S(2)}, u32[]{:S(2)}) collective-permute-start(f32[3,4,16,128]{3,2,1,0:T(8,128)S(1)} %get-tuple-element.51), channel_id=1, source_target_pairs={{0,16},{8,24},{16,0},{24,8},{1,17},{9,25},{17,1},{25,9},{2,18},{10... | collective-permute-start | bytes 294920 | tf_op jit(solution)/shard_map/ppermute | solution.py:156
  25.5 9.4 %collective-permute-start.3 = (f32[4,4,16,128]{3,2,1,0:T(8,128)S(1)}, f32[4,4,16,128]{3,2,1,0:T(8,128)S(1)}, u32[]{:S(2)}, u32[]{:S(2)}) collective-permute-start(f32[4,4,16,128]{3,2,1,0:T(8,128)S(1)} %get-tuple-element.41), channel_id=1, source_target_pairs={{0,1},{1,0},{2,3},{3,2},{4,5},{5,4},{6,7},{7,6},{8,9},{9,8},{10,11... | collective-permute-start | bytes 393224 | tf_op jit(solution)/shard_map/ppermute | solution.py:156
  25.6 6.7 %collective-permute-start.12 = (f32[3,4,16,128]{3,2,1,0:T(8,128)S(1)}, f32[3,4,16,128]{3,2,1,0:T(8,128)S(1)}, u32[]{:S(2)}, u32[]{:S(2)}) collective-permute-start(f32[3,4,16,128]{3,2,1,0:T(8,128)S(1)} %get-tuple-element.52), channel_id=1, source_target_pairs={{0,8},{8,0},{16,24},{24,16},{1,9},{9,1},{17,25},{25,17},{2,10},{10... | collective-permute-start | bytes 294920 | tf_op jit(solution)/shard_map/ppermute | solution.py:156
  28.7 6.5 %collective-permute-start.18 = (f32[4,4,16,128]{3,2,1,0:T(8,128)S(1)}, f32[4,4,16,128]{3,2,1,0:T(8,128)S(1)}, u32[]{:S(2)}, u32[]{:S(2)}) collective-permute-start(f32[4,4,16,128]{3,2,1,0:T(8,128)S(1)} %get-tuple-element.60), channel_id=1, source_target_pairs={{0,3},{1,2},{2,1},{3,0},{4,7},{5,6},{6,5},{7,4},{8,11},{9,10},{10,... | collective-permute-start | bytes 393224 | tf_op jit(solution)/shard_map/ppermute | solution.py:156
  28.7 8.5 %collective-permute-start.19 = (f32[4,4,16,128]{3,2,1,0:T(8,128)S(1)}, f32[4,4,16,128]{3,2,1,0:T(8,128)S(1)}, u32[]{:S(2)}, u32[]{:S(2)}) collective-permute-start(f32[4,4,16,128]{3,2,1,0:T(8,128)S(1)} %get-tuple-element.61), channel_id=1, source_target_pairs={{0,5},{1,4},{2,7},{3,6},{4,1},{5,0},{6,3},{7,2},{8,13},{9,12},{10,... | collective-permute-start | bytes 393224 | tf_op jit(solution)/shard_map/ppermute | solution.py:156
  31.5 8.1 %collective-permute-start.20 = (f32[4,4,16,128]{3,2,1,0:T(8,128)S(1)}, f32[4,4,16,128]{3,2,1,0:T(8,128)S(1)}, u32[]{:S(2)}, u32[]{:S(2)}) collective-permute-start(f32[4,4,16,128]{3,2,1,0:T(8,128)S(1)} %get-tuple-element.62), channel_id=1, source_target_pairs={{0,7},{1,6},{2,5},{3,4},{4,3},{5,2},{6,1},{7,0},{8,15},{9,14},{10,... | collective-permute-start | bytes 393224 | tf_op jit(solution)/shard_map/ppermute | solution.py:156
  32.8 8.5 %collective-permute-start.13 = (f32[3,4,16,128]{3,2,1,0:T(8,128)S(1)}, f32[3,4,16,128]{3,2,1,0:T(8,128)S(1)}, u32[]{:S(2)}, u32[]{:S(2)}) collective-permute-start(f32[3,4,16,128]{3,2,1,0:T(8,128)S(1)} %get-tuple-element.54), channel_id=1, source_target_pairs={{0,24},{8,16},{16,8},{24,0},{1,25},{9,17},{17,9},{25,1},{2,26},{10... | collective-permute-start | bytes 294920 | tf_op jit(solution)/shard_map/ppermute | solution.py:156
  34.9 9.7 %collective-permute-start.14 = (f32[3,4,16,128]{3,2,1,0:T(8,128)S(1)}, f32[3,4,16,128]{3,2,1,0:T(8,128)S(1)}, u32[]{:S(2)}, u32[]{:S(2)}) collective-permute-start(f32[3,4,16,128]{3,2,1,0:T(8,128)S(1)} %get-tuple-element.55), channel_id=1, source_target_pairs={{0,16},{8,24},{16,0},{24,8},{1,17},{9,25},{17,1},{25,9},{2,18},{10... | collective-permute-start | bytes 294920 | tf_op jit(solution)/shard_map/ppermute | solution.py:156
  35.1 9.5 %collective-permute-start.15 = (f32[3,4,16,128]{3,2,1,0:T(8,128)S(1)}, f32[3,4,16,128]{3,2,1,0:T(8,128)S(1)}, u32[]{:S(2)}, u32[]{:S(2)}) collective-permute-start(f32[3,4,16,128]{3,2,1,0:T(8,128)S(1)} %get-tuple-element.56), channel_id=1, source_target_pairs={{0,8},{8,0},{16,24},{24,16},{1,9},{9,1},{17,25},{25,17},{2,10},{10... | collective-permute-start | bytes 294920 | tf_op jit(solution)/shard_map/ppermute | solution.py:156
  37.3 10.4 %collective-permute-start.4 = (f32[2,4,16,128]{3,2,1,0:T(8,128)S(1)}, f32[2,4,16,128]{3,2,1,0:T(8,128)S(1)}, u32[]{:S(2)}, u32[]{:S(2)}) collective-permute-start(f32[2,4,16,128]{3,2,1,0:T(8,128)S(1)} %get-tuple-element.43), channel_id=1, source_target_pairs={{0,24},{8,16},{16,8},{24,0},{1,25},{9,17},{17,9},{25,1},{2,26},{10... | collective-permute-start | bytes 196616 | tf_op jit(solution)/shard_map/ppermute | solution.py:156
  39.6 19.9 %collective-permute-start.21 = (f32[3,4,16,128]{3,2,1,0:T(8,128)S(1)}, f32[3,4,16,128]{3,2,1,0:T(8,128)S(1)}, u32[]{:S(2)}, u32[]{:S(2)}) collective-permute-start(f32[3,4,16,128]{3,2,1,0:T(8,128)S(1)} %get-tuple-element.64), channel_id=1, source_target_pairs={{0,24},{8,16},{16,8},{24,0},{1,25},{9,17},{17,9},{25,1},{2,26},{10... | collective-permute-start | bytes 294920 | tf_op jit(solution)/shard_map/ppermute | solution.py:156
  41.3 18.3 %collective-permute-start.22 = (f32[3,4,16,128]{3,2,1,0:T(8,128)S(1)}, f32[3,4,16,128]{3,2,1,0:T(8,128)S(1)}, u32[]{:S(2)}, u32[]{:S(2)}) collective-permute-start(f32[3,4,16,128]{3,2,1,0:T(8,128)S(1)} %get-tuple-element.65), channel_id=1, source_target_pairs={{0,16},{8,24},{16,0},{24,8},{1,17},{9,25},{17,1},{25,9},{2,18},{10... | collective-permute-start | bytes 294920 | tf_op jit(solution)/shard_map/ppermute | solution.py:156
  44.7 14.9 %collective-permute-start.23 = (f32[3,4,16,128]{3,2,1,0:T(8,128)S(1)}, f32[3,4,16,128]{3,2,1,0:T(8,128)S(1)}, u32[]{:S(2)}, u32[]{:S(2)}) collective-permute-start(f32[3,4,16,128]{3,2,1,0:T(8,128)S(1)} %get-tuple-element.66), channel_id=1, source_target_pairs={{0,8},{8,0},{16,24},{24,16},{1,9},{9,1},{17,25},{25,17},{2,10},{10... | collective-permute-start | bytes 294920 | tf_op jit(solution)/shard_map/ppermute | solution.py:156
  44.7 13.9 %collective-permute-start.5 = (f32[2,4,16,128]{3,2,1,0:T(8,128)S(1)}, f32[2,4,16,128]{3,2,1,0:T(8,128)S(1)}, u32[]{:S(2)}, u32[]{:S(2)}) collective-permute-start(f32[2,4,16,128]{3,2,1,0:T(8,128)S(1)} %get-tuple-element.44), channel_id=1, source_target_pairs={{0,16},{8,24},{16,0},{24,8},{1,17},{9,25},{17,1},{25,9},{2,18},{10... | collective-permute-start | bytes 196616 | tf_op jit(solution)/shard_map/ppermute | solution.py:156
  47.7 10.9 %collective-permute-start.6 = (f32[2,4,16,128]{3,2,1,0:T(8,128)S(1)}, f32[2,4,16,128]{3,2,1,0:T(8,128)S(1)}, u32[]{:S(2)}, u32[]{:S(2)}) collective-permute-start(f32[2,4,16,128]{3,2,1,0:T(8,128)S(1)} %get-tuple-element.45), channel_id=1, source_target_pairs={{0,8},{8,0},{16,24},{24,16},{1,9},{9,1},{17,25},{25,17},{2,10},{10... | collective-permute-start | bytes 196616 | tf_op jit(solution)/shard_map/ppermute | solution.py:156
